TPU v7x, 128 devices: a whole 4x4x4 slice. The times are simulated.
128 devices in a mesh: gp: 128 (over z, y, x, core).
Axes of the slice: x: 4, y: 4, z: 4, core: 2. Of those that a mesh axis runs over, the one named last changes fastest.
Arguments:
- features: bfloat16 [1572864, 128], P('gp')
- labels: int32 [1572864], P('gp')
- train_mask: float32 [1572864], P('gp')
- send_idx: int32 [16384, 64], P('gp')
- src_idx: int32 [3145728], P('gp')
- dst_idx: int32 [3145728], P('gp')
- inv_deg: float32 [1572864], P('gp')
- w_self_1: bfloat16 [128, 256], replicated
- w_neigh_1: bfloat16 [128, 256], replicated
- bias_1: float32 [256], replicated
- w_self_2: bfloat16 [256, 256], replicated
- w_neigh_2: bfloat16 [256, 256], replicated
- bias_2: float32 [256], replicated
- w_self_3: bfloat16 [256, 40], replicated
- w_neigh_3: bfloat16 [256, 40], replicated
- bias_3: float32 [40], replicated
Outputs:
- output 1: float32 [], replicated
- output 2: float32 [128, 256], replicated
- output 3: float32 [128, 256], replicated
- output 4: float32 [256], replicated
- output 5: float32 [256, 256], replicated
- output 6: float32 [256, 256], replicated
- output 7: float32 [256], replicated
- output 8: float32 [256, 40], replicated
- output 9: float32 [256, 40], replicated
- output 10: float32 [40], replicated
All inputs are finite; a program needn't handle non-finite values.
Results may differ from a plain program's by a relative error of at most 0.00569115.
Values are sent between devices in bfloat16 or wider.
A program may use at most 1 GiB of HBM per device.

v0:
```python
import math

import jax
import jax.numpy as jnp
from jax import lax
from jax.experimental import pallas as pl
from jax.experimental.pallas import tpu as pltpu
from jax.sharding import PartitionSpec as P

GROUP_AXIS = 'gp'
LANES = 128
SPREAD = 40
BLOCK = 128
GROUP = 8
TAIL = 8
F32 = jnp.float32
BF16 = jnp.bfloat16
VMEM_LIMIT = 60 * 2 ** 20

SMEM_SPEC = pl.BlockSpec(memory_space=pltpu.SMEM)
HBM_SPEC = pl.BlockSpec(memory_space=pltpu.HBM)


def whole_spec(shape):
    return pl.BlockSpec(shape, lambda i: (0,) * len(shape))


def row_spec(rows, width):
    return pl.BlockSpec((rows, width), lambda i: (i, 0))


def params():
    return pltpu.CompilerParams(vmem_limit_bytes=VMEM_LIMIT, dimension_semantics=('arbitrary',))


def cost(micros):
    return pl.CostEstimate(flops=int(micros * 4e6), bytes_accessed=int(micros * 1e6), transcendentals=0)


def mm(a, b):
    return jnp.dot(a, b, preferred_element_type=F32)


def tile_linear(row):
    return ((row >> 3) << 4) | (row & 7)


def put_rows(tab, row0, x, nc):
    rows = x.shape[0]
    if nc == 1:
        tab[pl.ds(pl.multiple_of(row0, 8), rows), :] = x
    else:
        for g in range(rows // 8):
            for c in range(nc):
                at = pl.multiple_of((row0 + g * 8) * nc + c * 8, 8)
                tab[pl.ds(at, 8), :] = x[g * 8:g * 8 + 8, c * LANES:(c + 1) * LANES]


def fetch(src, stage, sem, parts):
    rows = src.shape[0] // parts
    copies = [pltpu.make_async_copy(src.at[pl.ds(k * rows, rows)], stage.at[pl.ds(k * rows, rows)], sem.at[k])
              for k in range(parts)]
    for c in copies:
        c.start()
    return copies


def unpack(copies, stage, tab, row0, nc):
    rows = stage.shape[0] // len(copies)
    step = next(d for d in (128, 96, 64, 32, 16) if rows % d == 0)
    for p, c in enumerate(copies):
        c.wait()

        def body(k, carry):
            at = pl.multiple_of(p * rows + k * step, step)
            put_rows(tab, row0 + at, stage[pl.ds(at, step), :].astype(F32), nc)
            return carry
        lax.fori_loop(0, rows // step, body, 0)


def group_of(blocks):
    return next(u for u in (GROUP, 4, 2) if blocks % u == 0)


def zero_rows(acc):
    rows = acc.shape[0]
    step = next(s for s in (256, 128, 64, 32, 16, 8) if rows % s == 0)

    def body(k, carry):
        acc[pl.ds(pl.multiple_of(k * step, step), step), :] = jnp.zeros((step, acc.shape[1]), F32)
        return carry
    lax.fori_loop(0, rows // step, body, 0)


def gather_16(idx, first, tab, nc):
    sub = lax.broadcasted_iota(jnp.int32, (8, LANES), 0)
    halves = [[None, None] for _ in range(nc)]
    for h in range(2):
        for k in range(8):
            at = idx[first + h * 8 + k]
            for c in range(nc):
                row = jnp.broadcast_to(tab[pl.ds(at + 8 * c, 1), :], (8, LANES))
                halves[c][h] = row if k == 0 else jnp.where(sub == k, row, halves[c][h])
    return [jnp.concatenate(halves[c], axis=0).astype(BF16) for c in range(nc)]


def segment_sums(meta, meta_at, idx, seg, tab, acc, bufs, nc, window, blocks):
    unroll = group_of(blocks)
    first_trip, end_trip, most = [meta[meta_at + 2 * blocks + k] for k in range(3)]

    def fill(b, buf):
        for g in range(BLOCK // 16):
            parts = gather_16(idx, b * BLOCK + g * 16, tab, nc)
            for c in range(nc):
                buf[g * 16:g * 16 + 16, c * LANES:(c + 1) * LANES] = parts[c]

    def sums(b, at, buf):
        rows = lax.broadcasted_iota(jnp.int32, (window, BLOCK), 0) + at
        return mm(jnp.where(rows == seg[b], 1.0, 0.0).astype(BF16), buf[...])

    def add(at, x):
        acc[pl.ds(pl.multiple_of(at, 8), window), :] += x

    fill(jnp.minimum(first_trip * unroll, blocks - 1), bufs[0])

    def body(t, carry):
        before = None
        for u in range(unroll):
            b = t * unroll + u
            now = (meta[meta_at + b], sums(b, meta[meta_at + b], bufs[u % 2]))
            fill(jnp.minimum(b + 1, blocks - 1), bufs[(u + 1) % 2])
            if before is not None:
                add(*before)
            before = now
        add(*before)
        return carry
    lax.fori_loop(first_trip, end_trip, body, 0)

    @pl.when(most > 1)
    def _():
        def again(b, carry):
            count = meta[meta_at + blocks + b]

            @pl.when(count > 1)
            def _():
                fill(b, bufs[0])

                def more(w, c):
                    at = meta[meta_at + b] + w * window
                    add(at, sums(b, at, bufs[0]))
                    return c
                lax.fori_loop(1, count, more, 0)
            return carry
        lax.fori_loop(first_trip * unroll, end_trip * unroll, again, 0)


def spread_lanes():
    return lax.broadcasted_iota(jnp.int32, (1, LANES), 1)


def split3(x):
    hi = x.astype(BF16).astype(F32)
    rest = x - hi
    mid = rest.astype(BF16).astype(F32)
    low = rest - mid
    lane = spread_lanes()
    out = jnp.where(lane < SPREAD, hi, jnp.where(lane < 2 * SPREAD, mid, low))
    return jnp.where(lane < 3 * SPREAD, out, 0.0).astype(BF16)


def pieces3(a):
    hi = a.astype(BF16)
    rest = a - hi.astype(F32)
    mid = rest.astype(BF16)
    low = (rest - mid.astype(F32)).astype(BF16)
    return jnp.concatenate([hi, mid, low], axis=1)


def fold3(a, folder):
    return mm(pieces3(a), folder)


def add_rows(ref, x):
    ref[...] += jnp.sum(x.reshape(x.shape[0] // 8, 8, x.shape[1]), axis=0)


def pick_rows(name, src, idx, peers, slots, mask):
    n = src.shape[0]
    per = math.gcd(peers, 16)
    extra = 0 if mask is None else TAIL
    parts = math.gcd(n // 128, 4)

    def kern(idx_ref, src_ref, *refs):
        if extra:
            mask_ref, out, tab, stage, sem, tail = refs
        else:
            out, tab, stage, sem = refs

        @pl.when(pl.program_id(0) == 0)
        def _():
            copies = fetch(src_ref, stage, sem, parts)
            if extra:
                total = jnp.sum(mask_ref[...], axis=(0, 1), keepdims=True)
                high = jnp.floor(total * (1.0 / LANES))
                first = lax.broadcasted_iota(jnp.int32, (TAIL, LANES), 0) == 0
                lane = lax.broadcasted_iota(jnp.int32, (TAIL, LANES), 1)
                digits = jnp.where(lane == 0, high, jnp.where(lane == 1, total - high * LANES, 0.0))
                tail[...] = jnp.where(first, digits, 0.0).astype(BF16)
            unpack(copies, stage, tab, 0, 1)

        def body(p, carry):
            for g in range(slots // 16):
                out[p, g * 16:g * 16 + 16, :] = gather_16(idx_ref, p * slots + g * 16, tab, 1)[0]
            if extra:
                out[p, slots:slots + extra, :] = tail[...]
            return carry
        lax.fori_loop(0, per, body, 0)

    operands = [idx, src] + ([mask] if extra else [])
    specs = [pl.BlockSpec((per * slots,), lambda i: (i,), memory_space=pltpu.SMEM), HBM_SPEC] + ([whole_spec(mask.shape)] if extra else [])
    return pl.pallas_call(
        kern, name=name, grid=(peers // per,),
        out_shape=jax.ShapeDtypeStruct((peers, slots + extra, LANES), BF16),
        in_specs=specs,
        out_specs=pl.BlockSpec((per, slots + extra, LANES), lambda i: (i, 0, 0)),
        scratch_shapes=([pltpu.VMEM((n, LANES), F32), pltpu.VMEM((n, LANES), BF16), pltpu.SemaphoreType.DMA((parts,))]
                        + ([pltpu.VMEM((TAIL, LANES), BF16)] if extra else [])),
        compiler_params=params(), cost_estimate=cost(10))(*operands)


def edge_call(name, edges, nc, table_rows, acc_rows, window, sources, build, hbm_in, blocked, fixed, outs, rows_out,
              tile, epilogue, micros, init=None, sub=1024):
    meta, meta_at, idx, seg = edges
    blocks = seg.shape[0]
    width = nc * LANES
    nh, nb, nf, no, ns = len(hbm_in), len(blocked), len(fixed), len(outs), len(sources)
    acc_total = -(-(acc_rows + window) // 256) * 256
    parts = 4
    sub = math.gcd(sub, tile)

    def kern(meta_ref, idx_ref, seg_ref, *refs):
        hb, refs = refs[:nh], refs[nh:]
        bl, refs = refs[:nb], refs[nb:]
        fx, refs = refs[:nf], refs[nf:]
        out, refs = refs[:no], refs[no:]
        tab, acc, buf_0, buf_1, isem = refs[:5]
        stages, sems = refs[5:5 + ns], refs[5 + ns:]
        i = pl.program_id(0)

        @pl.when(i == 0)
        def _():
            copies = [fetch(h, st, sm, parts) for h, st, sm in zip(hb, stages, sems)]
            if init is None:
                zero_rows(acc)
            else:
                start = pltpu.make_async_copy(hb[init], acc.at[pl.ds(0, acc_rows), :], isem)
                start.start()
            for o, (_, _, sums) in zip(out, outs):
                if sums:
                    o[...] = jnp.zeros_like(o)
            build(copies, stages, tab, fx)
            if init is not None:
                start.wait()
            segment_sums(meta_ref, meta_at, idx_ref, seg_ref, tab, acc, (buf_0, buf_1), nc, window, blocks)
            if epilogue is None:
                done = pltpu.make_async_copy(acc.at[pl.ds(0, acc_rows), :], out[0], isem)
                done.start()
                done.wait()
        if epilogue is not None:
            def part(j, carry):
                at = pl.multiple_of(j * sub, sub)
                epilogue(acc[pl.ds(pl.multiple_of(i * tile + at, sub), sub), :], [r.at[pl.ds(at, sub), :] for r in bl], fx,
                         [o if sums else o.at[pl.ds(at, sub), :] for o, (_, _, sums) in zip(out, outs)])
                return carry
            lax.fori_loop(0, tile // sub, part, 0)

    out_shape, out_specs = [], []
    for shape, dtype, sums in outs:
        out_shape.append(jax.ShapeDtypeStruct(shape, dtype))
        out_specs.append(HBM_SPEC if epilogue is None else whole_spec(shape) if sums else row_spec(tile, shape[1]))
    return pl.pallas_call(
        kern, name=name, grid=(1 if epilogue is None else rows_out // tile,), out_shape=out_shape,
        in_specs=([SMEM_SPEC, SMEM_SPEC, whole_spec(seg.shape)] + [HBM_SPEC] * nh
                  + [row_spec(tile, x.shape[1]) for x in blocked] + [whole_spec(x.shape) for x in fixed]),
        out_specs=out_specs,
        scratch_shapes=([pltpu.VMEM((table_rows * nc, LANES), F32), pltpu.VMEM((acc_total, width), F32),
                         pltpu.VMEM((BLOCK, width), BF16), pltpu.VMEM((BLOCK, width), BF16),
                         pltpu.SemaphoreType.DMA(())]
                        + [pltpu.VMEM(shape, BF16) for shape in sources]
                        + [pltpu.SemaphoreType.DMA((parts,)) for _ in sources]),
        compiler_params=params(), cost_estimate=cost(micros))(meta, idx, seg, *hbm_in, *blocked, *fixed)


def sum_over_devices(x, peers):
    _, chips, rows, lanes = x.shape

    def device(chip, core):
        return chip * 2 + core

    def kern(x_ref, out_ref, half, mine, got, pair_sem, send_sem, recv_sem, send_2, recv_2):
        me = lax.axis_index(GROUP_AXIS)
        chip, core = me // 2, me % 2
        mate = device(chip, 1 - core)

        def pair(src, dst, k):
            return pltpu.make_async_remote_copy(src_ref=src, dst_ref=dst, send_sem=pair_sem.at[2 * k],
                                                recv_sem=pair_sem.at[2 * k + 1], device_id=(mate,),
                                                device_id_type=pl.DeviceIdType.MESH)
        first = pair(x_ref.at[1 - core], half, 0)
        first.start()
        first.wait()

        def add(c, carry):
            mine[c] = x_ref[core, c] + half[c]
            return carry
        lax.fori_loop(0, chips, add, 0)

        def share(k):
            to = (chip + k) % chips
            return pltpu.make_async_remote_copy(src_ref=mine.at[to], dst_ref=got.at[chip], send_sem=send_sem.at[k],
                                                recv_sem=recv_sem.at[chip], device_id=(device(to, core),),
                                                device_id_type=pl.DeviceIdType.MESH)

        def landed(k):
            frm = (chip + k) % chips
            return pltpu.make_async_remote_copy(src_ref=mine.at[frm], dst_ref=got.at[frm], send_sem=send_sem.at[k],
                                                recv_sem=recv_sem.at[frm], device_id=(me,),
                                                device_id_type=pl.DeviceIdType.MESH)

        def start(k, carry):
            share(k).start()
            return carry
        lax.fori_loop(1, chips, start, 0)
        got[chip] = mine[chip]

        def settle(k, carry):
            landed(k).wait_recv()
            return carry
        lax.fori_loop(1, chips, settle, 0)

        def more(c, total):
            return total + got[c]
        out_ref[core, chip] = lax.fori_loop(0, chips, more, jnp.zeros((rows, lanes), F32))

        def drain(k, carry):
            share(k).wait_send()
            return carry
        lax.fori_loop(1, chips, drain, 0)

        def give(k):
            return pltpu.make_async_remote_copy(src_ref=out_ref.at[core, chip], dst_ref=out_ref.at[core, chip],
                                                send_sem=send_2.at[k], recv_sem=recv_2.at[chip],
                                                device_id=(device((chip + k) % chips, core),),
                                                device_id_type=pl.DeviceIdType.MESH)

        def given(k):
            frm = (chip + k) % chips
            return pltpu.make_async_remote_copy(src_ref=out_ref.at[core, frm], dst_ref=out_ref.at[core, frm],
                                                send_sem=send_2.at[k], recv_sem=recv_2.at[frm], device_id=(me,),
                                                device_id_type=pl.DeviceIdType.MESH)

        def start_2(k, carry):
            give(k).start()
            return carry
        lax.fori_loop(1, chips, start_2, 0)

        def settle_2(k, carry):
            given(k).wait_recv()
            return carry
        lax.fori_loop(1, chips, settle_2, 0)

        def drain_2(k, carry):
            give(k).wait_send()
            return carry
        lax.fori_loop(1, chips, drain_2, 0)
        last = pair(out_ref.at[core], out_ref.at[core], 1)
        last.start()
        last.wait()

    return pl.pallas_call(
        kern, name='sum_all', out_shape=jax.ShapeDtypeStruct(x.shape, F32),
        in_specs=[pl.BlockSpec(memory_space=pltpu.VMEM)], out_specs=pl.BlockSpec(memory_space=pltpu.VMEM),
        scratch_shapes=[pltpu.VMEM((chips, rows, lanes), F32), pltpu.VMEM((chips, rows, lanes), F32),
                        pltpu.VMEM((chips, rows, lanes), F32), pltpu.SemaphoreType.DMA((4,)),
                        pltpu.SemaphoreType.DMA((chips,)), pltpu.SemaphoreType.DMA((chips,)),
                        pltpu.SemaphoreType.DMA((chips,)), pltpu.SemaphoreType.DMA((chips,))],
        compiler_params=pltpu.CompilerParams(has_side_effects=True), cost_estimate=cost(25))(x)


def edge_meta(seg_first, seg_last, window, first_block, end_block):
    blocks = seg_first.shape[0]
    unroll = group_of(blocks)
    at = jnp.arange(blocks, dtype=jnp.int32)
    base = seg_first & ~7
    count = jnp.where((at >= first_block) & (at < end_block), (seg_last - base) // window + 1, 1)
    tail = jnp.stack([first_block // unroll, (end_block + unroll - 1) // unroll, jnp.max(count)])
    return [base, count, tail]


def join_meta(*metas):
    offsets, at = [], 0
    for m in metas:
        offsets.append(at)
        at += sum(x.shape[0] for x in m)
    return jnp.concatenate([x for m in metas for x in m]).astype(jnp.int32), offsets


def bits_for(n):
    return max(1, (n - 1).bit_length())


def spread3(w):
    w = jnp.pad(w, ((0, 0), (0, SPREAD - w.shape[1])))
    return jnp.pad(jnp.concatenate([w, w, w], axis=1), ((0, 0), (0, LANES - 3 * SPREAD)))


def lanes_pad(w):
    return jnp.pad(w, ((0, 0), (0, LANES - w.shape[1])))


def solution(mesh):
    peers = mesh.shape[GROUP_AXIS]

    def exchange(x):
        return lax.all_to_all(x, GROUP_AXIS, 0, 0, tiled=True)

    def device_step(features, labels, train_mask, send_idx, src_idx, dst_idx, inv_deg,
                    w_self_1, w_neigh_1, bias_1, w_self_2, w_neigh_2, bias_2,
                    w_self_3, w_neigh_3, bias_3):
        n = features.shape[0]
        slots = send_idx.shape[1]
        halo = peers * slots
        edges = src_idx.shape[0]
        hidden = w_self_1.shape[1]
        classes = w_self_3.shape[1]
        send_flat = send_idx.reshape(-1)
        tile = next(t for t in (4096, 1024) if n % t == 0)
        slot_bits = bits_for(halo)
        dst_bits = bits_for(n)
        table = n + halo

        blocks = edges // BLOCK
        halo_blocks = halo // BLOCK
        zero = jnp.int32(0)
        win_e, win_h, win_r = 176, 192, 240
        owned = jnp.sum((src_idx < n).astype(jnp.int32))
        near_end = (owned + BLOCK - 1) // BLOCK
        far_start = owned // BLOCK

        src_bits = bits_for(table)
        far_bit = dst_bits + src_bits
        by_dst = lax.sort(((src_idx >= n).astype(jnp.int32) << far_bit) | (dst_idx << src_bits) | src_idx, is_stable=False)
        src_f = by_dst & ((1 << src_bits) - 1)
        dst_f = (by_dst >> src_bits) & ((1 << dst_bits) - 1)
        is_far = src_f >= n
        src_near = jnp.minimum(src_f, n - 1)
        src_far = jnp.maximum(src_f - n, 0)
        seg_near = jnp.where(is_far, -1, dst_f).reshape(blocks, 1, BLOCK)
        seg_far = jnp.where(is_far, dst_f, -1).reshape(blocks, 1, BLOCK)
        first, last = dst_f[::BLOCK], dst_f[BLOCK - 1::BLOCK]
        meta_f, (near_at, far_at) = join_meta(
            edge_meta(first, jnp.where(is_far[BLOCK - 1::BLOCK], n - 1, last), win_e, zero, near_end),
            edge_meta(jnp.where(is_far[::BLOCK], first, 0), last, win_e, far_start, jnp.int32(blocks)))

        inv = jnp.broadcast_to(inv_deg[:, None], (n, LANES))
        b1 = bias_1.reshape(1, -1)
        b2 = bias_2.reshape(1, -1)
        lane = jnp.arange(LANES, dtype=jnp.int32)
        used = lane < 3 * SPREAD
        folder = jnp.tile(((lane[:, None] % SPREAD == lane[None, :] % SPREAD) & used[:, None] & used[None, :]).astype(BF16),
                          (3, 1))
        b3 = jnp.where(lane < 3 * SPREAD, spread3(bias_3.reshape(1, -1)), -1e30)
        if classes < SPREAD:
            b3 = jnp.where(lane % SPREAD < classes, b3, -1e30)
        target = jnp.where(lane[None, :] < 3 * SPREAD,
                           train_mask[:, None] * (1.0 + (labels[:, None] == lane[None, :] % SPREAD)), 0.0).astype(BF16)
        ws3, wn3 = spread3(w_self_3), spread3(w_neigh_3)
        ws3_t, wn3_t = lanes_pad(w_self_3).T, lanes_pad(w_neigh_3).T

        def rows_of(nc):
            def build(copies, stages, tab, fx):
                unpack(copies[0], stages[0], tab, 0, nc)
            return build

        def near_sums(name, nc, idx, rows, also):
            return edge_call(name, (meta_f, near_at, idx, seg_near), nc, n, n, win_e, [rows.shape], rows_of(nc),
                             [rows] + also, [], [], [((n, nc * LANES), F32, False)], n, tile, None, 20)[0]

        out_1 = pick_rows('send_1', features, send_flat, peers, slots, train_mask.reshape(-1, LANES))
        got_1 = exchange(out_1)
        near_1 = near_sums('near_1', 1, src_near, features, [inv])
        counts = got_1[:, slots, :2].astype(F32)
        total = jnp.sum(counts[:, 0]) * LANES + jnp.sum(counts[:, 1])

        def build_1(copies, stages, tab, fx):
            per = peers // len(copies[0])
            some = math.gcd(per, 8)
            for p in range(len(copies[0])):
                copies[0][p].wait()

                def body(k, carry):
                    q = p * per + k * some
                    rows = stages[0][pl.ds(q, some), :slots, :].reshape(some * slots, LANES)
                    put_rows(tab, q * slots, rows.astype(F32), 1)
                    return carry
                lax.fori_loop(0, per // some, body, 0)

        def epi_1(a, bl, fx, out):
            mean = (a * bl[1][...]).astype(BF16)
            z = mm(bl[0][...], fx[0][...]) + mm(mean, fx[1][...]) + fx[2][...]
            out[0][...] = mean
            out[1][...] = jnp.maximum(z, 0.0).astype(BF16)

        mean_1, hidden_1 = edge_call(
            'layer_1', (meta_f, far_at, src_far, seg_far), 1, halo, n, win_e, [(peers, slots + TAIL, LANES)], build_1,
            [got_1, near_1], [features, inv], [w_self_1, w_neigh_1, b1],
            [((n, LANES), BF16, False), ((n, hidden), BF16, False)], n, tile, epi_1, 25, init=1)

        keys = jnp.concatenate([(src_idx << dst_bits) | dst_idx,
                                (1 << 30) | (send_flat << slot_bits) | jnp.arange(halo, dtype=jnp.int32)])
        keys = lax.optimization_barrier((keys, mean_1))[0]
        ordered = lax.sort(keys, is_stable=False)
        by_src, by_row = ordered[:edges], ordered[edges:] & ((1 << 30) - 1)
        src_s = by_src >> dst_bits
        dst_s = by_src & ((1 << dst_bits) - 1)
        row_s = by_row >> slot_bits
        slot_s = by_row & ((1 << slot_bits) - 1)
        first, last = src_s[::BLOCK], src_s[BLOCK - 1::BLOCK]
        meta_b, (own_at, halo_at, owner_at) = join_meta(
            edge_meta(jnp.minimum(first, n - 1), jnp.minimum(last, n - 1), win_e, zero, near_end),
            edge_meta(jnp.maximum(first - n, 0), jnp.maximum(last - n, 0), win_h, far_start, jnp.int32(blocks)),
            edge_meta(row_s[::BLOCK], row_s[BLOCK - 1::BLOCK], win_r, zero, jnp.int32(halo_blocks)))
        seg_o = src_s.reshape(blocks, 1, BLOCK)
        seg_h = seg_o - n
        seg_r = row_s.reshape(halo_blocks, 1, BLOCK)
        dst_wide = tile_linear(dst_s)

        out_2 = pick_rows('send_2', mean_1, send_flat, peers, slots, None)
        got_2 = exchange(out_2)
        near_2 = near_sums('near_2', 2, tile_linear(src_near), hidden_1, [])

        def build_2(copies, stages, tab, fx):
            per = peers // len(copies[0])
            some = math.gcd(per, 8)
            for p in range(len(copies[0])):
                copies[0][p].wait()
                copies[1][p].wait()

                def body(k, carry):
                    q = p * per + k * some
                    f = stages[0][pl.ds(q, some), :slots, :].reshape(some * slots, LANES)
                    m = stages[1][pl.ds(q, some)].reshape(some * slots, LANES)
                    z = mm(f, fx[3][...]) + mm(m, fx[4][...]) + fx[5][...]
                    put_rows(tab, q * slots, jnp.maximum(z, 0.0).astype(BF16).astype(F32), 2)
                    return carry
                lax.fori_loop(0, per // some, body, 0)

        def epi_2(a, bl, fx, out):
            scale = bl[1][...]
            mean = (a * jnp.concatenate([scale, scale], axis=1)).astype(BF16)
            z = mm(bl[0][...], fx[0][...]) + mm(mean, fx[1][...]) + fx[2][...]
            h = jnp.maximum(z, 0.0).astype(BF16)
            out[0][...] = mean
            out[1][...] = h
            both = mm(h, fx[6][...])
            out[2][...] = split3(both[:, :LANES])
            out[3][...] = both[:, LANES:]

        mean_2, hidden_2, proj, logits_self = edge_call(
            'layer_2', (meta_f, far_at, tile_linear(src_far), seg_far), 2, halo, n, win_e,
            [(peers, slots + TAIL, LANES), (peers, slots, LANES)], build_2, [got_1, got_2, near_2],
            [hidden_1, inv], [w_self_2, w_neigh_2, b2, w_self_1, w_neigh_1, b1, jnp.concatenate([wn3, ws3], axis=1)],
            [((n, hidden), BF16, False), ((n, hidden), BF16, False), ((n, LANES), BF16, False),
             ((n, LANES), F32, False)], n, tile, epi_2, 40, init=2)

        out_3 = pick_rows('send_3', proj, send_flat, peers, slots, None)
        got_3 = exchange(out_3).reshape(halo, LANES)
        near_3 = near_sums('near_3', 1, src_near, proj, [target])
        inv_total = (1.0 / total).reshape(1, 1)

        def epi_3(a, bl, fx, out):
            scale = bl[1][...]
            z = bl[0][...] + fold3(a * scale, fx[2][...]) + fx[0][...]
            lane = spread_lanes()
            z = jnp.where(lane < 3 * SPREAD, z, -1e30)
            top = jnp.max(z, axis=1, keepdims=True)
            e = jnp.where(lane < SPREAD, jnp.exp(z - top), 0.0)
            lse = top + jnp.log(jnp.sum(e, axis=1, keepdims=True))
            t = bl[2][...].astype(F32)
            hit = t > 1.5
            d = jnp.where(t > 0.5, jnp.exp(z - lse) - jnp.where(hit, 1.0, 0.0), 0.0) * fx[1][...]
            db = d.astype(BF16)
            out[0][...] = db
            out[1][...] = split3(db.astype(F32) * scale)
            add_rows(out[2], d)
            add_rows(out[3], jnp.where(hit & (lane < SPREAD), lse - z, 0.0))

        d_bf_3, scaled_3, g_b3, loss_parts = edge_call(
            'layer_3', (meta_f, far_at, src_far, seg_far), 1, halo, n, win_e, [(halo, LANES)], rows_of(1), [got_3, near_3],
            [logits_self, inv, target], [b3, jnp.broadcast_to(inv_total, (1, LANES)), folder],
            [((n, LANES), BF16, False), ((n, LANES), BF16, False), ((8, LANES), F32, True), ((8, LANES), F32, True)],
            n, tile, epi_3, 30, init=1)

        def epi_b3h(a, bl, fx, out):
            out[0][...] = split3(fold3(a, fx[0][...]))

        tile_h = next(t for t in (4096, 512) if halo % t == 0)
        back_3 = edge_call('back_3_halo', (meta_b, halo_at, dst_s, seg_h), 1, n, halo, win_h, [(n, LANES)], rows_of(1),
                           [scaled_3], [], [folder], [((halo, LANES), BF16, False)], halo, tile_h, epi_b3h, 15)[0]
        ret_3 = exchange(back_3.reshape(peers, slots, LANES)).reshape(halo, LANES)
        own_3 = edge_call('back_3_own', (meta_b, own_at, dst_s, seg_o), 1, n, n, win_e, [(n, LANES)], rows_of(1),
                          [scaled_3], [], [], [((n, LANES), F32, False)], n, tile, None, 20)[0]

        def epi_o3(a, bl, fx, out):
            tb = fold3(a, fx[2][...]).astype(BF16)
            d_h = mm(jnp.concatenate([bl[0][...], tb], axis=1), fx[0][...])
            d_pre = jnp.where(bl[1][...].astype(F32) > 0, d_h, 0.0)
            db = d_pre.astype(BF16)
            scale = bl[2][...]
            out[0][...] = tb
            out[1][...] = db
            out[2][...] = (mm(db, fx[1][...]) * jnp.concatenate([scale, scale], axis=1)).astype(BF16)
            add_rows(out[3], d_pre)

        tb_3, d_bf_2, scaled_2, g_b2 = edge_call(
            'owner_3', (meta_b, owner_at, slot_s, seg_r), 1, halo, n, win_r, [(halo, LANES)], rows_of(1), [ret_3, own_3],
            [d_bf_3, hidden_2, inv], [jnp.concatenate([ws3_t, wn3_t], axis=0), w_neigh_2.T, folder],
            [((n, LANES), BF16, False), ((n, hidden), BF16, False), ((n, hidden), BF16, False), ((8, hidden), F32, True)],
            n, tile, epi_o3, 30, init=1, sub=512)

        def epi_b2h(a, bl, fx, out):
            out[0][...] = a.astype(BF16)

        def epi_b2o(a, bl, fx, out):
            out[0][...] = a + mm(bl[0][...], fx[0][...])

        back_2 = edge_call('back_2_halo', (meta_b, halo_at, dst_wide, seg_h), 2, n, halo, win_h, [(n, hidden)], rows_of(2),
                           [scaled_2], [], [], [((halo, hidden), BF16, False)], halo, tile_h, epi_b2h, 20)[0]
        ret_2 = exchange(back_2.reshape(peers, slots, hidden)).reshape(halo, hidden)
        own_2 = edge_call('back_2_own', (meta_b, own_at, dst_wide, seg_o), 2, n, n, win_e, [(n, hidden)], rows_of(2),
                          [scaled_2], [d_bf_2], [w_self_2.T], [((n, hidden), F32, False)], n, tile, epi_b2o, 30)[0]

        def epi_o2(a, bl, fx, out):
            d_pre = jnp.where(bl[0][...].astype(F32) > 0, a, 0.0)
            out[0][...] = d_pre.astype(BF16)
            add_rows(out[1], d_pre)

        d_bf_1, g_b1 = edge_call(
            'owner_2', (meta_b, owner_at, tile_linear(slot_s), seg_r), 2, halo, n, win_r, [(halo, hidden)], rows_of(2),
            [ret_2, own_2], [hidden_1], [], [((n, hidden), BF16, False), ((8, hidden), F32, True)], n, tile, epi_o2, 25,
            init=1)

        def contract(a, b):
            return jnp.einsum('nd,ne->de', a, b, preferred_element_type=F32)

        parts = [contract(features, d_bf_1), contract(mean_1, d_bf_1), jnp.sum(g_b1, axis=0),
                 contract(hidden_1, d_bf_2), contract(mean_2, d_bf_2), jnp.sum(g_b2, axis=0),
                 contract(hidden_2, d_bf_3)[:, :classes], contract(hidden_2, tb_3)[:, :classes],
                 jnp.sum(g_b3, axis=0)[:classes], jnp.sum(loss_parts).reshape(1)]
        sizes = [p.size for p in parts]
        whole = sum(sizes)
        rows = -(-whole // (peers * LANES * 8)) * 8
        flat = jnp.concatenate([p.reshape(-1) for p in parts] + [jnp.zeros((peers * rows * LANES - whole,), F32)])
        full = sum_over_devices(flat.reshape(2, peers // 2, rows, LANES), peers).reshape(-1)
        outs, at = [], 0
        for p, size in zip(parts, sizes):
            outs.append(full[at:at + size].reshape(p.shape))
            at += size
        return (outs[-1][0] / total,) + tuple(outs[:-1])

    sharded = P(GROUP_AXIS)
    whole = P()
    return jax.shard_map(device_step, mesh=mesh,
                         in_specs=(sharded,) * 7 + (whole,) * 9,
                         out_specs=(whole,) * 10, check_vma=False)
```

profile of v0, /device:TPU:1, one launch (start us, length us, event | category | flops | bytes accessed | tf_op | source)
XLA Modules:
  0.0 561.6 jit_solution(2666948011859330474)
XLA Ops:
  0.7 0.9 copy.34
  2.3 11.1 %send_1.1 = bf16[128,72,128]{2,1,0:T(8,128)(2,1)} custom-call(s32[8192]{0:T(1024)} %reshape.251.idx_ref, bf16[12288,128]{1,0:T(8,128)(2,1)} %refs_2_.1, f32[96,128]{1,0:T(8,128)} %bitcast.93), custom_call_target="tpu_custom_call" | custom-call | flops 40000000 | bytes 10000000 | tf_op jit(solution)/shard_map/send_1/pallas_call | solution.py:221
  13.5 11.5 %all-to-all-start = ((bf16[128,72,128]{2,1,0:T(8,128)(2,1)}), bf16[128,72,128]{2,1,0:T(8,128)(2,1)S(1)}, u32[]{:S(2)}, u32[]{:S(2)}) async-start(bf16[128,72,128]{2,1,0:T(8,128)(2,1)} %send_1.1), calls=%async_computation | async-start | bytes 4718592 | tf_op jit(solution)/shard_map/all_to_all | solution.py:425
  28.9 8.6 %sort.14 = s32[24576]{0:T(1024)S(1)} sort(s32[24576]{0:T(1024)S(1)} %get-tuple-element.77), dimensions={0}, to_apply=%region_0.0 | sort | flops 368640 | bytes 196608 | tf_op jit(solution)/shard_map/sort | solution.py:452
  40.9 2.0 concatenate.28.meta_ref
  42.9 3.8 broadcast_in_dim.60.refs_1_.refs_3_.refs_4_
  46.7 19.7 %near_1.1.refs_1_ = f32[12288,128]{1,0:T(8,128)} custom-call(s32[774]{0:T(1024)} %concatenate.28.meta_ref, s32[24576]{0:T(1024)} %get-tuple-element.88.idx_ref, s32[192,1,128]{2,1,0:T(1,128)} %bitcast.70, bf16[12288,128]{1,0:T(8,128)(2,1)} %refs_2_.1, f32[12288,128]{1,0:T(8,128)} %broadcast_in_dim.60.refs_1_.refs_3_.refs_4_), custom_call_target="tpu_custom_call" | custom-call | flops 80000000 | bytes 20000000 | tf_op jit(solution)/shard_map/near_1/pallas_call | solution.py:281
  68.0 1.4 copy-done.3
  69.3 28.6 %layer_1.1 = (bf16[12288,128]{1,0:T(8,128)(2,1)}, bf16[12288,256]{1,0:T(8,128)(2,1)}) custom-call(s32[774]{0:T(1024)} %concatenate.28.meta_ref, s32[24576]{0:T(1024)} %get-tuple-element.90.idx_ref, s32[192,1,128]{2,1,0:T(1,128)} %bitcast.76, bf16[128,72,128]{2,1,0:T(8,128)(2,1)} %copy-done.3, f32[12288,128]{1,0:T(8,128)} %near_1.1.refs_1_, ...), custom_call_target="tpu_custom_call" | custom-call | flops 100000000 | bytes 25000000 | tf_op jit(solution)/shard_map/layer_1/pallas_call | solution.py:281
  98.0 11.2 %send_2.1 = bf16[128,64,128]{2,1,0:T(8,128)(2,1)} custom-call(s32[8192]{0:T(1024)} %reshape.251.idx_ref, bf16[12288,128]{1,0:T(8,128)(2,1)} %get-tuple-element.27.src_ref), custom_call_target="tpu_custom_call" | custom-call | flops 40000000 | bytes 10000000 | tf_op jit(solution)/shard_map/send_2/pallas_call | solution.py:221
  109.2 11.2 %all-to-all-start.1 = ((bf16[128,64,128]{2,1,0:T(8,128)(2,1)}), bf16[128,64,128]{2,1,0:T(8,128)(2,1)S(1)}, u32[]{:S(2)}, u32[]{:S(2)}) async-start(bf16[128,64,128]{2,1,0:T(8,128)(2,1)} %send_2.1), calls=%async_computation.1 | async-start | bytes 4194304 | tf_op jit(solution)/shard_map/all_to_all | solution.py:425
  120.4 6.6 %select_convert_fusion.refs_1_.refs_4_ = bf16[12288,128]{1,0:T(8,128)(2,1)} fusion(s32[128]{0:T(128)S(1)} %and_select_fusion, f32[12288]{0:T(1024)S(1)} %copy-done.13, s32[12288]{0:T(1024)S(1)} %copy-done.19, pred[128]{0:T(512)(128)(4,1)S(1)} %iota_compare_fusion.2), kind=kLoop, calls=%fused_computation | loop fusion | flops 9437184 | bytes 3244672 | tf_op jit(solution)/shard_map/convert_element_type | solution.py:476
  127.0 22.8 %near_2.1.refs_2_ = f32[12288,256]{1,0:T(8,128)} custom-call(s32[774]{0:T(1024)} %concatenate.28.meta_ref, s32[24576]{0:T(1024)} %get-tuple-element.86.idx_ref, s32[192,1,128]{2,1,0:T(1,128)} %bitcast.71, bf16[12288,256]{1,0:T(8,128)(2,1)} %get-tuple-element.29.refs_0_.refs_3_.refs_2_), custom_call_target="tpu_custom_call" | custom-call | flops 80000000 | bytes 20000000 | tf_op jit(solution)/shard_map/near_2/pallas_call | solution.py:281
  149.8 1.3 all-to-all-done.1.refs_1_
  151.1 1.4 copy-done.5
  152.5 36.6 %layer_2.1 = (bf16[12288,256]{1,0:T(8,128)(2,1)}, bf16[12288,256]{1,0:T(8,128)(2,1)}, bf16[12288,128]{1,0:T(8,128)(2,1)}, f32[12288,128]{1,0:T(8,128)}) custom-call(s32[774]{0:T(1024)} %concatenate.28.meta_ref, s32[24576]{0:T(1024)} %get-tuple-element.87.idx_ref, s32[192,1,128]{2,1,0:T(1,128)} %bitcast.77, bf16[128,72,128]{2,1,0:T(8,128)(2,1)} %copy-done.3, ...), custom_call_target="tpu_custom_call" | custom-call | flops 160000000 | bytes 40000000 | tf_op jit(solution)/shard_map/layer_2/pallas_call | solution.py:281
  189.1 11.1 %send_3.1 = bf16[128,64,128]{2,1,0:T(8,128)(2,1)} custom-call(s32[8192]{0:T(1024)} %reshape.251.idx_ref, bf16[12288,128]{1,0:T(8,128)(2,1)} %get-tuple-element.30.src_ref.refs_0_), custom_call_target="tpu_custom_call" | custom-call | flops 40000000 | bytes 10000000 | tf_op jit(solution)/shard_map/send_3/pallas_call | solution.py:221
  200.2 9.3 %all-to-all-start.2 = ((bf16[128,64,128]{2,1,0:T(8,128)(2,1)}), bf16[128,64,128]{2,1,0:T(8,128)(2,1)S(1)}, u32[]{:S(2)}, u32[]{:S(2)}) async-start(bf16[128,64,128]{2,1,0:T(8,128)(2,1)} %send_3.1), calls=%async_computation.2 | async-start | bytes 4194304 | tf_op jit(solution)/shard_map/all_to_all | solution.py:425
  209.5 7.3 %sort.15 = s32[32768]{0:T(1024)S(1)} sort(s32[32768]{0:T(1024)S(1)} %pad_add_fusion), dimensions={0}, to_apply=%region_4.5 | sort | flops 491520 | bytes 262144 | tf_op jit(solution)/shard_map/sort | solution.py:522
  219.0 1.0 slice_convert_fusion
  223.3 2.6 concatenate.29.meta_ref
  225.9 19.8 %near_3.1.refs_1_ = f32[12288,128]{1,0:T(8,128)} custom-call(s32[774]{0:T(1024)} %concatenate.28.meta_ref, s32[24576]{0:T(1024)} %get-tuple-element.88.idx_ref, s32[192,1,128]{2,1,0:T(1,128)} %bitcast.72, bf16[12288,128]{1,0:T(8,128)(2,1)} %get-tuple-element.30.src_ref.refs_0_, bf16[12288,128]{1,0:T(8,128)(2,1)} %select_convert_fusion.refs_1_.refs_4_), custom_call_target="tpu_custom_call" | custom-call | flops 80000000 | bytes 20000000 | tf_op jit(solution)/shard_map/near_3/pallas_call | solution.py:281
  247.1 33.4 %layer_3.1 = (bf16[12288,128]{1,0:T(8,128)(2,1)}, bf16[12288,128]{1,0:T(8,128)(2,1)}, f32[8,128]{1,0:T(8,128)}, f32[8,128]{1,0:T(8,128)}) custom-call(s32[774]{0:T(1024)} %concatenate.28.meta_ref, s32[24576]{0:T(1024)} %get-tuple-element.90.idx_ref, s32[192,1,128]{2,1,0:T(1,128)} %bitcast.78, bf16[8192,128]{1,0:T(8,128)(2,1)} %bitcast.64, ...), custom_call_target="tpu_custom_call" | custom-call | flops 120000000 | bytes 30000000 | tf_op jit(solution)/shard_map/layer_3/pallas_call | solution.py:281
  280.5 22.1 %back_3_halo.1 = bf16[8192,128]{1,0:T(8,128)(2,1)} custom-call(s32[905]{0:T(1024)} %concatenate.29.meta_ref, s32[24576]{0:T(1024)} %get-tuple-element.79.idx_ref, s32[192,1,128]{2,1,0:T(1,128)} %bitcast.83, bf16[12288,128]{1,0:T(8,128)(2,1)} %get-tuple-element.32.refs_0_, bf16[384,128]{1,0:T(8,128)(2,1)} %bitcast.74), custom_call_target="tpu_custom_call" | custom-call | flops 60000000 | bytes 15000000 | tf_op jit(solution)/shard_map/back_3_halo/pallas_call | solution.py:281
  302.6 11.4 %all-to-all-start.3 = ((bf16[128,64,128]{2,1,0:T(8,128)(2,1)}), bf16[128,64,128]{2,1,0:T(8,128)(2,1)S(1)}, u32[]{:S(2)}, u32[]{:S(2)}) async-start(bf16[128,64,128]{2,1,0:T(8,128)(2,1)} %bitcast.63), calls=%async_computation.3 | async-start | bytes 4194304 | tf_op jit(solution)/shard_map/all_to_all | solution.py:425
  315.5 19.6 %back_3_own.1.refs_1_ = f32[12288,128]{1,0:T(8,128)} custom-call(s32[905]{0:T(1024)} %concatenate.29.meta_ref, s32[24576]{0:T(1024)} %get-tuple-element.79.idx_ref, s32[192,1,128]{2,1,0:T(1,128)} %bitcast.81, bf16[12288,128]{1,0:T(8,128)(2,1)} %get-tuple-element.32.refs_0_), custom_call_target="tpu_custom_call" | custom-call | flops 80000000 | bytes 20000000 | tf_op jit(solution)/shard_map/back_3_own/pallas_call | solution.py:281
  335.1 13.2 %all-to-all-done.3 = bf16[128,64,128]{2,1,0:T(8,128)(2,1)S(1)} async-done(((bf16[128,64,128]{2,1,0:T(8,128)(2,1)}), bf16[128,64,128]{2,1,0:T(8,128)(2,1)S(1)}, u32[]{:S(2)}, u32[]{:S(2)}) %all-to-all-start.3) | async-done | bytes 2097184 | tf_op jit(solution)/shard_map/all_to_all | solution.py:425
  348.3 1.3 copy-done.4
  349.6 31.6 %owner_3.1 = (bf16[12288,128]{1,0:T(8,128)(2,1)}, bf16[12288,256]{1,0:T(8,128)(2,1)}, bf16[12288,256]{1,0:T(8,128)(2,1)}, f32[8,256]{1,0:T(8,128)}) custom-call(s32[905]{0:T(1024)} %concatenate.29.meta_ref, s32[8192]{0:T(1024)} %get-tuple-element.83.idx_ref, s32[64,1,128]{2,1,0:T(1,128)} %bitcast.91, bf16[8192,128]{1,0:T(8,128)(2,1)} %bitcast.62, ...), custom_call_target="tpu_custom_call" | custom-call | flops 120000000 | bytes 30000000 | tf_op jit(solution)/shard_map/owner_3/pallas_call | solution.py:281
  381.2 21.9 %back_2_halo.1 = bf16[8192,256]{1,0:T(8,128)(2,1)} custom-call(s32[905]{0:T(1024)} %concatenate.29.meta_ref, s32[24576]{0:T(1024)} %get-tuple-element.80.idx_ref, s32[192,1,128]{2,1,0:T(1,128)} %bitcast.84, bf16[12288,256]{1,0:T(8,128)(2,1)} %get-tuple-element.35.refs_0_), custom_call_target="tpu_custom_call" | custom-call | flops 80000000 | bytes 20000000 | tf_op jit(solution)/shard_map/back_2_halo/pallas_call | solution.py:281
  403.1 5.4 all-to-all-start.4
  409.3 4.6 fusion.2
  414.7 5.7 %fusion = f32[256,40]{1,0:T(8,128)S(1)} fusion(bf16[12288,256]{1,0:T(8,128)(2,1)} %get-tuple-element.34.refs_3_, bf16[12288,128]{1,0:T(8,128)(2,1)} %get-tuple-element.41), kind=kOutput, calls=%fused_computation.1 | convolution fusion | flops 251658240 | bytes 9478144 | tf_op jit(solution)/shard_map/slice | solution.py:658
  420.5 6.6 %convolution_bitcast_fusion = f32[32,2,8,128]{3,2,1,0:T(8,128)S(1)} fusion(bf16[12288,256]{1,0:T(8,128)(2,1)} %get-tuple-element.39, bf16[12288,256]{1,0:T(8,128)(2,1)} %get-tuple-element.36.refs_1_), kind=kOutput, calls=%fused_computation.5 | convolution fusion | flops 1610612736 | bytes 12845056 | tf_op jit(solution)/shard_map/nd,ne->de/dot_general | solution.py:654
  427.3 4.6 convolution_bitcast_fusion.1
  432.1 26.0 %back_2_own.1.refs_1_ = f32[12288,256]{1,0:T(8,128)} custom-call(s32[905]{0:T(1024)} %concatenate.29.meta_ref, s32[24576]{0:T(1024)} %get-tuple-element.80.idx_ref, s32[192,1,128]{2,1,0:T(1,128)} %bitcast.82, bf16[12288,256]{1,0:T(8,128)(2,1)} %get-tuple-element.35.refs_0_, bf16[12288,256]{1,0:T(8,128)(2,1)} %get-tuple-element.36.refs_1_, ...), custom_call_target="tpu_custom_call" | custom-call | flops 120000000 | bytes 30000000 | tf_op jit(solution)/shard_map/back_2_own/pallas_call | solution.py:281
  458.1 9.0 %all-to-all-done.4 = bf16[128,64,256]{2,1,0:T(8,128)(2,1)} async-done(((bf16[128,64,256]{2,1,0:T(8,128)(2,1)}), bf16[128,64,256]{2,1,0:T(8,128)(2,1)}, u32[]{:S(2)}, u32[]{:S(2)}) %all-to-all-start.4) | async-done | bytes 4194336 | tf_op jit(solution)/shard_map/all_to_all | solution.py:425
  467.1 23.1 %owner_2.1 = (bf16[12288,256]{1,0:T(8,128)(2,1)}, f32[8,256]{1,0:T(8,128)}) custom-call(s32[905]{0:T(1024)} %concatenate.29.meta_ref, s32[8192]{0:T(1024)} %get-tuple-element.84.idx_ref, s32[64,1,128]{2,1,0:T(1,128)} %bitcast.92, bf16[8192,256]{1,0:T(8,128)(2,1)} %bitcast.25.refs_0_, f32[12288,256]{1,0:T(8,128)} %back_2_own.1.refs_1_, ...), custom_call_target="tpu_custom_call" | custom-call | flops 100000000 | bytes 25000000 | tf_op jit(solution)/shard_map/owner_2/pallas_call | solution.py:281
  490.2 4.1 convolution_bitcast_fusion.2
  494.8 0.9 copy-done.1
  495.7 1.9 convolution_bitcast_fusion.3
  498.0 11.8 %concatenate.35 = f32[262144]{0:T(1024)} concatenate(f32[32768]{0:T(1024)S(1)} %bitcast.89, f32[32768]{0:T(1024)S(1)} %bitcast.88, f32[256]{0:T(256)S(1)} %reduce_sum.66, f32[65536]{0:T(1024)S(1)} %bitcast.80, f32[65536]{0:T(1024)S(1)} %bitcast.79, f32[256]{0:T(256)S(1)} %reduce_sum.67, f32[10240]{0:T(1024)S(1)} %reshape.267, f32[10240]{0:T(1024)S(1)} %reshape.268, ...), dimensions={0} | concatenate | bytes 2097152 | tf_op jit(solution)/shard_map/concatenate | solution.py:663
  509.8 40.3 %sum_all.1 = f32[2,64,16,128]{3,2,1,0:T(8,128)} custom-call(f32[2,64,16,128]{3,2,1,0:T(8,128)} %bitcast.69), custom_call_target="tpu_custom_call" | custom-call | flops 100000000 | bytes 25000000 | tf_op jit(solution)/shard_map/sum_all/pallas_call | solution.py:380
  550.1 1.5 slice.121
  553.2 0.9 fusion.21
  554.0 1.3 fusion.22
  555.3 1.2 slice.138
  556.5 1.2 slice.147
  (105 shorter events, 18.9 us)
Async XLA Ops:
  0.6 24.3 %copy-start.14 = (s32[24576]{0:T(1024)S(1)}, s32[24576]{0:T(1024)}, u32[]{:S(2)}) copy-start(s32[24576]{0:T(1024)} %param.20) | copy-start | bytes 294916
  0.7 24.3 %copy-start.15 = (s32[24576]{0:T(1024)S(1)}, s32[24576]{0:T(1024)}, u32[]{:S(2)}) copy-start(s32[24576]{0:T(1024)} %param.21) | copy-start | bytes 294916
  0.7 39.3 %copy-start.16 = (bf16[256,40]{0,1:T(8,128)(2,1)S(1)}, bf16[256,40]{0,1:T(8,128)(2,1)}, u32[]{:S(2)}) copy-start(bf16[256,40]{0,1:T(8,128)(2,1)} %param.30) | copy-start | bytes 61444
  0.7 39.4 %copy-start.17 = (bf16[256,40]{0,1:T(8,128)(2,1)S(1)}, bf16[256,40]{0,1:T(8,128)(2,1)}, u32[]{:S(2)}) copy-start(bf16[256,40]{0,1:T(8,128)(2,1)} %param.29) | copy-start | bytes 61444
  0.7 42.2 %copy-start.18 = (f32[12288]{0:T(1024)S(1)}, f32[12288]{0:T(1024)}, u32[]{:S(2)}) copy-start(f32[12288]{0:T(1024)} %param.22) | copy-start | bytes 147460
  13.5 54.5 %all-to-all-start = ((bf16[128,72,128]{2,1,0:T(8,128)(2,1)}), bf16[128,72,128]{2,1,0:T(8,128)(2,1)S(1)}, u32[]{:S(2)}, u32[]{:S(2)}) async-start(bf16[128,72,128]{2,1,0:T(8,128)(2,1)} %send_1.1), calls=%async_computation | async-start | bytes 4718592 | tf_op jit(solution)/shard_map/all_to_all | solution.py:425
  46.7 19.8 %copy-start.24 = (f32[40]{0:T(128)S(1)}, f32[40]{0:T(128)}, u32[]{:S(2)}) copy-start(f32[40]{0:T(128)} %param.31) | copy-start | bytes 484
  46.7 21.3 %copy-start.9 = (s32[8192]{0:T(1024)S(1)}, s32[8192]{0:T(1024)}, u32[]{:S(2)}) copy-start(s32[8192]{0:T(1024)} %reshape.251.idx_ref) | copy-start | bytes 98308
  68.0 1.4 copy-start.3
  98.0 22.4 %copy-start.13 = (f32[12288]{0:T(1024)S(1)}, f32[12288]{0:T(1024)}, u32[]{:S(2)}) copy-start(f32[12288]{0:T(1024)} %param.18) | copy-start | bytes 147460
  98.0 22.4 %copy-start.19 = (s32[12288]{0:T(1024)S(1)}, s32[12288]{0:T(1024)}, u32[]{:S(2)}) copy-start(s32[12288]{0:T(1024)} %param.17) | copy-start | bytes 147460
  109.2 41.9 %all-to-all-start.1 = ((bf16[128,64,128]{2,1,0:T(8,128)(2,1)}), bf16[128,64,128]{2,1,0:T(8,128)(2,1)S(1)}, u32[]{:S(2)}, u32[]{:S(2)}) async-start(bf16[128,64,128]{2,1,0:T(8,128)(2,1)} %send_2.1), calls=%async_computation.1 | async-start | bytes 4194304 | tf_op jit(solution)/shard_map/all_to_all | solution.py:425
  151.1 1.4 copy-start.5
  200.2 45.5 %all-to-all-start.2 = ((bf16[128,64,128]{2,1,0:T(8,128)(2,1)}), bf16[128,64,128]{2,1,0:T(8,128)(2,1)S(1)}, u32[]{:S(2)}, u32[]{:S(2)}) async-start(bf16[128,64,128]{2,1,0:T(8,128)(2,1)} %send_3.1), calls=%async_computation.2 | async-start | bytes 4194304 | tf_op jit(solution)/shard_map/all_to_all | solution.py:425
  217.5 28.2 %copy-start.12 = (s32[8192]{0:T(1024)}, s32[8192]{0:T(1024)S(1)}, u32[]{:S(2)}) copy-start(s32[8192]{0:T(1024)S(1)} %get-tuple-element.85) | copy-start | bytes 98308
  218.5 27.2 %copy-start.8 = (s32[24576]{0:T(1024)}, s32[24576]{0:T(1024)S(1)}, u32[]{:S(2)}) copy-start(s32[24576]{0:T(1024)S(1)} %get-tuple-element.82) | copy-start | bytes 294916
  245.7 1.4 copy-start.6
  280.5 33.6 %copy-start.10 = (bf16[256,256]{1,0:T(8,128)(2,1)S(1)}, bf16[256,256]{1,0:T(8,128)(2,1)}, u32[]{:S(2)}) copy-start(bf16[256,256]{1,0:T(8,128)(2,1)} %refs_6_.1) | copy-start | bytes 393220
  302.6 45.7 %all-to-all-start.3 = ((bf16[128,64,128]{2,1,0:T(8,128)(2,1)}), bf16[128,64,128]{2,1,0:T(8,128)(2,1)S(1)}, u32[]{:S(2)}, u32[]{:S(2)}) async-start(bf16[128,64,128]{2,1,0:T(8,128)(2,1)} %bitcast.63), calls=%async_computation.3 | async-start | bytes 4194304 | tf_op jit(solution)/shard_map/all_to_all | solution.py:425
  348.3 1.3 copy-start.4
  403.1 5.4 copy-start.11
  403.1 6.2 %copy-start.7 = (bf16[12288,128]{1,0:T(8,128)(2,1)S(1)}, bf16[12288,128]{1,0:T(8,128)(2,1)}, u32[]{:S(2)}) copy-start(bf16[12288,128]{1,0:T(8,128)(2,1)} %get-tuple-element.33.refs_2_) | copy-start | bytes 9437188
  403.1 64.0 %all-to-all-start.4 = ((bf16[128,64,256]{2,1,0:T(8,128)(2,1)}), bf16[128,64,256]{2,1,0:T(8,128)(2,1)}, u32[]{:S(2)}, u32[]{:S(2)}) async-start(bf16[128,64,256]{2,1,0:T(8,128)(2,1)} %bitcast.61), calls=%async_computation.4 | async-start | bytes 8388608 | tf_op jit(solution)/shard_map/all_to_all | solution.py:425
  408.5 5.5 copy-start.23
  408.5 6.1 %copy-start.22 = (f32[8,128]{1,0:T(8,128)S(1)}, f32[8,128]{1,0:T(8,128)}, u32[]{:S(2)}) copy-start(f32[8,128]{1,0:T(8,128)} %get-tuple-element.42) | copy-start | bytes 12292
  414.7 12.6 %slice-start = ((s8[6291456]{0:T(1024)(128)(4,1)}), s8[2097152]{0:T(1024)(128)(4,1)S(1)}, s32[]{:S(2)}) async-start(s8[6291456]{0:T(1024)(128)(4,1)} %bitcast.59), calls=%async_computation.5 | async-start | bytes 4194304
  420.5 6.7 %slice-start.1 = ((s8[6291456]{0:T(1024)(128)(4,1)}), s8[4194304]{0:T(1024)(128)(4,1)S(1)}, s32[]{:S(2)}) async-start(s8[6291456]{0:T(1024)(128)(4,1)} %bitcast.59), calls=%async_computation.6 | async-start | bytes 8388608
  427.3 4.8 copy-start.20
  467.1 23.1 %copy-start.2 = (bf16[12288,128]{1,0:T(8,128)(2,1)S(1)}, bf16[12288,128]{1,0:T(8,128)(2,1)}, u32[]{:S(2)}) copy-start(bf16[12288,128]{1,0:T(8,128)(2,1)} %get-tuple-element.27.src_ref) | copy-start | bytes 9437188
  490.2 4.6 copy-start
  490.2 5.5 copy-start.1
  495.7 2.2 copy-start.21
where the time goes:
time: 570 us; the launch traced here: 562 us
  Pallas kernels  379 us (66%)
  starting transfers between devices  48.9 us (9%)
  local copies, waits for them, and re-layouts  42.1 us (7%)
  other arithmetic  32.5 us (6%)
  matrix products  27.5 us (5%)
  waiting for transfers between devices  23.5 us (4%)
  between operations  8.23 us (1%)
    pallas_call x12, Pallas kernels, edge_call(): pl.pallas_call(kern, name=name, grid=(1 if epilogue is None else rows_out...  305 us
    all_to_all x5, starting transfers between devices, exchange(): return lax.all_to_all(x, GROUP_AXIS, 0, 0, tiled=True)  48.9 us
    pallas_call x1, Pallas kernels, sum_over_devices(): pl.pallas_call(kern, name='sum_all', out_shape=jax.ShapeDtypeStruct(x.sha...  40.3 us
    pallas_call x3, Pallas kernels, pick_rows(): pl.pallas_call(kern, name=name, grid=(peers // per,), out_shape=jax.Shape...  33.4 us
    all_to_all x5, waiting for transfers between devices, exchange(): return lax.all_to_all(x, GROUP_AXIS, 0, 0, tiled=True)  23.5 us
    dot_general x4, matrix products, contract(): return jnp.einsum('nd,ne->de', a, b, preferred_element_type=F32)  17.2 us
    concatenate x1, local copies, waits for them, and re-layouts, device_step(): jnp.concatenate([p.reshape(-1) for p in parts] + [jnp.zeros((peers * rows...  11.8 us
  transfers between devices with their start and end apart: 5, of which 3 were waited for; matrix products, arithmetic and copies ran while one was open for 12% of the time, Pallas kernels for 19%

commit v1 on v0

--- a/solution.py
+++ b/solution.py
@@ -228,23 +228,59 @@
         compiler_params=params(), cost_estimate=cost(10))(*operands)
 
 
+def pick_into(idx, tab, stage, peers, slots):
+    def body(p, carry):
+        for g in range(slots // 16):
+            stage[p, g * 16:g * 16 + 16, :] = gather_16(idx, p * slots + g * 16, tab, 1)[0]
+        return carry
+    lax.fori_loop(0, peers, body, 0)
+
+
+def send_out(stage, out, sem):
+    done = pltpu.make_async_copy(stage, out, sem)
+    done.start()
+    done.wait()
+
+
 def edge_call(name, edges, nc, table_rows, acc_rows, window, sources, build, hbm_in, blocked, fixed, outs, rows_out,
-              tile, epilogue, micros, init=None, sub=1024):
+              tile, epilogue, micros, init=None, sub=1024, keep=0, pick=None, then=None):
     meta, meta_at, idx, seg = edges
     blocks = seg.shape[0]
     width = nc * LANES
     nh, nb, nf, no, ns = len(hbm_in), len(blocked), len(fixed), len(outs), len(sources)
     acc_total = -(-(acc_rows + window) // 256) * 256
     parts = 4
+    steps = 1 if epilogue is None else rows_out // tile
     sub = math.gcd(sub, tile)
+    more_in, more_specs, more_out, more_scratch = [], [], [], []
+    if keep:
+        more_scratch.append(pltpu.VMEM((rows_out * keep, LANES), F32))
+    if pick:
+        p_idx, peers, slots = pick
+        more_in.append(p_idx)
+        more_specs.append(SMEM_SPEC)
+        more_out.append(jax.ShapeDtypeStruct((peers, slots, LANES), BF16))
+        more_scratch.append(pltpu.VMEM((peers, slots, LANES), BF16))
+    if then:
+        (t_meta, t_at, t_idx, t_seg), t_nc, t_rows, t_window, finish = then
+        t_width = t_nc * LANES
+        t_total = -(-(t_rows + t_window) // 256) * 256
+        more_in += [t_meta, t_idx, t_seg]
+        more_specs += [SMEM_SPEC, SMEM_SPEC, whole_spec(t_seg.shape)]
+        more_out.append(jax.ShapeDtypeStruct((t_rows, t_width), BF16))
+        more_scratch += [pltpu.VMEM((t_total, t_width), F32), pltpu.VMEM((BLOCK, t_width), BF16),
+                         pltpu.VMEM((BLOCK, t_width), BF16), pltpu.VMEM((t_rows, t_width), BF16)]
+    nm = len(more_in)
 
     def kern(meta_ref, idx_ref, seg_ref, *refs):
         hb, refs = refs[:nh], refs[nh:]
         bl, refs = refs[:nb], refs[nb:]
         fx, refs = refs[:nf], refs[nf:]
+        extra, refs = refs[:nm], refs[nm:]
         out, refs = refs[:no], refs[no:]
+        last_out, refs = refs[:len(more_out)], refs[len(more_out):]
         tab, acc, buf_0, buf_1, isem = refs[:5]
-        stages, sems = refs[5:5 + ns], refs[5 + ns:]
+        stages, sems, scratch = refs[5:5 + ns], refs[5 + ns:5 + 2 * ns], refs[5 + 2 * ns:]
         i = pl.program_id(0)
 
         @pl.when(i == 0)
@@ -258,49 +294,116 @@
             for o, (_, _, sums) in zip(out, outs):
                 if sums:
                     o[...] = jnp.zeros_like(o)
+            if then:
+                zero_rows(scratch[1])
             build(copies, stages, tab, fx)
             if init is not None:
                 start.wait()
             segment_sums(meta_ref, meta_at, idx_ref, seg_ref, tab, acc, (buf_0, buf_1), nc, window, blocks)
             if epilogue is None:
-                done = pltpu.make_async_copy(acc.at[pl.ds(0, acc_rows), :], out[0], isem)
-                done.start()
-                done.wait()
+                send_out(acc.at[pl.ds(0, acc_rows), :], out[0], isem)
         if epilogue is not None:
             def part(j, carry):
                 at = pl.multiple_of(j * sub, sub)
-                epilogue(acc[pl.ds(pl.multiple_of(i * tile + at, sub), sub), :], [r.at[pl.ds(at, sub), :] for r in bl], fx,
-                         [o if sums else o.at[pl.ds(at, sub), :] for o, (_, _, sums) in zip(out, outs)])
+                row0 = pl.multiple_of(i * tile + at, sub)
+
+                def put(x):
+                    put_rows(scratch[0], row0, x, keep)
+                epilogue(acc[pl.ds(row0, sub), :], [r.at[pl.ds(at, sub), :] for r in bl], fx,
+                         [o if sums else o.at[pl.ds(at, sub), :] for o, (_, _, sums) in zip(out, outs)], put)
                 return carry
             lax.fori_loop(0, tile // sub, part, 0)
+
+        if pick:
+            @pl.when(i == steps - 1)
+            def _():
+                pick_into(extra[0], scratch[0], scratch[1], peers, slots)
+                send_out(scratch[1], last_out[0], isem)
+        if then:
+            @pl.when(i == steps - 1)
+            def _():
+                kept, acc_2, buf_2, buf_3, stage = scratch
+                segment_sums(extra[0], t_at, extra[1], extra[2], kept, acc_2, (buf_2, buf_3), t_nc, t_window,
+                             t_seg.shape[0])
+                step = math.gcd(1024, t_rows)
+
+                def part(j, carry):
+                    at = pl.multiple_of(j * step, step)
+                    stage[pl.ds(at, step), :] = finish(acc_2[pl.ds(at, step), :], fx)
+                    return carry
+                lax.fori_loop(0, t_rows // step, part, 0)
+                send_out(stage, last_out[0], isem)
 
     out_shape, out_specs = [], []
     for shape, dtype, sums in outs:
         out_shape.append(jax.ShapeDtypeStruct(shape, dtype))
         out_specs.append(HBM_SPEC if epilogue is None else whole_spec(shape) if sums else row_spec(tile, shape[1]))
     return pl.pallas_call(
-        kern, name=name, grid=(1 if epilogue is None else rows_out // tile,), out_shape=out_shape,
+        kern, name=name, grid=(steps,), out_shape=out_shape + more_out,
         in_specs=([SMEM_SPEC, SMEM_SPEC, whole_spec(seg.shape)] + [HBM_SPEC] * nh
-                  + [row_spec(tile, x.shape[1]) for x in blocked] + [whole_spec(x.shape) for x in fixed]),
-        out_specs=out_specs,
+                  + [row_spec(tile, x.shape[1]) for x in blocked] + [whole_spec(x.shape) for x in fixed] + more_specs),
+        out_specs=out_specs + [HBM_SPEC] * len(more_out),
         scratch_shapes=([pltpu.VMEM((table_rows * nc, LANES), F32), pltpu.VMEM((acc_total, width), F32),
                          pltpu.VMEM((BLOCK, width), BF16), pltpu.VMEM((BLOCK, width), BF16),
                          pltpu.SemaphoreType.DMA(())]
                         + [pltpu.VMEM(shape, BF16) for shape in sources]
-                        + [pltpu.SemaphoreType.DMA((parts,)) for _ in sources]),
-        compiler_params=params(), cost_estimate=cost(micros))(meta, idx, seg, *hbm_in, *blocked, *fixed)
-
-
-def sum_over_devices(x, peers):
-    _, chips, rows, lanes = x.shape
+                        + [pltpu.SemaphoreType.DMA((parts,)) for _ in sources] + more_scratch),
+        compiler_params=params(), cost_estimate=cost(micros))(meta, idx, seg, *hbm_in, *blocked, *fixed, *more_in)
+
+
+SHARE = 16
+
+
+def grad_places(shapes):
+    places, at = [], 0
+    for rows, width in shapes:
+        columns = []
+        for _ in range(width // LANES):
+            columns.append(at)
+            at += -(-rows // SHARE)
+        places.append(columns)
+    return places, at
+
+
+def sum_over_devices(grads, sums, peers):
+    chips = peers // 2
+    places, used = grad_places([g.shape for g in grads] + [(SHARE, LANES)])
+    rounds = -(-used // peers)
+    rows = SHARE * rounds
+    widths = [x.shape[1] for x in sums]
 
     def device(chip, core):
         return chip * 2 + core
 
-    def kern(x_ref, out_ref, half, mine, got, pair_sem, send_sem, recv_sem, send_2, recv_2):
+    def kern(*refs):
+        ng, ns = len(grads), len(sums)
+        g_refs, s_refs, out_ref = refs[:ng], refs[ng:ng + ns], refs[ng + ns]
+        x_ref, half, mine, got, pair_sem, send_sem, recv_sem, send_2, recv_2 = refs[ng + ns + 1:]
         me = lax.axis_index(GROUP_AXIS)
         chip, core = me // 2, me % 2
         mate = device(chip, 1 - core)
+
+        def at(q):
+            unit = q // rounds
+            return unit // chips, unit % chips, (q % rounds) * SHARE
+
+        def put(q, value):
+            h, c, r = at(q)
+            x_ref[h, c, r:r + SHARE, :] = value
+        for g, columns in zip(g_refs, places):
+            for w, first in enumerate(columns):
+                for k in range(g.shape[0] // SHARE):
+                    put(first + k, g[k * SHARE:(k + 1) * SHARE, w * LANES:(w + 1) * LANES])
+        row = lax.broadcasted_iota(jnp.int32, (SHARE, LANES), 0)
+        small, line = jnp.zeros((SHARE, LANES), F32), 0
+        for s_ref, width in zip(s_refs, widths):
+            for w in range(width // LANES):
+                total = jnp.sum(s_ref[:, w * LANES:(w + 1) * LANES], axis=0, keepdims=True)
+                small = jnp.where(row == line, total, small)
+                line += 1
+        put(places[-1][0], small)
+        for q in range(used, peers * rounds):
+            put(q, jnp.zeros((SHARE, LANES), F32))
 
         def pair(src, dst, k):
             return pltpu.make_async_remote_copy(src_ref=src, dst_ref=dst, send_sem=pair_sem.at[2 * k],
@@ -340,7 +443,7 @@
 
         def more(c, total):
             return total + got[c]
-        out_ref[core, chip] = lax.fori_loop(0, chips, more, jnp.zeros((rows, lanes), F32))
+        out_ref[core, chip] = lax.fori_loop(0, chips, more, jnp.zeros((rows, LANES), F32))
 
         def drain(k, carry):
             share(k).wait_send()
@@ -377,14 +480,36 @@
         last.start()
         last.wait()
 
-    return pl.pallas_call(
-        kern, name='sum_all', out_shape=jax.ShapeDtypeStruct(x.shape, F32),
-        in_specs=[pl.BlockSpec(memory_space=pltpu.VMEM)], out_specs=pl.BlockSpec(memory_space=pltpu.VMEM),
-        scratch_shapes=[pltpu.VMEM((chips, rows, lanes), F32), pltpu.VMEM((chips, rows, lanes), F32),
-                        pltpu.VMEM((chips, rows, lanes), F32), pltpu.SemaphoreType.DMA((4,)),
+    vmem = pl.BlockSpec(memory_space=pltpu.VMEM)
+    shape = (2, chips, rows, LANES)
+    full = pl.pallas_call(
+        kern, name='sum_all', out_shape=jax.ShapeDtypeStruct(shape, F32),
+        in_specs=[vmem] * (len(grads) + len(sums)), out_specs=vmem,
+        scratch_shapes=[pltpu.VMEM(shape, F32), pltpu.VMEM(shape[1:], F32), pltpu.VMEM(shape[1:], F32),
+                        pltpu.VMEM(shape[1:], F32), pltpu.SemaphoreType.DMA((4,)),
                         pltpu.SemaphoreType.DMA((chips,)), pltpu.SemaphoreType.DMA((chips,)),
                         pltpu.SemaphoreType.DMA((chips,)), pltpu.SemaphoreType.DMA((chips,))],
-        compiler_params=pltpu.CompilerParams(has_side_effects=True), cost_estimate=cost(25))(x)
+        compiler_params=pltpu.CompilerParams(has_side_effects=True), cost_estimate=cost(25))(*grads, *sums)
+
+    def unpack_kern(full_ref, *outs):
+        def at(q):
+            unit = q // rounds
+            return unit // chips, unit % chips, (q % rounds) * SHARE
+        for o, columns in zip(outs, places):
+            for w, first in enumerate(columns):
+                for k in range(o.shape[0] // SHARE):
+                    h, c, r = at(first + k)
+                    o[k * SHARE:(k + 1) * SHARE, w * LANES:(w + 1) * LANES] = full_ref[h, c, r:r + SHARE, :]
+        h, c, r = at(places[-1][0])
+        small, line = full_ref[h, c, r:r + SHARE, :], 0
+        for o, width in zip(outs[len(grads):], widths):
+            for w in range(width // LANES):
+                o[:, w * LANES:(w + 1) * LANES] = small[line:line + 1, :]
+                line += 1
+    outs = [jax.ShapeDtypeStruct(g.shape, F32) for g in grads] + [jax.ShapeDtypeStruct((1, w), F32) for w in widths]
+    got = pl.pallas_call(unpack_kern, name='unpack_sums', out_shape=outs, in_specs=[vmem], out_specs=[vmem] * len(outs),
+                         cost_estimate=cost(3))(full)
+    return got[:len(grads)], got[len(grads):]
 
 
 def edge_meta(seg_first, seg_last, window, first_block, end_block):
@@ -435,6 +560,7 @@
         classes = w_self_3.shape[1]
         send_flat = send_idx.reshape(-1)
         tile = next(t for t in (4096, 1024) if n % t == 0)
+        half_tile = tile // 2
         slot_bits = bits_for(halo)
         dst_bits = bits_for(n)
         table = n + halo
@@ -505,16 +631,18 @@
                     return carry
                 lax.fori_loop(0, per // some, body, 0)
 
-        def epi_1(a, bl, fx, out):
+        def epi_1(a, bl, fx, out, put):
             mean = (a * bl[1][...]).astype(BF16)
             z = mm(bl[0][...], fx[0][...]) + mm(mean, fx[1][...]) + fx[2][...]
             out[0][...] = mean
             out[1][...] = jnp.maximum(z, 0.0).astype(BF16)
-
-        mean_1, hidden_1 = edge_call(
+            put(mean.astype(F32))
+
+        mean_1, hidden_1, out_2 = edge_call(
             'layer_1', (meta_f, far_at, src_far, seg_far), 1, halo, n, win_e, [(peers, slots + TAIL, LANES)], build_1,
             [got_1, near_1], [features, inv], [w_self_1, w_neigh_1, b1],
-            [((n, LANES), BF16, False), ((n, hidden), BF16, False)], n, tile, epi_1, 25, init=1)
+            [((n, LANES), BF16, False), ((n, hidden), BF16, False)], n, tile, epi_1, 25, init=1,
+            keep=1, pick=(send_flat, peers, slots))
 
         keys = jnp.concatenate([(src_idx << dst_bits) | dst_idx,
                                 (1 << 30) | (send_flat << slot_bits) | jnp.arange(halo, dtype=jnp.int32)])
@@ -535,7 +663,6 @@
         seg_r = row_s.reshape(halo_blocks, 1, BLOCK)
         dst_wide = tile_linear(dst_s)
 
-        out_2 = pick_rows('send_2', mean_1, send_flat, peers, slots, None)
         got_2 = exchange(out_2)
         near_2 = near_sums('near_2', 2, tile_linear(src_near), hidden_1, [])
 
@@ -555,7 +682,7 @@
                     return carry
                 lax.fori_loop(0, per // some, body, 0)
 
-        def epi_2(a, bl, fx, out):
+        def epi_2(a, bl, fx, out, put):
             scale = bl[1][...]
             mean = (a * jnp.concatenate([scale, scale], axis=1)).astype(BF16)
             z = mm(bl[0][...], fx[0][...]) + mm(mean, fx[1][...]) + fx[2][...]
@@ -563,22 +690,23 @@
             out[0][...] = mean
             out[1][...] = h
             both = mm(h, fx[6][...])
-            out[2][...] = split3(both[:, :LANES])
+            pieces = split3(both[:, :LANES])
+            out[2][...] = pieces
             out[3][...] = both[:, LANES:]
-
-        mean_2, hidden_2, proj, logits_self = edge_call(
+            put(pieces.astype(F32))
+
+        mean_2, hidden_2, proj, logits_self, out_3 = edge_call(
             'layer_2', (meta_f, far_at, tile_linear(src_far), seg_far), 2, halo, n, win_e,
             [(peers, slots + TAIL, LANES), (peers, slots, LANES)], build_2, [got_1, got_2, near_2],
             [hidden_1, inv], [w_self_2, w_neigh_2, b2, w_self_1, w_neigh_1, b1, jnp.concatenate([wn3, ws3], axis=1)],
             [((n, hidden), BF16, False), ((n, hidden), BF16, False), ((n, LANES), BF16, False),
-             ((n, LANES), F32, False)], n, tile, epi_2, 40, init=2)
-
-        out_3 = pick_rows('send_3', proj, send_flat, peers, slots, None)
+             ((n, LANES), F32, False)], n, half_tile, epi_2, 40, init=2, keep=1, pick=(send_flat, peers, slots))
+
         got_3 = exchange(out_3).reshape(halo, LANES)
         near_3 = near_sums('near_3', 1, src_near, proj, [target])
         inv_total = (1.0 / total).reshape(1, 1)
 
-        def epi_3(a, bl, fx, out):
+        def epi_3(a, bl, fx, out, put):
             scale = bl[1][...]
             z = bl[0][...] + fold3(a * scale, fx[2][...]) + fx[0][...]
             lane = spread_lanes()
@@ -591,27 +719,26 @@
             d = jnp.where(t > 0.5, jnp.exp(z - lse) - jnp.where(hit, 1.0, 0.0), 0.0) * fx[1][...]
             db = d.astype(BF16)
             out[0][...] = db
-            out[1][...] = split3(db.astype(F32) * scale)
+            pieces = split3(db.astype(F32) * scale)
+            out[1][...] = pieces
+            put(pieces.astype(F32))
             add_rows(out[2], d)
             add_rows(out[3], jnp.where(hit & (lane < SPREAD), lse - z, 0.0))
 
-        d_bf_3, scaled_3, g_b3, loss_parts = edge_call(
+        def finish_3(a, fx):
+            return split3(fold3(a, fx[2][...]))
+
+        d_bf_3, scaled_3, g_b3, loss_parts, back_3 = edge_call(
             'layer_3', (meta_f, far_at, src_far, seg_far), 1, halo, n, win_e, [(halo, LANES)], rows_of(1), [got_3, near_3],
             [logits_self, inv, target], [b3, jnp.broadcast_to(inv_total, (1, LANES)), folder],
             [((n, LANES), BF16, False), ((n, LANES), BF16, False), ((8, LANES), F32, True), ((8, LANES), F32, True)],
-            n, tile, epi_3, 30, init=1)
-
-        def epi_b3h(a, bl, fx, out):
-            out[0][...] = split3(fold3(a, fx[0][...]))
-
-        tile_h = next(t for t in (4096, 512) if halo % t == 0)
-        back_3 = edge_call('back_3_halo', (meta_b, halo_at, dst_s, seg_h), 1, n, halo, win_h, [(n, LANES)], rows_of(1),
-                           [scaled_3], [], [folder], [((halo, LANES), BF16, False)], halo, tile_h, epi_b3h, 15)[0]
+            n, tile, epi_3, 30, init=1, keep=1, then=((meta_b, halo_at, dst_s, seg_h), 1, halo, win_h, finish_3))
+
         ret_3 = exchange(back_3.reshape(peers, slots, LANES)).reshape(halo, LANES)
         own_3 = edge_call('back_3_own', (meta_b, own_at, dst_s, seg_o), 1, n, n, win_e, [(n, LANES)], rows_of(1),
                           [scaled_3], [], [], [((n, LANES), F32, False)], n, tile, None, 20)[0]
 
-        def epi_o3(a, bl, fx, out):
+        def epi_o3(a, bl, fx, out, put):
             tb = fold3(a, fx[2][...]).astype(BF16)
             d_h = mm(jnp.concatenate([bl[0][...], tb], axis=1), fx[0][...])
             d_pre = jnp.where(bl[1][...].astype(F32) > 0, d_h, 0.0)
@@ -619,28 +746,29 @@
             scale = bl[2][...]
             out[0][...] = tb
             out[1][...] = db
-            out[2][...] = (mm(db, fx[1][...]) * jnp.concatenate([scale, scale], axis=1)).astype(BF16)
+            scaled = (mm(db, fx[1][...]) * jnp.concatenate([scale, scale], axis=1)).astype(BF16)
+            out[2][...] = scaled
+            put(scaled.astype(F32))
             add_rows(out[3], d_pre)
 
-        tb_3, d_bf_2, scaled_2, g_b2 = edge_call(
+        def finish_2(a, fx):
+            return a.astype(BF16)
+
+        tb_3, d_bf_2, scaled_2, g_b2, back_2 = edge_call(
             'owner_3', (meta_b, owner_at, slot_s, seg_r), 1, halo, n, win_r, [(halo, LANES)], rows_of(1), [ret_3, own_3],
             [d_bf_3, hidden_2, inv], [jnp.concatenate([ws3_t, wn3_t], axis=0), w_neigh_2.T, folder],
             [((n, LANES), BF16, False), ((n, hidden), BF16, False), ((n, hidden), BF16, False), ((8, hidden), F32, True)],
-            n, tile, epi_o3, 30, init=1, sub=512)
-
-        def epi_b2h(a, bl, fx, out):
-            out[0][...] = a.astype(BF16)
-
-        def epi_b2o(a, bl, fx, out):
+            n, half_tile, epi_o3, 30, init=1, sub=512, keep=2,
+            then=((meta_b, halo_at, dst_wide, seg_h), 2, halo, win_h, finish_2))
+
+        def epi_b2o(a, bl, fx, out, put):
             out[0][...] = a + mm(bl[0][...], fx[0][...])
 
-        back_2 = edge_call('back_2_halo', (meta_b, halo_at, dst_wide, seg_h), 2, n, halo, win_h, [(n, hidden)], rows_of(2),
-                           [scaled_2], [], [], [((halo, hidden), BF16, False)], halo, tile_h, epi_b2h, 20)[0]
         ret_2 = exchange(back_2.reshape(peers, slots, hidden)).reshape(halo, hidden)
         own_2 = edge_call('back_2_own', (meta_b, own_at, dst_wide, seg_o), 2, n, n, win_e, [(n, hidden)], rows_of(2),
                           [scaled_2], [d_bf_2], [w_self_2.T], [((n, hidden), F32, False)], n, tile, epi_b2o, 30)[0]
 
-        def epi_o2(a, bl, fx, out):
+        def epi_o2(a, bl, fx, out, put):
             d_pre = jnp.where(bl[0][...].astype(F32) > 0, a, 0.0)
             out[0][...] = d_pre.astype(BF16)
             add_rows(out[1], d_pre)
@@ -653,20 +781,13 @@
         def contract(a, b):
             return jnp.einsum('nd,ne->de', a, b, preferred_element_type=F32)
 
-        parts = [contract(features, d_bf_1), contract(mean_1, d_bf_1), jnp.sum(g_b1, axis=0),
-                 contract(hidden_1, d_bf_2), contract(mean_2, d_bf_2), jnp.sum(g_b2, axis=0),
-                 contract(hidden_2, d_bf_3)[:, :classes], contract(hidden_2, tb_3)[:, :classes],
-                 jnp.sum(g_b3, axis=0)[:classes], jnp.sum(loss_parts).reshape(1)]
-        sizes = [p.size for p in parts]
-        whole = sum(sizes)
-        rows = -(-whole // (peers * LANES * 8)) * 8
-        flat = jnp.concatenate([p.reshape(-1) for p in parts] + [jnp.zeros((peers * rows * LANES - whole,), F32)])
-        full = sum_over_devices(flat.reshape(2, peers // 2, rows, LANES), peers).reshape(-1)
-        outs, at = [], 0
-        for p, size in zip(parts, sizes):
-            outs.append(full[at:at + size].reshape(p.shape))
-            at += size
-        return (outs[-1][0] / total,) + tuple(outs[:-1])
+        at = jnp.arange(LANES, dtype=jnp.int32)[None, :]
+        g_3 = jnp.where(at < SPREAD, contract(hidden_2, d_bf_3), contract(hidden_2, tb_3))
+        g, sums = sum_over_devices([contract(features, d_bf_1), contract(mean_1, d_bf_1), contract(hidden_1, d_bf_2),
+                                    contract(mean_2, d_bf_2), g_3], [g_b1, g_b2, g_b3, loss_parts], peers)
+        loss = jnp.sum(sums[3]) / total
+        return (loss, g[0], g[1], sums[0].reshape(-1), g[2], g[3], sums[1].reshape(-1), g[4][:, :classes],
+                g[4][:, SPREAD:SPREAD + classes], sums[2].reshape(-1)[:classes])
 
     sharded = P(GROUP_AXIS)
     whole = P()

time: 570 us -> 544 us (0.954)
  local copies, waits for them, and re-layouts: 42.1 us -> 23.1 us
  Pallas kernels: 379 us -> 367 us
    pallas_call x3 -> x1, Pallas kernels: 33.4 us -> 11.1 us  [pick_rows(): pl.pallas_call(kern, name=name, grid=(peers // per,), out_shape=jax.Shape...]
    concatenate x1 -> x0, local copies, waits for them, and re-layouts: 11.8 us -> none  [device_step(): jnp.concatenate([p.reshape(-1) for p in parts] + [jnp.zeros((peers * rows...]
    slice x2 -> x0, matrix products: 10.3 us -> none  [the longest x1 5.7 us: device_step(): contract(hidden_2, tb_3)[:, :classes]]
    pallas_call x13 -> x12, Pallas kernels: 346 us -> 356 us  [the longest x10 314 us: edge_call(): pl.pallas_call(kern, name=name, grid=(steps,), out_shape=out_shape + more...]
    dot_general x4 -> x6, matrix products: 17.2 us -> 26.7 us  [contract(): return jnp.einsum('nd,ne->de', a, b, preferred_element_type=F32)]
  transfers between devices with their start and end apart: 5 -> 5, of which waited for: 3 -> 3; matrix products, arithmetic and copies ran while one was open for 12% -> 12% of each run, Pallas kernels for 19% -> 21%
where the time goes in v1:
time: 544 us; the launch traced here: 535 us
  Pallas kernels  367 us (67%)
  starting transfers between devices  53.5 us (10%)
  other arithmetic  33.2 us (6%)
  matrix products  26.7 us (5%)
  local copies, waits for them, and re-layouts  23.1 us (4%)
  waiting for transfers between devices  23.1 us (4%)
  between operations  8.06 us (1%)
    pallas_call x10, Pallas kernels, edge_call(): pl.pallas_call(kern, name=name, grid=(steps,), out_shape=out_shape + more...  314 us
    all_to_all x5, starting transfers between devices, exchange(): return lax.all_to_all(x, GROUP_AXIS, 0, 0, tiled=True)  53.5 us
    pallas_call x1, Pallas kernels, sum_over_devices(): pl.pallas_call(kern, name='sum_all', out_shape=jax.ShapeDtypeStruct(shape...  39.1 us
    dot_general x6, matrix products, contract(): return jnp.einsum('nd,ne->de', a, b, preferred_element_type=F32)  26.7 us
    all_to_all x5, waiting for transfers between devices, exchange(): return lax.all_to_all(x, GROUP_AXIS, 0, 0, tiled=True)  23.1 us
    pallas_call x1, Pallas kernels, pick_rows(): pl.pallas_call(kern, name=name, grid=(peers // per,), out_shape=jax.Shape...  11.1 us
  transfers between devices with their start and end apart: 5, of which 3 were waited for; matrix products, arithmetic and copies ran while one was open for 12% of the time, Pallas kernels for 21%

profile of v1, /device:TPU:1, one launch (start us, length us, event | category | flops | bytes accessed | tf_op | source)
XLA Modules:
  0.0 534.5 jit_solution(12236227370196665870)
XLA Ops:
  0.7 0.9 copy.37
  1.6 0.7 reshape.219.idx_ref.refs_7_.refs_12_
  2.3 11.1 %send_1.1 = bf16[128,72,128]{2,1,0:T(8,128)(2,1)} custom-call(s32[8192]{0:T(1024)} %reshape.219.idx_ref.refs_7_.refs_12_, bf16[12288,128]{1,0:T(8,128)(2,1)} %refs_2_.1, f32[96,128]{1,0:T(8,128)} %bitcast.72), custom_call_target="tpu_custom_call" | custom-call | flops 40000000 | bytes 10000000 | tf_op jit(solution)/shard_map/send_1/pallas_call | solution.py:221
  13.5 11.5 %all-to-all-start = ((bf16[128,72,128]{2,1,0:T(8,128)(2,1)}), bf16[128,72,128]{2,1,0:T(8,128)(2,1)S(1)}, u32[]{:S(2)}, u32[]{:S(2)}) async-start(bf16[128,72,128]{2,1,0:T(8,128)(2,1)} %send_1.1), calls=%async_computation | async-start | bytes 4718592 | tf_op jit(solution)/shard_map/all_to_all | solution.py:550
  27.0 8.6 %sort.14 = s32[24576]{0:T(1024)S(1)} sort(s32[24576]{0:T(1024)S(1)} %get-tuple-element.105), dimensions={0}, to_apply=%region_0.0 | sort | flops 368640 | bytes 196608 | tf_op jit(solution)/shard_map/sort | solution.py:578
  35.6 0.8 broadcast_select_fusion
  36.6 0.7 broadcast_select_fusion.1
  40.9 2.0 concatenate.25.meta_ref
  42.9 3.9 broadcast_in_dim.66.refs_1_.refs_3_.refs_4_
  46.8 20.8 %near_1.1.refs_1_ = f32[12288,128]{1,0:T(8,128)} custom-call(s32[774]{0:T(1024)} %concatenate.25.meta_ref, s32[24576]{0:T(1024)} %get-tuple-element.118.idx_ref, s32[192,1,128]{2,1,0:T(1,128)} %bitcast.58, bf16[12288,128]{1,0:T(8,128)(2,1)} %refs_2_.1, f32[12288,128]{1,0:T(8,128)} %broadcast_in_dim.66.refs_1_.refs_3_.refs_4_), custom_call_target="tpu_custom_call" | custom-call | flops 80000000 | bytes 20000000 | tf_op jit(solution)/shard_map/near_1/pallas_call | solution.py:341
  69.2 1.4 copy-done.2
  70.6 36.5 %layer_1.1 = (bf16[12288,128]{1,0:T(8,128)(2,1)}, bf16[12288,256]{1,0:T(8,128)(2,1)}, bf16[128,64,128]{2,1,0:T(8,128)(2,1)}) custom-call(s32[774]{0:T(1024)} %concatenate.25.meta_ref, s32[24576]{0:T(1024)} %get-tuple-element.120.idx_ref, s32[192,1,128]{2,1,0:T(1,128)} %bitcast.55, bf16[128,72,128]{2,1,0:T(8,128)(2,1)} %copy-done.2, ...), custom_call_target="tpu_custom_call" | custom-call | flops 100000000 | bytes 25000000 | tf_op jit(solution)/shard_map/layer_1/pallas_call | solution.py:341
  107.1 11.7 %all-to-all-start.1 = ((bf16[128,64,128]{2,1,0:T(8,128)(2,1)}), bf16[128,64,128]{2,1,0:T(8,128)(2,1)S(1)}, u32[]{:S(2)}, u32[]{:S(2)}) async-start(bf16[128,64,128]{2,1,0:T(8,128)(2,1)} %get-tuple-element.42), calls=%async_computation.1 | async-start | bytes 4194304 | tf_op jit(solution)/shard_map/all_to_all | solution.py:550
  118.8 6.6 %select_convert_fusion.refs_1_.refs_4_ = bf16[12288,128]{1,0:T(8,128)(2,1)} fusion(s32[128]{0:T(128)S(1)} %and_select_fusion, f32[12288]{0:T(1024)S(1)} %copy-done.14, s32[12288]{0:T(1024)S(1)} %copy-done.20, pred[128]{0:T(512)(128)(4,1)S(1)} %iota_compare_fusion.3), kind=kLoop, calls=%fused_computation | loop fusion | flops 9437184 | bytes 3244672 | tf_op jit(solution)/shard_map/convert_element_type | solution.py:602
  125.5 23.8 %near_2.1.refs_2_ = f32[12288,256]{1,0:T(8,128)} custom-call(s32[774]{0:T(1024)} %concatenate.25.meta_ref, s32[24576]{0:T(1024)} %get-tuple-element.116.idx_ref, s32[192,1,128]{2,1,0:T(1,128)} %bitcast.59, bf16[12288,256]{1,0:T(8,128)(2,1)} %get-tuple-element.43.refs_0_.refs_3_.refs_2_), custom_call_target="tpu_custom_call" | custom-call | flops 80000000 | bytes 20000000 | tf_op jit(solution)/shard_map/near_2/pallas_call | solution.py:341
  149.5 1.3 copy-done.7
  150.8 44.5 %layer_2.1 = (bf16[12288,256]{1,0:T(8,128)(2,1)}, bf16[12288,256]{1,0:T(8,128)(2,1)}, bf16[12288,128]{1,0:T(8,128)(2,1)}, f32[12288,128]{1,0:T(8,128)}, bf16[128,64,128]{2,1,0:T(8,128)(2,1)}) custom-call(s32[774]{0:T(1024)} %concatenate.25.meta_ref, s32[24576]{0:T(1024)} %get-tuple-element.117.idx_ref, s32[192,1,128]{2,1,0:T(1,128)} %bitcast.56, ...), custom_call_target="tpu_custom_call" | custom-call | flops 160000000 | bytes 40000000 | tf_op jit(solution)/shard_map/layer_2/pallas_call | solution.py:341
  195.4 11.0 %all-to-all-start.2 = ((bf16[128,64,128]{2,1,0:T(8,128)(2,1)}), bf16[128,64,128]{2,1,0:T(8,128)(2,1)S(1)}, u32[]{:S(2)}, u32[]{:S(2)}) async-start(bf16[128,64,128]{2,1,0:T(8,128)(2,1)} %get-tuple-element.44), calls=%async_computation.2 | async-start | bytes 4194304 | tf_op jit(solution)/shard_map/all_to_all | solution.py:550
  206.4 7.3 %sort.15 = s32[32768]{0:T(1024)S(1)} sort(s32[32768]{0:T(1024)S(1)} %pad_add_fusion), dimensions={0}, to_apply=%region_4.5 | sort | flops 491520 | bytes 262144 | tf_op jit(solution)/shard_map/sort | solution.py:650
  213.7 0.7 and_or_fusion
  215.8 1.0 slice_convert_fusion
  220.1 2.6 concatenate.26.refs_8_.meta_ref
  222.8 20.8 %near_3.1.refs_1_ = f32[12288,128]{1,0:T(8,128)} custom-call(s32[774]{0:T(1024)} %concatenate.25.meta_ref, s32[24576]{0:T(1024)} %get-tuple-element.118.idx_ref, s32[192,1,128]{2,1,0:T(1,128)} %bitcast.60, bf16[12288,128]{1,0:T(8,128)(2,1)} %get-tuple-element.45.refs_0_, bf16[12288,128]{1,0:T(8,128)(2,1)} %select_convert_fusion.refs_1_.refs_4_), custom_call_target="tpu_custom_call" | custom-call | flops 80000000 | bytes 20000000 | tf_op jit(solution)/shard_map/near_3/pallas_call | solution.py:341
  244.1 0.8 tile.13
  245.0 50.5 %layer_3.1 = (bf16[12288,128]{1,0:T(8,128)(2,1)}, bf16[12288,128]{1,0:T(8,128)(2,1)}, f32[8,128]{1,0:T(8,128)}, f32[8,128]{1,0:T(8,128)}, bf16[8192,128]{1,0:T(8,128)(2,1)}) custom-call(s32[774]{0:T(1024)} %concatenate.25.meta_ref, s32[24576]{0:T(1024)} %get-tuple-element.120.idx_ref, s32[192,1,128]{2,1,0:T(1,128)} %bitcast.57, bf16[8192,128]{1,0:T(8,128)(2,1)} %bitcast.51, ...), custom_call_target="tpu_custom_call" | custom-call | flops 120000000 | bytes 30000000 | tf_op jit(solution)/shard_map/layer_3/pallas_call | solution.py:341
  295.5 12.3 %all-to-all-start.3 = ((bf16[128,64,128]{2,1,0:T(8,128)(2,1)}), bf16[128,64,128]{2,1,0:T(8,128)(2,1)S(1)}, u32[]{:S(2)}, u32[]{:S(2)}) async-start(bf16[128,64,128]{2,1,0:T(8,128)(2,1)} %bitcast.54), calls=%async_computation.3 | async-start | bytes 4194304 | tf_op jit(solution)/shard_map/all_to_all | solution.py:550
  307.8 0.8 copy.44
  309.2 20.6 %back_3_own.1.refs_1_ = f32[12288,128]{1,0:T(8,128)} custom-call(s32[905]{0:T(1024)} %concatenate.26.refs_8_.meta_ref, s32[24576]{0:T(1024)} %get-tuple-element.111.refs_9_.idx_ref, s32[192,1,128]{2,1,0:T(1,128)} %bitcast.61, bf16[12288,128]{1,0:T(8,128)(2,1)} %get-tuple-element.48.refs_0_), custom_call_target="tpu_custom_call" | custom-call | flops 80000000 | bytes 20000000 | tf_op jit(solution)/shard_map/back_3_own/pallas_call | solution.py:341
  329.9 12.2 %all-to-all-done.3 = bf16[128,64,128]{2,1,0:T(8,128)(2,1)S(1)} async-done(((bf16[128,64,128]{2,1,0:T(8,128)(2,1)}), bf16[128,64,128]{2,1,0:T(8,128)(2,1)S(1)}, u32[]{:S(2)}, u32[]{:S(2)}) %all-to-all-start.3) | async-done | bytes 2097184 | tf_op jit(solution)/shard_map/all_to_all | solution.py:550
  342.0 1.3 copy-done.8
  343.3 46.6 %owner_3.1 = (bf16[12288,128]{1,0:T(8,128)(2,1)}, bf16[12288,256]{1,0:T(8,128)(2,1)}, bf16[12288,256]{1,0:T(8,128)(2,1)}, f32[8,256]{1,0:T(8,128)}, bf16[8192,256]{1,0:T(8,128)(2,1)}) custom-call(s32[905]{0:T(1024)} %concatenate.26.refs_8_.meta_ref, s32[8192]{0:T(1024)} %get-tuple-element.113.idx_ref, s32[64,1,128]{2,1,0:T(1,128)} %bitcast.70, ...), custom_call_target="tpu_custom_call" | custom-call | flops 120000000 | bytes 30000000 | tf_op jit(solution)/shard_map/owner_3/pallas_call | solution.py:341
  389.9 7.0 %all-to-all-start.4 = ((bf16[128,64,256]{2,1,0:T(8,128)(2,1)}), bf16[128,64,256]{2,1,0:T(8,128)(2,1)}, u32[]{:S(2)}, u32[]{:S(2)}) async-start(bf16[128,64,256]{2,1,0:T(8,128)(2,1)} %bitcast.53), calls=%async_computation.4 | async-start | bytes 8388608 | tf_op jit(solution)/shard_map/all_to_all | solution.py:550
  397.0 0.8 copy.45
  397.7 4.6 fusion.21
  402.4 27.1 %back_2_own.1.refs_1_ = f32[12288,256]{1,0:T(8,128)} custom-call(s32[905]{0:T(1024)} %concatenate.26.refs_8_.meta_ref, s32[24576]{0:T(1024)} %get-tuple-element.109.refs_9_.idx_ref, s32[192,1,128]{2,1,0:T(1,128)} %bitcast.62, bf16[12288,256]{1,0:T(8,128)(2,1)} %get-tuple-element.52.refs_0_, bf16[12288,256]{1,0:T(8,128)(2,1)} %get-tuple-element.53.refs_1_, ...), custom_call_target="tpu_custom_call" | custom-call | flops 120000000 | bytes 30000000 | tf_op jit(solution)/shard_map/back_2_own/pallas_call | solution.py:341
  429.5 5.4 %convolution_select_fusion.refs_4_ = f32[256,128]{1,0:T(8,128)} fusion(f32[256,128]{1,0:T(8,128)S(1)} %fusion.21, bf16[12288,256]{1,0:T(8,128)(2,1)} %get-tuple-element.50.refs_3_, bf16[12288,128]{1,0:T(8,128)(2,1)S(1)} %copy-done.4, pred[128]{0:T(512)(128)(4,1)S(1)} %iota_compare_fusion.2), kind=kOutput, calls=%fused_computation.2 | convolution fusion | flops 805339136 | bytes 9699456 | tf_op jit(solution)/shard_map/nd,ne->de/dot_general | solution.py:782
  434.9 7.3 %fusion.19.refs_2_ = f32[256,256]{1,0:T(8,128)} fusion(bf16[12288,256]{1,0:T(8,128)(2,1)} %get-tuple-element.43.refs_0_.refs_3_.refs_2_, bf16[12288,256]{1,0:T(8,128)(2,1)} %get-tuple-element.53.refs_1_), kind=kOutput, calls=%fused_computation.75 | convolution fusion | flops 1610612736 | bytes 12845056 | tf_op jit(solution)/shard_map/nd,ne->de/dot_general | solution.py:782
  442.2 2.5 fusion.20.refs_3_
  444.8 10.7 %all-to-all-done.4 = bf16[128,64,256]{2,1,0:T(8,128)(2,1)} async-done(((bf16[128,64,256]{2,1,0:T(8,128)(2,1)}), bf16[128,64,256]{2,1,0:T(8,128)(2,1)}, u32[]{:S(2)}, u32[]{:S(2)}) %all-to-all-start.4) | async-done | bytes 4194336 | tf_op jit(solution)/shard_map/all_to_all | solution.py:550
  455.5 23.2 %owner_2.1 = (bf16[12288,256]{1,0:T(8,128)(2,1)}, f32[8,256]{1,0:T(8,128)}) custom-call(s32[905]{0:T(1024)} %concatenate.26.refs_8_.meta_ref, s32[8192]{0:T(1024)} %get-tuple-element.114.idx_ref, s32[64,1,128]{2,1,0:T(1,128)} %bitcast.71, bf16[8192,256]{1,0:T(8,128)(2,1)} %bitcast.25.refs_0_, f32[12288,256]{1,0:T(8,128)} %back_2_own.1.refs_1_, ...), custom_call_target="tpu_custom_call" | custom-call | flops 100000000 | bytes 25000000 | tf_op jit(solution)/shard_map/owner_2/pallas_call | solution.py:341
  478.7 5.0 convolution_bitcast_fusion.refs_0_
  484.3 1.9 fusion.18.refs_1_
  486.1 39.1 %sum_all.1.full_ref = f32[2,64,16,128]{3,2,1,0:T(8,128)} custom-call(f32[128,256]{1,0:T(8,128)} %convolution_bitcast_fusion.refs_0_, f32[128,256]{1,0:T(8,128)} %fusion.18.refs_1_, f32[256,256]{1,0:T(8,128)} %fusion.19.refs_2_, f32[256,256]{1,0:T(8,128)} %fusion.20.refs_3_, f32[256,128]{1,0:T(8,128)} %convolution_select_fusion.refs_4_, ...), custom_call_target="tpu_custom_call" | custom-call | flops 100000000 | bytes 25000000 | tf_op jit(solution)/shard_map/sum_all/pallas_call | solution.py:485
  525.3 2.2 unpack_sums.1
  527.4 1.3 reduce_sum.39
  529.4 1.1 fusion.17
  530.4 0.7 copy.47
  531.8 1.1 slice_bitcast_fusion
  (83 shorter events, 10.2 us)
Async XLA Ops:
  0.6 24.3 %copy-start.15 = (s32[24576]{0:T(1024)S(1)}, s32[24576]{0:T(1024)}, u32[]{:S(2)}) copy-start(s32[24576]{0:T(1024)} %param.20) | copy-start | bytes 294916
  0.7 24.3 %copy-start.16 = (s32[24576]{0:T(1024)S(1)}, s32[24576]{0:T(1024)}, u32[]{:S(2)}) copy-start(s32[24576]{0:T(1024)} %param.21) | copy-start | bytes 294916
  0.7 39.3 %copy-start.17 = (bf16[256,40]{0,1:T(8,128)(2,1)S(1)}, bf16[256,40]{0,1:T(8,128)(2,1)}, u32[]{:S(2)}) copy-start(bf16[256,40]{0,1:T(8,128)(2,1)} %param.30) | copy-start | bytes 61444
  0.7 39.4 %copy-start.18 = (bf16[256,40]{0,1:T(8,128)(2,1)S(1)}, bf16[256,40]{0,1:T(8,128)(2,1)}, u32[]{:S(2)}) copy-start(bf16[256,40]{0,1:T(8,128)(2,1)} %param.29) | copy-start | bytes 61444
  0.7 42.2 %copy-start.19 = (f32[12288]{0:T(1024)S(1)}, f32[12288]{0:T(1024)}, u32[]{:S(2)}) copy-start(f32[12288]{0:T(1024)} %param.22) | copy-start | bytes 147460
  13.5 55.7 %all-to-all-start = ((bf16[128,72,128]{2,1,0:T(8,128)(2,1)}), bf16[128,72,128]{2,1,0:T(8,128)(2,1)S(1)}, u32[]{:S(2)}, u32[]{:S(2)}) async-start(bf16[128,72,128]{2,1,0:T(8,128)(2,1)} %send_1.1), calls=%async_computation | async-start | bytes 4718592 | tf_op jit(solution)/shard_map/all_to_all | solution.py:550
  46.7 20.8 %copy-start.21 = (f32[40]{0:T(128)S(1)}, f32[40]{0:T(128)}, u32[]{:S(2)}) copy-start(f32[40]{0:T(128)} %param.31) | copy-start | bytes 484
  46.8 22.4 %copy-start.10 = (s32[8192]{0:T(1024)S(1)}, s32[8192]{0:T(1024)}, u32[]{:S(2)}) copy-start(s32[8192]{0:T(1024)} %reshape.219.idx_ref.refs_7_.refs_12_) | copy-start | bytes 98308
  69.2 1.4 copy-start.2
  70.6 48.2 %copy-start.14 = (f32[12288]{0:T(1024)S(1)}, f32[12288]{0:T(1024)}, u32[]{:S(2)}) copy-start(f32[12288]{0:T(1024)} %param.18) | copy-start | bytes 147460
  70.6 48.3 %copy-start.20 = (s32[12288]{0:T(1024)S(1)}, s32[12288]{0:T(1024)}, u32[]{:S(2)}) copy-start(s32[12288]{0:T(1024)} %param.17) | copy-start | bytes 147460
  107.1 42.5 %all-to-all-start.1 = ((bf16[128,64,128]{2,1,0:T(8,128)(2,1)}), bf16[128,64,128]{2,1,0:T(8,128)(2,1)S(1)}, u32[]{:S(2)}, u32[]{:S(2)}) async-start(bf16[128,64,128]{2,1,0:T(8,128)(2,1)} %get-tuple-element.42), calls=%async_computation.1 | async-start | bytes 4194304 | tf_op jit(solution)/shard_map/all_to_all | solution.py:550
  149.5 1.3 copy-start.7
  195.4 48.2 %all-to-all-start.2 = ((bf16[128,64,128]{2,1,0:T(8,128)(2,1)}), bf16[128,64,128]{2,1,0:T(8,128)(2,1)S(1)}, u32[]{:S(2)}, u32[]{:S(2)}) async-start(bf16[128,64,128]{2,1,0:T(8,128)(2,1)} %get-tuple-element.44), calls=%async_computation.2 | async-start | bytes 4194304 | tf_op jit(solution)/shard_map/all_to_all | solution.py:550
  214.4 29.1 %copy-start.9 = (s32[24576]{0:T(1024)}, s32[24576]{0:T(1024)S(1)}, u32[]{:S(2)}) copy-start(s32[24576]{0:T(1024)S(1)} %get-tuple-element.112) | copy-start | bytes 294916
  215.5 28.1 %copy-start.13 = (s32[8192]{0:T(1024)}, s32[8192]{0:T(1024)S(1)}, u32[]{:S(2)}) copy-start(s32[8192]{0:T(1024)S(1)} %get-tuple-element.115) | copy-start | bytes 98308
  243.6 1.4 copy-start.6
  245.0 62.8 %copy-start.11 = (bf16[256,256]{1,0:T(8,128)(2,1)S(1)}, bf16[256,256]{1,0:T(8,128)(2,1)}, u32[]{:S(2)}) copy-start(bf16[256,256]{1,0:T(8,128)(2,1)} %refs_6_.1) | copy-start | bytes 393220
  295.5 46.5 %all-to-all-start.3 = ((bf16[128,64,128]{2,1,0:T(8,128)(2,1)}), bf16[128,64,128]{2,1,0:T(8,128)(2,1)S(1)}, u32[]{:S(2)}, u32[]{:S(2)}) async-start(bf16[128,64,128]{2,1,0:T(8,128)(2,1)} %bitcast.54), calls=%async_computation.3 | async-start | bytes 4194304 | tf_op jit(solution)/shard_map/all_to_all | solution.py:550
  342.0 1.3 copy-start.8
  389.9 7.0 %copy-start.12 = (bf16[256,256]{1,0:T(8,128)(2,1)S(1)}, bf16[256,256]{1,0:T(8,128)(2,1)}, u32[]{:S(2)}) copy-start(bf16[256,256]{1,0:T(8,128)(2,1)} %refs_5_.3) | copy-start | bytes 393220
  389.9 7.8 %copy-start.1 = (bf16[12288,128]{1,0:T(8,128)(2,1)S(1)}, bf16[12288,128]{1,0:T(8,128)(2,1)}, u32[]{:S(2)}) copy-start(bf16[12288,128]{1,0:T(8,128)(2,1)} %get-tuple-element.49.refs_2_) | copy-start | bytes 9437188
  389.9 65.6 %all-to-all-start.4 = ((bf16[128,64,256]{2,1,0:T(8,128)(2,1)}), bf16[128,64,256]{2,1,0:T(8,128)(2,1)}, u32[]{:S(2)}, u32[]{:S(2)}) async-start(bf16[128,64,256]{2,1,0:T(8,128)(2,1)} %bitcast.53), calls=%async_computation.4 | async-start | bytes 8388608 | tf_op jit(solution)/shard_map/all_to_all | solution.py:550
  402.4 27.1 %copy-start.4 = (bf16[12288,128]{1,0:T(8,128)(2,1)S(1)}, bf16[12288,128]{1,0:T(8,128)(2,1)}, u32[]{:S(2)}) copy-start(bf16[12288,128]{1,0:T(8,128)(2,1)} %get-tuple-element.56) | copy-start | bytes 9437188
  429.5 12.7 %slice-start = ((s8[6291456]{0:T(1024)(128)(4,1)}), s8[4194304]{0:T(1024)(128)(4,1)S(1)}, s32[]{:S(2)}) async-start(s8[6291456]{0:T(1024)(128)(4,1)} %bitcast.47), calls=%async_computation.5 | async-start | bytes 8388608
  429.5 12.7 %slice-start.2 = ((s8[6291456]{0:T(1024)(128)(4,1)}), s8[4194304]{0:T(1024)(128)(4,1)S(1)}, s32[]{:S(2)}) async-start(s8[6291456]{0:T(1024)(128)(4,1)} %bitcast.49), calls=%async_computation.7 | async-start | bytes 8388608
  434.9 7.3 %slice-start.1 = ((s8[6291456]{0:T(1024)(128)(4,1)}), s8[2097152]{0:T(1024)(128)(4,1)S(1)}, s32[]{:S(2)}) async-start(s8[6291456]{0:T(1024)(128)(4,1)} %bitcast.47), calls=%async_computation.6 | async-start | bytes 4194304
  434.9 7.3 %slice-start.3 = ((s8[6291456]{0:T(1024)(128)(4,1)}), s8[2097152]{0:T(1024)(128)(4,1)S(1)}, s32[]{:S(2)}) async-start(s8[6291456]{0:T(1024)(128)(4,1)} %bitcast.49), calls=%async_computation.8 | async-start | bytes 4194304
  455.5 23.2 %copy-start = (bf16[12288,128]{1,0:T(8,128)(2,1)S(1)}, bf16[12288,128]{1,0:T(8,128)(2,1)}, u32[]{:S(2)}) copy-start(bf16[12288,128]{1,0:T(8,128)(2,1)} %refs_2_.1) | copy-start | bytes 9437188
  478.7 5.0 copy-start.3
  478.7 5.6 %copy-start.5 = (bf16[12288,128]{1,0:T(8,128)(2,1)S(1)}, bf16[12288,128]{1,0:T(8,128)(2,1)}, u32[]{:S(2)}) copy-start(bf16[12288,128]{1,0:T(8,128)(2,1)} %get-tuple-element.40) | copy-start | bytes 9437188

commit v2 on v1

--- a/solution.py
+++ b/solution.py
@@ -92,12 +92,13 @@
     lax.fori_loop(0, rows // step, body, 0)
 
 
-def gather_16(idx, first, tab, nc):
+def gather_16(idx, base, first, reach, tab, nc, stride=1):
     sub = lax.broadcasted_iota(jnp.int32, (8, LANES), 0)
+    room = idx.shape[0] - (reach - 1) * stride
     halves = [[None, None] for _ in range(nc)]
     for h in range(2):
         for k in range(8):
-            at = idx[first + h * 8 + k]
+            at = idx.at[pl.ds((first + h * 8 + k) * stride, room)][base]
             for c in range(nc):
                 row = jnp.broadcast_to(tab[pl.ds(at + 8 * c, 1), :], (8, LANES))
                 halves[c][h] = row if k == 0 else jnp.where(sub == k, row, halves[c][h])
@@ -108,9 +109,9 @@
     unroll = group_of(blocks)
     first_trip, end_trip, most = [meta[meta_at + 2 * blocks + k] for k in range(3)]
 
-    def fill(b, buf):
+    def fill(base, first, reach, buf):
         for g in range(BLOCK // 16):
-            parts = gather_16(idx, b * BLOCK + g * 16, tab, nc)
+            parts = gather_16(idx, base, first + g * 16, reach, tab, nc)
             for c in range(nc):
                 buf[g * 16:g * 16 + 16, c * LANES:(c + 1) * LANES] = parts[c]
 
@@ -121,14 +122,19 @@
     def add(at, x):
         acc[pl.ds(pl.multiple_of(at, 8), window), :] += x
 
-    fill(jnp.minimum(first_trip * unroll, blocks - 1), bufs[0])
+    span = unroll * BLOCK
+    last_trip = blocks // unroll - 1
+    fill(jnp.minimum(first_trip, last_trip) * span, 0, span, bufs[0])
 
     def body(t, carry):
         before = None
         for u in range(unroll):
             b = t * unroll + u
             now = (meta[meta_at + b], sums(b, meta[meta_at + b], bufs[u % 2]))
-            fill(jnp.minimum(b + 1, blocks - 1), bufs[(u + 1) % 2])
+            if u + 1 < unroll:
+                fill(t * span, (u + 1) * BLOCK, span, bufs[(u + 1) % 2])
+            else:
+                fill(jnp.minimum(t + 1, last_trip) * span, 0, span, bufs[0])
             if before is not None:
                 add(*before)
             before = now
@@ -143,7 +149,7 @@
 
             @pl.when(count > 1)
             def _():
-                fill(b, bufs[0])
+                fill(b * BLOCK, 0, BLOCK, bufs[0])
 
                 def more(w, c):
                     at = meta[meta_at + b] + w * window
@@ -207,17 +213,18 @@
                 digits = jnp.where(lane == 0, high, jnp.where(lane == 1, total - high * LANES, 0.0))
                 tail[...] = jnp.where(first, digits, 0.0).astype(BF16)
             unpack(copies, stage, tab, 0, 1)
+        first = pl.program_id(0) * per
 
         def body(p, carry):
             for g in range(slots // 16):
-                out[p, g * 16:g * 16 + 16, :] = gather_16(idx_ref, p * slots + g * 16, tab, 1)[0]
+                out[p, g * 16:g * 16 + 16, :] = gather_16(idx_ref, first + p, g * 16, slots, tab, 1, peers)[0]
             if extra:
                 out[p, slots:slots + extra, :] = tail[...]
             return carry
         lax.fori_loop(0, per, body, 0)
 
     operands = [idx, src] + ([mask] if extra else [])
-    specs = [pl.BlockSpec((per * slots,), lambda i: (i,), memory_space=pltpu.SMEM), HBM_SPEC] + ([whole_spec(mask.shape)] if extra else [])
+    specs = [SMEM_SPEC, HBM_SPEC] + ([whole_spec(mask.shape)] if extra else [])
     return pl.pallas_call(
         kern, name=name, grid=(peers // per,),
         out_shape=jax.ShapeDtypeStruct((peers, slots + extra, LANES), BF16),
@@ -231,7 +238,7 @@
 def pick_into(idx, tab, stage, peers, slots):
     def body(p, carry):
         for g in range(slots // 16):
-            stage[p, g * 16:g * 16 + 16, :] = gather_16(idx, p * slots + g * 16, tab, 1)[0]
+            stage[p, g * 16:g * 16 + 16, :] = gather_16(idx, p, g * 16, slots, tab, 1, peers)[0]
         return carry
     lax.fori_loop(0, peers, body, 0)
 
@@ -243,7 +250,7 @@
 
 
 def edge_call(name, edges, nc, table_rows, acc_rows, window, sources, build, hbm_in, blocked, fixed, outs, rows_out,
-              tile, epilogue, micros, init=None, sub=1024, keep=0, pick=None, then=None):
+              tile, epilogue, micros, init=None, late=False, sub=1024, keep=0, pick=None, then=None):
     meta, meta_at, idx, seg = edges
     blocks = seg.shape[0]
     width = nc * LANES
@@ -253,6 +260,7 @@
     steps = 1 if epilogue is None else rows_out // tile
     sub = math.gcd(sub, tile)
     more_in, more_specs, more_out, more_scratch = [], [], [], []
+    late_scratch = [pltpu.VMEM((acc_rows, width), F32)] if late else []
     if keep:
         more_scratch.append(pltpu.VMEM((rows_out * keep, LANES), F32))
     if pick:
@@ -281,25 +289,29 @@
         last_out, refs = refs[:len(more_out)], refs[len(more_out):]
         tab, acc, buf_0, buf_1, isem = refs[:5]
         stages, sems, scratch = refs[5:5 + ns], refs[5 + ns:5 + 2 * ns], refs[5 + 2 * ns:]
+        if late:
+            begin, scratch = scratch[0], scratch[1:]
         i = pl.program_id(0)
 
         @pl.when(i == 0)
         def _():
             copies = [fetch(h, st, sm, parts) for h, st, sm in zip(hb, stages, sems)]
-            if init is None:
+            if init is not None:
+                start = pltpu.make_async_copy(hb[init], begin if late else acc.at[pl.ds(0, acc_rows), :], isem)
+                start.start()
+            if init is None or late:
                 zero_rows(acc)
-            else:
-                start = pltpu.make_async_copy(hb[init], acc.at[pl.ds(0, acc_rows), :], isem)
-                start.start()
             for o, (_, _, sums) in zip(out, outs):
                 if sums:
                     o[...] = jnp.zeros_like(o)
             if then:
                 zero_rows(scratch[1])
             build(copies, stages, tab, fx)
-            if init is not None:
+            if init is not None and not late:
                 start.wait()
             segment_sums(meta_ref, meta_at, idx_ref, seg_ref, tab, acc, (buf_0, buf_1), nc, window, blocks)
+            if late:
+                start.wait()
             if epilogue is None:
                 send_out(acc.at[pl.ds(0, acc_rows), :], out[0], isem)
         if epilogue is not None:
@@ -309,7 +321,10 @@
 
                 def put(x):
                     put_rows(scratch[0], row0, x, keep)
-                epilogue(acc[pl.ds(row0, sub), :], [r.at[pl.ds(at, sub), :] for r in bl], fx,
+                a = acc[pl.ds(row0, sub), :]
+                if late:
+                    a = a + begin[pl.ds(row0, sub), :]
+                epilogue(a, [r.at[pl.ds(at, sub), :] for r in bl], fx,
                          [o if sums else o.at[pl.ds(at, sub), :] for o, (_, _, sums) in zip(out, outs)], put)
                 return carry
             lax.fori_loop(0, tile // sub, part, 0)
@@ -347,7 +362,7 @@
                          pltpu.VMEM((BLOCK, width), BF16), pltpu.VMEM((BLOCK, width), BF16),
                          pltpu.SemaphoreType.DMA(())]
                         + [pltpu.VMEM(shape, BF16) for shape in sources]
-                        + [pltpu.SemaphoreType.DMA((parts,)) for _ in sources] + more_scratch),
+                        + [pltpu.SemaphoreType.DMA((parts,)) for _ in sources] + late_scratch + more_scratch),
         compiler_params=params(), cost_estimate=cost(micros))(meta, idx, seg, *hbm_in, *blocked, *fixed, *more_in)
 
 
@@ -365,7 +380,7 @@
     return places, at
 
 
-def sum_over_devices(grads, sums, peers):
+def sum_over_devices(grads, sums, total, classes, peers):
     chips = peers // 2
     places, used = grad_places([g.shape for g in grads] + [(SHARE, LANES)])
     rounds = -(-used // peers)
@@ -491,25 +506,32 @@
                         pltpu.SemaphoreType.DMA((chips,)), pltpu.SemaphoreType.DMA((chips,))],
         compiler_params=pltpu.CompilerParams(has_side_effects=True), cost_estimate=cost(25))(*grads, *sums)
 
-    def unpack_kern(full_ref, *outs):
-        def at(q):
+    def unpack_kern(full_ref, total_ref, *outs):
+        def part(q):
             unit = q // rounds
-            return unit // chips, unit % chips, (q % rounds) * SHARE
-        for o, columns in zip(outs, places):
+            r = (q % rounds) * SHARE
+            return full_ref[unit // chips, unit % chips, r:r + SHARE, :]
+        for o, columns in zip(outs, places[:-2]):
             for w, first in enumerate(columns):
                 for k in range(o.shape[0] // SHARE):
-                    h, c, r = at(first + k)
-                    o[k * SHARE:(k + 1) * SHARE, w * LANES:(w + 1) * LANES] = full_ref[h, c, r:r + SHARE, :]
-        h, c, r = at(places[-1][0])
-        small, line = full_ref[h, c, r:r + SHARE, :], 0
-        for o, width in zip(outs[len(grads):], widths):
+                    o[k * SHARE:(k + 1) * SHARE, w * LANES:(w + 1) * LANES] = part(first + k)
+        o_self, o_neigh = outs[len(grads) - 1], outs[len(grads)]
+        for k in range(o_self.shape[0] // SHARE):
+            both = part(places[-2][0] + k)
+            o_self[k * SHARE:(k + 1) * SHARE, :] = both[:, :classes]
+            o_neigh[k * SHARE:(k + 1) * SHARE, :] = pltpu.roll(both, LANES - SPREAD, 1)[:, :classes]
+        small, line = part(places[-1][0]), 0
+        for o, width in zip(outs[len(grads) + 1:-1], widths):
             for w in range(width // LANES):
-                o[:, w * LANES:(w + 1) * LANES] = small[line:line + 1, :]
+                wide = min(LANES, o.shape[1] - w * LANES)
+                o[:, w * LANES:w * LANES + wide] = small[line:line + 1, :wide]
                 line += 1
-    outs = [jax.ShapeDtypeStruct(g.shape, F32) for g in grads] + [jax.ShapeDtypeStruct((1, w), F32) for w in widths]
-    got = pl.pallas_call(unpack_kern, name='unpack_sums', out_shape=outs, in_specs=[vmem], out_specs=[vmem] * len(outs),
-                         cost_estimate=cost(3))(full)
-    return got[:len(grads)], got[len(grads):]
+        outs[-1][...] = jnp.sum(small[line:line + 1, :], axis=1, keepdims=True) / total_ref[...]
+    rows_3 = grads[-1].shape[0]
+    outs = ([g.shape for g in grads[:-1]] + [(rows_3, classes)] * 2
+            + [(1, w) for w in widths[:-2]] + [(1, classes), (1, 1)])
+    return pl.pallas_call(unpack_kern, name='unpack_sums', out_shape=[jax.ShapeDtypeStruct(o, F32) for o in outs],
+                          in_specs=[vmem, vmem], out_specs=[vmem] * len(outs), cost_estimate=cost(3))(full, total)
 
 
 def edge_meta(seg_first, seg_last, window, first_block, end_block):
@@ -558,7 +580,7 @@
         edges = src_idx.shape[0]
         hidden = w_self_1.shape[1]
         classes = w_self_3.shape[1]
-        send_flat = send_idx.reshape(-1)
+        send_flat = send_idx.T.reshape(-1)
         tile = next(t for t in (4096, 1024) if n % t == 0)
         half_tile = tile // 2
         slot_bits = bits_for(halo)
@@ -641,11 +663,12 @@
         mean_1, hidden_1, out_2 = edge_call(
             'layer_1', (meta_f, far_at, src_far, seg_far), 1, halo, n, win_e, [(peers, slots + TAIL, LANES)], build_1,
             [got_1, near_1], [features, inv], [w_self_1, w_neigh_1, b1],
-            [((n, LANES), BF16, False), ((n, hidden), BF16, False)], n, tile, epi_1, 25, init=1,
+            [((n, LANES), BF16, False), ((n, hidden), BF16, False)], n, tile, epi_1, 25, init=1, late=True,
             keep=1, pick=(send_flat, peers, slots))
 
+        place = jnp.arange(halo, dtype=jnp.int32)
         keys = jnp.concatenate([(src_idx << dst_bits) | dst_idx,
-                                (1 << 30) | (send_flat << slot_bits) | jnp.arange(halo, dtype=jnp.int32)])
+                                (1 << 30) | (send_flat << slot_bits) | (place % peers * slots + place // peers)])
         keys = lax.optimization_barrier((keys, mean_1))[0]
         ordered = lax.sort(keys, is_stable=False)
         by_src, by_row = ordered[:edges], ordered[edges:] & ((1 << 30) - 1)
@@ -732,7 +755,8 @@
             'layer_3', (meta_f, far_at, src_far, seg_far), 1, halo, n, win_e, [(halo, LANES)], rows_of(1), [got_3, near_3],
             [logits_self, inv, target], [b3, jnp.broadcast_to(inv_total, (1, LANES)), folder],
             [((n, LANES), BF16, False), ((n, LANES), BF16, False), ((8, LANES), F32, True), ((8, LANES), F32, True)],
-            n, tile, epi_3, 30, init=1, keep=1, then=((meta_b, halo_at, dst_s, seg_h), 1, halo, win_h, finish_3))
+            n, half_tile, epi_3, 30, init=1, late=True, keep=1,
+            then=((meta_b, halo_at, dst_s, seg_h), 1, halo, win_h, finish_3))
 
         ret_3 = exchange(back_3.reshape(peers, slots, LANES)).reshape(halo, LANES)
         own_3 = edge_call('back_3_own', (meta_b, own_at, dst_s, seg_o), 1, n, n, win_e, [(n, LANES)], rows_of(1),
@@ -758,7 +782,7 @@
             'owner_3', (meta_b, owner_at, slot_s, seg_r), 1, halo, n, win_r, [(halo, LANES)], rows_of(1), [ret_3, own_3],
             [d_bf_3, hidden_2, inv], [jnp.concatenate([ws3_t, wn3_t], axis=0), w_neigh_2.T, folder],
             [((n, LANES), BF16, False), ((n, hidden), BF16, False), ((n, hidden), BF16, False), ((8, hidden), F32, True)],
-            n, half_tile, epi_o3, 30, init=1, sub=512, keep=2,
+            n, half_tile, epi_o3, 30, init=1, late=True, sub=512, keep=2,
             then=((meta_b, halo_at, dst_wide, seg_h), 2, halo, win_h, finish_2))
 
         def epi_b2o(a, bl, fx, out, put):
@@ -776,18 +800,17 @@
         d_bf_1, g_b1 = edge_call(
             'owner_2', (meta_b, owner_at, tile_linear(slot_s), seg_r), 2, halo, n, win_r, [(halo, hidden)], rows_of(2),
             [ret_2, own_2], [hidden_1], [], [((n, hidden), BF16, False), ((8, hidden), F32, True)], n, tile, epi_o2, 25,
-            init=1)
+            init=1, late=True)
 
         def contract(a, b):
             return jnp.einsum('nd,ne->de', a, b, preferred_element_type=F32)
 
         at = jnp.arange(LANES, dtype=jnp.int32)[None, :]
         g_3 = jnp.where(at < SPREAD, contract(hidden_2, d_bf_3), contract(hidden_2, tb_3))
-        g, sums = sum_over_devices([contract(features, d_bf_1), contract(mean_1, d_bf_1), contract(hidden_1, d_bf_2),
-                                    contract(mean_2, d_bf_2), g_3], [g_b1, g_b2, g_b3, loss_parts], peers)
-        loss = jnp.sum(sums[3]) / total
-        return (loss, g[0], g[1], sums[0].reshape(-1), g[2], g[3], sums[1].reshape(-1), g[4][:, :classes],
-                g[4][:, SPREAD:SPREAD + classes], sums[2].reshape(-1)[:classes])
+        g1s, g1n, g2s, g2n, g3s, g3n, s1, s2, s3, loss = sum_over_devices(
+            [contract(features, d_bf_1), contract(mean_1, d_bf_1), contract(hidden_1, d_bf_2), contract(mean_2, d_bf_2), g_3],
+            [g_b1, g_b2, g_b3, loss_parts], total.reshape(1, 1), classes, peers)
+        return (loss.reshape(()), g1s, g1n, s1.reshape(-1), g2s, g2n, s2.reshape(-1), g3s, g3n, s3.reshape(-1))
 
     sharded = P(GROUP_AXIS)
     whole = P()

time: 544 us -> 497 us (0.914)
  Pallas kernels: 367 us -> 320 us
  waiting for transfers between devices: 23.1 us -> 35.6 us
  starting transfers between devices: 53.5 us -> 48 us
    pallas_call x10, Pallas kernels: 314 us -> 269 us  [edge_call(): pl.pallas_call(kern, name=name, grid=(steps,), out_shape=out_shape + more...]
    all_to_all x5, waiting for transfers between devices: 23.1 us -> 35.6 us  [exchange(): return lax.all_to_all(x, GROUP_AXIS, 0, 0, tiled=True)]
  transfers between devices with their start and end apart: 5 -> 5, of which waited for: 3 -> 4; matrix products, arithmetic and copies ran while one was open for 12% -> 13% of each run, Pallas kernels for 21% -> 20%
where the time goes in v2:
time: 497 us; the launch traced here: 489 us
  Pallas kernels  320 us (64%)
  starting transfers between devices  48 us (10%)
  waiting for transfers between devices  35.6 us (7%)
  other arithmetic  31.9 us (6%)
  matrix products  26.7 us (5%)
  local copies, waits for them, and re-layouts  21.1 us (4%)
  between operations  6.02 us (1%)
    pallas_call x10, Pallas kernels, edge_call(): pl.pallas_call(kern, name=name, grid=(steps,), out_shape=out_shape + more...  269 us
    all_to_all x5, starting transfers between devices, exchange(): return lax.all_to_all(x, GROUP_AXIS, 0, 0, tiled=True)  48 us
    pallas_call x1, Pallas kernels, sum_over_devices(): pl.pallas_call(kern, name='sum_all', out_shape=jax.ShapeDtypeStruct(shape...  39.2 us
    all_to_all x5, waiting for transfers between devices, exchange(): return lax.all_to_all(x, GROUP_AXIS, 0, 0, tiled=True)  35.6 us
    dot_general x6, matrix products, contract(): return jnp.einsum('nd,ne->de', a, b, preferred_element_type=F32)  26.7 us
  transfers between devices with their start and end apart: 5, of which 4 were waited for; matrix products, arithmetic and copies ran while one was open for 13% of the time, Pallas kernels for 20%

profile of v2, /device:TPU:1, one launch (start us, length us, event | category | flops | bytes accessed | tf_op | source)
XLA Modules:
  0.0 489.0 jit_solution(3828309140561415705)
XLA Ops:
  0.7 9.7 %send_1.1 = bf16[128,72,128]{2,1,0:T(8,128)(2,1)} custom-call(s32[8192]{0:T(1024)} %bitcast.73, bf16[12288,128]{1,0:T(8,128)(2,1)} %refs_2_.1, f32[96,128]{1,0:T(8,128)} %bitcast.80), custom_call_target="tpu_custom_call" | custom-call | flops 40000000 | bytes 10000000 | tf_op jit(solution)/shard_map/send_1/pallas_call | solution.py:228
  10.4 11.5 %all-to-all-start = ((bf16[128,72,128]{2,1,0:T(8,128)(2,1)}), bf16[128,72,128]{2,1,0:T(8,128)(2,1)S(1)}, u32[]{:S(2)}, u32[]{:S(2)}) async-start(bf16[128,72,128]{2,1,0:T(8,128)(2,1)} %send_1.1), calls=%async_computation | async-start | bytes 4718592 | tf_op jit(solution)/shard_map/all_to_all | solution.py:572
  23.9 8.6 %sort.14 = s32[24576]{0:T(1024)S(1)} sort(s32[24576]{0:T(1024)S(1)} %get-tuple-element.97), dimensions={0}, to_apply=%region_0.0 | sort | flops 368640 | bytes 196608 | tf_op jit(solution)/shard_map/sort | solution.py:600
  32.4 0.8 broadcast_select_fusion
  33.5 0.7 broadcast_select_fusion.1
  37.8 2.0 concatenate.25.meta_ref
  39.7 3.9 broadcast_in_dim.66.refs_1_.refs_3_.refs_4_
  43.6 17.4 %near_1.1.refs_1_ = f32[12288,128]{1,0:T(8,128)} custom-call(s32[774]{0:T(1024)} %concatenate.25.meta_ref, s32[24576]{0:T(1024)} %get-tuple-element.108.idx_ref, s32[192,1,128]{2,1,0:T(1,128)} %bitcast.63, bf16[12288,128]{1,0:T(8,128)(2,1)} %refs_2_.1, f32[12288,128]{1,0:T(8,128)} %broadcast_in_dim.66.refs_1_.refs_3_.refs_4_), custom_call_target="tpu_custom_call" | custom-call | flops 80000000 | bytes 20000000 | tf_op jit(solution)/shard_map/near_1/pallas_call | solution.py:356
  61.9 0.7 pad_maximum_fusion.refs_11_
  62.7 1.4 copy-done.2
  64.1 29.6 %layer_1.1 = (bf16[12288,128]{1,0:T(8,128)(2,1)}, bf16[12288,256]{1,0:T(8,128)(2,1)}, bf16[128,64,128]{2,1,0:T(8,128)(2,1)}) custom-call(s32[774]{0:T(1024)} %concatenate.25.meta_ref, s32[24576]{0:T(1024)} %get-tuple-element.110.idx_ref, s32[192,1,128]{2,1,0:T(1,128)} %bitcast.60, bf16[128,72,128]{2,1,0:T(8,128)(2,1)} %copy-done.2, ...), custom_call_target="tpu_custom_call" | custom-call | flops 100000000 | bytes 25000000 | tf_op jit(solution)/shard_map/layer_1/pallas_call | solution.py:356
  93.7 11.3 %all-to-all-start.1 = ((bf16[128,64,128]{2,1,0:T(8,128)(2,1)}), bf16[128,64,128]{2,1,0:T(8,128)(2,1)S(1)}, u32[]{:S(2)}, u32[]{:S(2)}) async-start(bf16[128,64,128]{2,1,0:T(8,128)(2,1)} %get-tuple-element.43), calls=%async_computation.1 | async-start | bytes 4194304 | tf_op jit(solution)/shard_map/all_to_all | solution.py:572
  105.0 6.6 %select_convert_fusion.refs_1_.refs_4_ = bf16[12288,128]{1,0:T(8,128)(2,1)} fusion(s32[128]{0:T(128)S(1)} %and_select_fusion, f32[12288]{0:T(1024)S(1)} %copy-done.14, s32[12288]{0:T(1024)S(1)} %copy-done.20, pred[128]{0:T(512)(128)(4,1)S(1)} %iota_compare_fusion.3), kind=kLoop, calls=%fused_computation | loop fusion | flops 9437184 | bytes 3244672 | tf_op jit(solution)/shard_map/convert_element_type | solution.py:624
  111.6 21.3 %near_2.1.refs_2_ = f32[12288,256]{1,0:T(8,128)} custom-call(s32[774]{0:T(1024)} %concatenate.25.meta_ref, s32[24576]{0:T(1024)} %get-tuple-element.106.idx_ref, s32[192,1,128]{2,1,0:T(1,128)} %bitcast.64, bf16[12288,256]{1,0:T(8,128)(2,1)} %get-tuple-element.44.refs_0_.refs_3_.refs_2_), custom_call_target="tpu_custom_call" | custom-call | flops 80000000 | bytes 20000000 | tf_op jit(solution)/shard_map/near_2/pallas_call | solution.py:356
  132.9 6.3 %all-to-all-done.1.refs_1_ = bf16[128,64,128]{2,1,0:T(8,128)(2,1)S(1)} async-done(((bf16[128,64,128]{2,1,0:T(8,128)(2,1)}), bf16[128,64,128]{2,1,0:T(8,128)(2,1)S(1)}, u32[]{:S(2)}, u32[]{:S(2)}) %all-to-all-start.1) | async-done | bytes 2097184 | tf_op jit(solution)/shard_map/all_to_all | solution.py:572
  139.2 1.3 copy-done.7
  140.5 39.9 %layer_2.1 = (bf16[12288,256]{1,0:T(8,128)(2,1)}, bf16[12288,256]{1,0:T(8,128)(2,1)}, bf16[12288,128]{1,0:T(8,128)(2,1)}, f32[12288,128]{1,0:T(8,128)}, bf16[128,64,128]{2,1,0:T(8,128)(2,1)}) custom-call(s32[774]{0:T(1024)} %concatenate.25.meta_ref, s32[24576]{0:T(1024)} %get-tuple-element.107.idx_ref, s32[192,1,128]{2,1,0:T(1,128)} %bitcast.61, ...), custom_call_target="tpu_custom_call" | custom-call | flops 160000000 | bytes 40000000 | tf_op jit(solution)/shard_map/layer_2/pallas_call | solution.py:356
  180.4 5.5 %all-to-all-start.2 = ((bf16[128,64,128]{2,1,0:T(8,128)(2,1)}), bf16[128,64,128]{2,1,0:T(8,128)(2,1)S(1)}, u32[]{:S(2)}, u32[]{:S(2)}) async-start(bf16[128,64,128]{2,1,0:T(8,128)(2,1)} %get-tuple-element.45), calls=%async_computation.2 | async-start | bytes 4194304 | tf_op jit(solution)/shard_map/all_to_all | solution.py:572
  185.9 7.3 %sort.15 = s32[32768]{0:T(1024)S(1)} sort(s32[32768]{0:T(1024)S(1)} %pad_add_fusion), dimensions={0}, to_apply=%region_4.5 | sort | flops 491520 | bytes 262144 | tf_op jit(solution)/shard_map/sort | solution.py:673
  193.3 0.7 and_or_fusion
  195.4 1.0 slice_convert_fusion
  196.4 0.7 slice_reduce_fusion
  199.7 2.6 concatenate.26.refs_8_.meta_ref
  202.3 17.7 %near_3.1.refs_1_ = f32[12288,128]{1,0:T(8,128)} custom-call(s32[774]{0:T(1024)} %concatenate.25.meta_ref, s32[24576]{0:T(1024)} %get-tuple-element.108.idx_ref, s32[192,1,128]{2,1,0:T(1,128)} %bitcast.65, bf16[12288,128]{1,0:T(8,128)(2,1)} %get-tuple-element.46.refs_0_, bf16[12288,128]{1,0:T(8,128)(2,1)} %select_convert_fusion.refs_1_.refs_4_), custom_call_target="tpu_custom_call" | custom-call | flops 80000000 | bytes 20000000 | tf_op jit(solution)/shard_map/near_3/pallas_call | solution.py:356
  220.7 0.8 tile.13
  221.6 42.8 %layer_3.1 = (bf16[12288,128]{1,0:T(8,128)(2,1)}, bf16[12288,128]{1,0:T(8,128)(2,1)}, f32[8,128]{1,0:T(8,128)}, f32[8,128]{1,0:T(8,128)}, bf16[8192,128]{1,0:T(8,128)(2,1)}) custom-call(s32[774]{0:T(1024)} %concatenate.25.meta_ref, s32[24576]{0:T(1024)} %get-tuple-element.110.idx_ref, s32[192,1,128]{2,1,0:T(1,128)} %bitcast.62, bf16[8192,128]{1,0:T(8,128)(2,1)} %bitcast.56, ...), custom_call_target="tpu_custom_call" | custom-call | flops 120000000 | bytes 30000000 | tf_op jit(solution)/shard_map/layer_3/pallas_call | solution.py:356
  264.3 11.9 %all-to-all-start.3 = ((bf16[128,64,128]{2,1,0:T(8,128)(2,1)}), bf16[128,64,128]{2,1,0:T(8,128)(2,1)S(1)}, u32[]{:S(2)}, u32[]{:S(2)}) async-start(bf16[128,64,128]{2,1,0:T(8,128)(2,1)} %bitcast.59), calls=%async_computation.3 | async-start | bytes 4194304 | tf_op jit(solution)/shard_map/all_to_all | solution.py:572
  276.3 0.8 copy.32
  277.0 0.7 pad_maximum_fusion.1.refs_5_
  277.7 17.3 %back_3_own.1.refs_1_ = f32[12288,128]{1,0:T(8,128)} custom-call(s32[905]{0:T(1024)} %concatenate.26.refs_8_.meta_ref, s32[24576]{0:T(1024)} %get-tuple-element.101.refs_9_.idx_ref, s32[192,1,128]{2,1,0:T(1,128)} %bitcast.66, bf16[12288,128]{1,0:T(8,128)(2,1)} %get-tuple-element.49.refs_0_), custom_call_target="tpu_custom_call" | custom-call | flops 80000000 | bytes 20000000 | tf_op jit(solution)/shard_map/back_3_own/pallas_call | solution.py:356
  295.0 15.4 %all-to-all-done.3 = bf16[128,64,128]{2,1,0:T(8,128)(2,1)S(1)} async-done(((bf16[128,64,128]{2,1,0:T(8,128)(2,1)}), bf16[128,64,128]{2,1,0:T(8,128)(2,1)S(1)}, u32[]{:S(2)}, u32[]{:S(2)}) %all-to-all-start.3) | async-done | bytes 2097184 | tf_op jit(solution)/shard_map/all_to_all | solution.py:572
  310.5 1.3 copy-done.8
  311.8 40.1 %owner_3.1 = (bf16[12288,128]{1,0:T(8,128)(2,1)}, bf16[12288,256]{1,0:T(8,128)(2,1)}, bf16[12288,256]{1,0:T(8,128)(2,1)}, f32[8,256]{1,0:T(8,128)}, bf16[8192,256]{1,0:T(8,128)(2,1)}) custom-call(s32[905]{0:T(1024)} %concatenate.26.refs_8_.meta_ref, s32[8192]{0:T(1024)} %get-tuple-element.103.idx_ref, s32[64,1,128]{2,1,0:T(1,128)} %bitcast.78, ...), custom_call_target="tpu_custom_call" | custom-call | flops 120000000 | bytes 30000000 | tf_op jit(solution)/shard_map/owner_3/pallas_call | solution.py:356
  351.9 7.9 %all-to-all-start.4 = ((bf16[128,64,256]{2,1,0:T(8,128)(2,1)}), bf16[128,64,256]{2,1,0:T(8,128)(2,1)}, u32[]{:S(2)}, u32[]{:S(2)}) async-start(bf16[128,64,256]{2,1,0:T(8,128)(2,1)} %bitcast.58), calls=%async_computation.4 | async-start | bytes 8388608 | tf_op jit(solution)/shard_map/all_to_all | solution.py:572
  359.8 0.8 copy.33
  360.6 4.6 fusion.30
  365.2 24.3 %back_2_own.1.refs_1_ = f32[12288,256]{1,0:T(8,128)} custom-call(s32[905]{0:T(1024)} %concatenate.26.refs_8_.meta_ref, s32[24576]{0:T(1024)} %get-tuple-element.99.refs_9_.idx_ref, s32[192,1,128]{2,1,0:T(1,128)} %bitcast.67, bf16[12288,256]{1,0:T(8,128)(2,1)} %get-tuple-element.53.refs_0_, bf16[12288,256]{1,0:T(8,128)(2,1)} %get-tuple-element.54.refs_1_, ...), custom_call_target="tpu_custom_call" | custom-call | flops 120000000 | bytes 30000000 | tf_op jit(solution)/shard_map/back_2_own/pallas_call | solution.py:356
  389.6 5.4 %convolution_select_fusion.refs_4_ = f32[256,128]{1,0:T(8,128)} fusion(f32[256,128]{1,0:T(8,128)S(1)} %fusion.30, bf16[12288,256]{1,0:T(8,128)(2,1)} %get-tuple-element.51.refs_3_, bf16[12288,128]{1,0:T(8,128)(2,1)S(1)} %copy-done.4, pred[128]{0:T(512)(128)(4,1)S(1)} %iota_compare_fusion.2), kind=kOutput, calls=%fused_computation.2 | convolution fusion | flops 805339136 | bytes 9699456 | tf_op jit(solution)/shard_map/nd,ne->de/dot_general | solution.py:806
  395.0 7.3 %fusion.28.refs_2_ = f32[256,256]{1,0:T(8,128)} fusion(bf16[12288,256]{1,0:T(8,128)(2,1)} %get-tuple-element.44.refs_0_.refs_3_.refs_2_, bf16[12288,256]{1,0:T(8,128)(2,1)} %get-tuple-element.54.refs_1_), kind=kOutput, calls=%fused_computation.86 | convolution fusion | flops 1610612736 | bytes 12845056 | tf_op jit(solution)/shard_map/nd,ne->de/dot_general | solution.py:806
  402.3 2.5 fusion.29.refs_3_
  404.8 13.7 %all-to-all-done.4 = bf16[128,64,256]{2,1,0:T(8,128)(2,1)} async-done(((bf16[128,64,256]{2,1,0:T(8,128)(2,1)}), bf16[128,64,256]{2,1,0:T(8,128)(2,1)}, u32[]{:S(2)}, u32[]{:S(2)}) %all-to-all-start.4) | async-done | bytes 4194336 | tf_op jit(solution)/shard_map/all_to_all | solution.py:572
  418.5 18.2 %owner_2.1 = (bf16[12288,256]{1,0:T(8,128)(2,1)}, f32[8,256]{1,0:T(8,128)}) custom-call(s32[905]{0:T(1024)} %concatenate.26.refs_8_.meta_ref, s32[8192]{0:T(1024)} %get-tuple-element.104.idx_ref, s32[64,1,128]{2,1,0:T(1,128)} %bitcast.79, bf16[8192,256]{1,0:T(8,128)(2,1)} %bitcast.28.refs_0_, f32[12288,256]{1,0:T(8,128)} %back_2_own.1.refs_1_, ...), custom_call_target="tpu_custom_call" | custom-call | flops 100000000 | bytes 25000000 | tf_op jit(solution)/shard_map/owner_2/pallas_call | solution.py:356
  436.7 5.0 %convolution_bitcast_fusion.refs_0_ = f32[128,256]{1,0:T(8,128)} fusion(bf16[12288,256]{1,0:T(8,128)(2,1)} %get-tuple-element.55, bf16[12288,128]{1,0:T(8,128)(2,1)S(1)} %copy-done), kind=kOutput, calls=%fused_computation.1 | convolution fusion | flops 805306368 | bytes 9568256 | tf_op jit(solution)/shard_map/nd,ne->de/dot_general | solution.py:806
  442.3 1.9 fusion.27.refs_1_
  444.1 39.2 %sum_all.1.full_ref = f32[2,64,16,128]{3,2,1,0:T(8,128)} custom-call(f32[128,256]{1,0:T(8,128)} %convolution_bitcast_fusion.refs_0_, f32[128,256]{1,0:T(8,128)} %fusion.27.refs_1_, f32[256,256]{1,0:T(8,128)} %fusion.28.refs_2_, f32[256,256]{1,0:T(8,128)} %fusion.29.refs_3_, f32[256,128]{1,0:T(8,128)} %convolution_select_fusion.refs_4_, ...), custom_call_target="tpu_custom_call" | custom-call | flops 100000000 | bytes 25000000 | tf_op jit(solution)/shard_map/sum_all/pallas_call | solution.py:500
  483.3 2.2 unpack_sums.1
  485.5 1.6 copy.35
  487.1 1.6 copy.36
  (78 shorter events, 7.3 us)
Async XLA Ops:
  0.6 21.2 %copy-start.15 = (s32[24576]{0:T(1024)S(1)}, s32[24576]{0:T(1024)}, u32[]{:S(2)}) copy-start(s32[24576]{0:T(1024)} %param.20) | copy-start | bytes 294916
  0.7 21.2 %copy-start.16 = (s32[24576]{0:T(1024)S(1)}, s32[24576]{0:T(1024)}, u32[]{:S(2)}) copy-start(s32[24576]{0:T(1024)} %param.21) | copy-start | bytes 294916
  0.7 36.2 %copy-start.17 = (bf16[256,40]{0,1:T(8,128)(2,1)S(1)}, bf16[256,40]{0,1:T(8,128)(2,1)}, u32[]{:S(2)}) copy-start(bf16[256,40]{0,1:T(8,128)(2,1)} %param.30) | copy-start | bytes 61444
  0.7 36.3 %copy-start.18 = (bf16[256,40]{0,1:T(8,128)(2,1)S(1)}, bf16[256,40]{0,1:T(8,128)(2,1)}, u32[]{:S(2)}) copy-start(bf16[256,40]{0,1:T(8,128)(2,1)} %param.29) | copy-start | bytes 61444
  0.7 39.1 %copy-start.19 = (f32[12288]{0:T(1024)S(1)}, f32[12288]{0:T(1024)}, u32[]{:S(2)}) copy-start(f32[12288]{0:T(1024)} %param.22) | copy-start | bytes 147460
  10.4 52.3 %all-to-all-start = ((bf16[128,72,128]{2,1,0:T(8,128)(2,1)}), bf16[128,72,128]{2,1,0:T(8,128)(2,1)S(1)}, u32[]{:S(2)}, u32[]{:S(2)}) async-start(bf16[128,72,128]{2,1,0:T(8,128)(2,1)} %send_1.1), calls=%async_computation | async-start | bytes 4718592 | tf_op jit(solution)/shard_map/all_to_all | solution.py:572
  43.6 17.5 %copy-start.21 = (f32[40]{0:T(128)S(1)}, f32[40]{0:T(128)}, u32[]{:S(2)}) copy-start(f32[40]{0:T(128)} %param.31) | copy-start | bytes 484
  43.6 19.0 %copy-start.10 = (s32[128,64]{0,1:T(8,128)S(1)}, s32[128,64]{0,1:T(8,128)}, u32[]{:S(2)}) copy-start(s32[128,64]{0,1:T(8,128)} %param.19) | copy-start | bytes 98308
  62.7 1.4 copy-start.2
  64.1 40.9 %copy-start.14 = (f32[12288]{0:T(1024)S(1)}, f32[12288]{0:T(1024)}, u32[]{:S(2)}) copy-start(f32[12288]{0:T(1024)} %param.18) | copy-start | bytes 147460
  64.1 40.9 %copy-start.20 = (s32[12288]{0:T(1024)S(1)}, s32[12288]{0:T(1024)}, u32[]{:S(2)}) copy-start(s32[12288]{0:T(1024)} %param.17) | copy-start | bytes 147460
  93.7 45.5 %all-to-all-start.1 = ((bf16[128,64,128]{2,1,0:T(8,128)(2,1)}), bf16[128,64,128]{2,1,0:T(8,128)(2,1)S(1)}, u32[]{:S(2)}, u32[]{:S(2)}) async-start(bf16[128,64,128]{2,1,0:T(8,128)(2,1)} %get-tuple-element.43), calls=%async_computation.1 | async-start | bytes 4194304 | tf_op jit(solution)/shard_map/all_to_all | solution.py:572
  139.2 1.3 copy-start.7
  180.4 39.7 %all-to-all-start.2 = ((bf16[128,64,128]{2,1,0:T(8,128)(2,1)}), bf16[128,64,128]{2,1,0:T(8,128)(2,1)S(1)}, u32[]{:S(2)}, u32[]{:S(2)}) async-start(bf16[128,64,128]{2,1,0:T(8,128)(2,1)} %get-tuple-element.45), calls=%async_computation.2 | async-start | bytes 4194304 | tf_op jit(solution)/shard_map/all_to_all | solution.py:572
  194.0 26.0 %copy-start.9 = (s32[24576]{0:T(1024)}, s32[24576]{0:T(1024)S(1)}, u32[]{:S(2)}) copy-start(s32[24576]{0:T(1024)S(1)} %get-tuple-element.102) | copy-start | bytes 294916
  195.1 25.0 %copy-start.13 = (s32[8192]{0:T(1024)}, s32[8192]{0:T(1024)S(1)}, u32[]{:S(2)}) copy-start(s32[8192]{0:T(1024)S(1)} %get-tuple-element.105) | copy-start | bytes 98308
  220.2 1.4 copy-start.6
  221.6 54.7 %copy-start.11 = (bf16[256,256]{1,0:T(8,128)(2,1)S(1)}, bf16[256,256]{1,0:T(8,128)(2,1)}, u32[]{:S(2)}) copy-start(bf16[256,256]{1,0:T(8,128)(2,1)} %refs_6_.1) | copy-start | bytes 393220
  264.3 46.2 %all-to-all-start.3 = ((bf16[128,64,128]{2,1,0:T(8,128)(2,1)}), bf16[128,64,128]{2,1,0:T(8,128)(2,1)S(1)}, u32[]{:S(2)}, u32[]{:S(2)}) async-start(bf16[128,64,128]{2,1,0:T(8,128)(2,1)} %bitcast.59), calls=%async_computation.3 | async-start | bytes 4194304 | tf_op jit(solution)/shard_map/all_to_all | solution.py:572
  310.5 1.3 copy-start.8
  351.9 7.9 %copy-start.12 = (bf16[256,256]{1,0:T(8,128)(2,1)S(1)}, bf16[256,256]{1,0:T(8,128)(2,1)}, u32[]{:S(2)}) copy-start(bf16[256,256]{1,0:T(8,128)(2,1)} %refs_5_.3) | copy-start | bytes 393220
  351.9 8.7 %copy-start.1 = (bf16[12288,128]{1,0:T(8,128)(2,1)S(1)}, bf16[12288,128]{1,0:T(8,128)(2,1)}, u32[]{:S(2)}) copy-start(bf16[12288,128]{1,0:T(8,128)(2,1)} %get-tuple-element.50.refs_2_) | copy-start | bytes 9437188
  351.9 66.6 %all-to-all-start.4 = ((bf16[128,64,256]{2,1,0:T(8,128)(2,1)}), bf16[128,64,256]{2,1,0:T(8,128)(2,1)}, u32[]{:S(2)}, u32[]{:S(2)}) async-start(bf16[128,64,256]{2,1,0:T(8,128)(2,1)} %bitcast.58), calls=%async_computation.4 | async-start | bytes 8388608 | tf_op jit(solution)/shard_map/all_to_all | solution.py:572
  365.2 24.3 %copy-start.4 = (bf16[12288,128]{1,0:T(8,128)(2,1)S(1)}, bf16[12288,128]{1,0:T(8,128)(2,1)}, u32[]{:S(2)}) copy-start(bf16[12288,128]{1,0:T(8,128)(2,1)} %get-tuple-element.57) | copy-start | bytes 9437188
  389.5 12.7 %slice-start = ((s8[6291456]{0:T(1024)(128)(4,1)}), s8[4194304]{0:T(1024)(128)(4,1)S(1)}, s32[]{:S(2)}) async-start(s8[6291456]{0:T(1024)(128)(4,1)} %bitcast.52), calls=%async_computation.5 | async-start | bytes 8388608
  389.5 12.7 %slice-start.2 = ((s8[6291456]{0:T(1024)(128)(4,1)}), s8[4194304]{0:T(1024)(128)(4,1)S(1)}, s32[]{:S(2)}) async-start(s8[6291456]{0:T(1024)(128)(4,1)} %bitcast.54), calls=%async_computation.7 | async-start | bytes 8388608
  395.0 7.3 %slice-start.1 = ((s8[6291456]{0:T(1024)(128)(4,1)}), s8[2097152]{0:T(1024)(128)(4,1)S(1)}, s32[]{:S(2)}) async-start(s8[6291456]{0:T(1024)(128)(4,1)} %bitcast.52), calls=%async_computation.6 | async-start | bytes 4194304
  395.0 7.3 %slice-start.3 = ((s8[6291456]{0:T(1024)(128)(4,1)}), s8[2097152]{0:T(1024)(128)(4,1)S(1)}, s32[]{:S(2)}) async-start(s8[6291456]{0:T(1024)(128)(4,1)} %bitcast.54), calls=%async_computation.8 | async-start | bytes 4194304
  418.5 18.2 %copy-start = (bf16[12288,128]{1,0:T(8,128)(2,1)S(1)}, bf16[12288,128]{1,0:T(8,128)(2,1)}, u32[]{:S(2)}) copy-start(bf16[12288,128]{1,0:T(8,128)(2,1)} %refs_2_.1) | copy-start | bytes 9437188
  436.7 5.0 %copy-start.3 = (bf16[12288,256]{1,0:T(8,128)(2,1)S(1)}, bf16[12288,256]{1,0:T(8,128)(2,1)}, u32[]{:S(2)}) copy-start(bf16[12288,256]{1,0:T(8,128)(2,1)} %get-tuple-element.55) | copy-start | bytes 18874372
  436.7 5.6 %copy-start.5 = (bf16[12288,128]{1,0:T(8,128)(2,1)S(1)}, bf16[12288,128]{1,0:T(8,128)(2,1)}, u32[]{:S(2)}) copy-start(bf16[12288,128]{1,0:T(8,128)(2,1)} %get-tuple-element.41) | copy-start | bytes 9437188

commit v3 on v2

--- a/solution.py
+++ b/solution.py
@@ -397,6 +397,16 @@
         me = lax.axis_index(GROUP_AXIS)
         chip, core = me // 2, me % 2
         mate = device(chip, 1 - core)
+        barrier = pltpu.get_barrier_semaphore()
+
+        def hello(to):
+            pl.semaphore_signal(barrier, inc=1, device_id=(to,), device_id_type=pl.DeviceIdType.MESH)
+
+        def greet(k, carry):
+            hello(device((chip + k) % chips, core))
+            return carry
+        lax.fori_loop(1, chips, greet, 0)
+        hello(mate)
 
         def at(q):
             unit = q // rounds
@@ -424,6 +434,7 @@
             return pltpu.make_async_remote_copy(src_ref=src, dst_ref=dst, send_sem=pair_sem.at[2 * k],
                                                 recv_sem=pair_sem.at[2 * k + 1], device_id=(mate,),
                                                 device_id_type=pl.DeviceIdType.MESH)
+        pl.semaphore_wait(barrier, chips)
         first = pair(x_ref.at[1 - core], half, 0)
         first.start()
         first.wait()
@@ -504,31 +515,36 @@
                         pltpu.VMEM(shape[1:], F32), pltpu.SemaphoreType.DMA((4,)),
                         pltpu.SemaphoreType.DMA((chips,)), pltpu.SemaphoreType.DMA((chips,)),
                         pltpu.SemaphoreType.DMA((chips,)), pltpu.SemaphoreType.DMA((chips,))],
-        compiler_params=pltpu.CompilerParams(has_side_effects=True), cost_estimate=cost(25))(*grads, *sums)
+        compiler_params=pltpu.CompilerParams(collective_id=0, has_side_effects=True), cost_estimate=cost(25))(*grads, *sums)
 
     def unpack_kern(full_ref, total_ref, *outs):
         def part(q):
             unit = q // rounds
             r = (q % rounds) * SHARE
             return full_ref[unit // chips, unit % chips, r:r + SHARE, :]
-        for o, columns in zip(outs, places[:-2]):
+
+        def move(o, columns, skip):
             for w, first in enumerate(columns):
                 for k in range(o.shape[0] // SHARE):
-                    o[k * SHARE:(k + 1) * SHARE, w * LANES:(w + 1) * LANES] = part(first + k)
-        o_self, o_neigh = outs[len(grads) - 1], outs[len(grads)]
-        for k in range(o_self.shape[0] // SHARE):
-            both = part(places[-2][0] + k)
-            o_self[k * SHARE:(k + 1) * SHARE, :] = both[:, :classes]
-            o_neigh[k * SHARE:(k + 1) * SHARE, :] = pltpu.roll(both, LANES - SPREAD, 1)[:, :classes]
+                    o[k * SHARE:(k + 1) * SHARE, w * LANES:(w + 1) * LANES] = part(first + skip + k)
+        move(outs[0], places[0], 0)
+        move(outs[1], places[0], outs[0].shape[0] // SHARE)
+        for o, columns in zip(outs[2:], places[1:-2]):
+            move(o, columns, 0)
+        both = jnp.concatenate([part(places[-2][0] + k) for k in range(rows_3 // SHARE)], axis=0).T
+        outs[ng][...] = both[:classes, :]
+        outs[ng + 1][...] = both[SPREAD:SPREAD + classes, :]
         small, line = part(places[-1][0]), 0
-        for o, width in zip(outs[len(grads) + 1:-1], widths):
+        for o, width in zip(outs[ng + 2:-1], widths):
             for w in range(width // LANES):
                 wide = min(LANES, o.shape[1] - w * LANES)
                 o[:, w * LANES:w * LANES + wide] = small[line:line + 1, :wide]
                 line += 1
         outs[-1][...] = jnp.sum(small[line:line + 1, :], axis=1, keepdims=True) / total_ref[...]
+    ng = len(grads)
     rows_3 = grads[-1].shape[0]
-    outs = ([g.shape for g in grads[:-1]] + [(rows_3, classes)] * 2
+    rows_1, width_1 = grads[0].shape
+    outs = ([(rows_1 // 2, width_1)] * 2 + [g.shape for g in grads[1:-1]] + [(classes, rows_3)] * 2
             + [(1, w) for w in widths[:-2]] + [(1, classes), (1, 1)])
     return pl.pallas_call(unpack_kern, name='unpack_sums', out_shape=[jax.ShapeDtypeStruct(o, F32) for o in outs],
                           in_specs=[vmem, vmem], out_specs=[vmem] * len(outs), cost_estimate=cost(3))(full, total)
@@ -794,13 +810,15 @@
 
         def epi_o2(a, bl, fx, out, put):
             d_pre = jnp.where(bl[0][...].astype(F32) > 0, a, 0.0)
-            out[0][...] = d_pre.astype(BF16)
+            inputs = jnp.concatenate([bl[1][...], bl[2][...]], axis=1)
+            out[0][...] += lax.dot_general(inputs, d_pre.astype(BF16), (((0,), (0,)), ((), ())),
+                                           preferred_element_type=F32)
             add_rows(out[1], d_pre)
 
-        d_bf_1, g_b1 = edge_call(
+        g_1, g_b1 = edge_call(
             'owner_2', (meta_b, owner_at, tile_linear(slot_s), seg_r), 2, halo, n, win_r, [(halo, hidden)], rows_of(2),
-            [ret_2, own_2], [hidden_1], [], [((n, hidden), BF16, False), ((8, hidden), F32, True)], n, tile, epi_o2, 25,
-            init=1, late=True)
+            [ret_2, own_2], [hidden_1, features, mean_1], [],
+            [((2 * LANES, hidden), F32, True), ((8, hidden), F32, True)], n, half_tile, epi_o2, 25, init=1, late=True)
 
         def contract(a, b):
             return jnp.einsum('nd,ne->de', a, b, preferred_element_type=F32)
@@ -808,9 +826,9 @@
         at = jnp.arange(LANES, dtype=jnp.int32)[None, :]
         g_3 = jnp.where(at < SPREAD, contract(hidden_2, d_bf_3), contract(hidden_2, tb_3))
         g1s, g1n, g2s, g2n, g3s, g3n, s1, s2, s3, loss = sum_over_devices(
-            [contract(features, d_bf_1), contract(mean_1, d_bf_1), contract(hidden_1, d_bf_2), contract(mean_2, d_bf_2), g_3],
+            [g_1, contract(hidden_1, d_bf_2), contract(mean_2, d_bf_2), g_3],
             [g_b1, g_b2, g_b3, loss_parts], total.reshape(1, 1), classes, peers)
-        return (loss.reshape(()), g1s, g1n, s1.reshape(-1), g2s, g2n, s2.reshape(-1), g3s, g3n, s3.reshape(-1))
+        return (loss.reshape(()), g1s, g1n, s1.reshape(-1), g2s, g2n, s2.reshape(-1), g3s.T, g3n.T, s3.reshape(-1))
 
     sharded = P(GROUP_AXIS)
     whole = P()

time: 497 us -> 486 us (0.978)
  matrix products: 26.7 us -> 19.9 us
    dot_general x6 -> x4, matrix products: 26.7 us -> 19.9 us  [contract(): return jnp.einsum('nd,ne->de', a, b, preferred_element_type=F32)]
where the time goes in v3:
time: 486 us; the launch traced here: 480 us
  Pallas kernels  320 us (66%)
  starting transfers between devices  49.3 us (10%)
  waiting for transfers between devices  35.6 us (7%)
  other arithmetic  32 us (7%)
  matrix products  19.9 us (4%)
  local copies, waits for them, and re-layouts  17.3 us (4%)
  between operations  6.21 us (1%)
    pallas_call x10, Pallas kernels, edge_call(): pl.pallas_call(kern, name=name, grid=(steps,), out_shape=out_shape + more...  270 us
    all_to_all x5, starting transfers between devices, exchange(): return lax.all_to_all(x, GROUP_AXIS, 0, 0, tiled=True)  49.3 us
    pallas_call x1, Pallas kernels, sum_over_devices(): pl.pallas_call(kern, name='sum_all', out_shape=jax.ShapeDtypeStruct(shape...  37.8 us
    all_to_all x5, waiting for transfers between devices, exchange(): return lax.all_to_all(x, GROUP_AXIS, 0, 0, tiled=True)  35.6 us
    dot_general x4, matrix products, contract(): return jnp.einsum('nd,ne->de', a, b, preferred_element_type=F32)  19.9 us
  transfers between devices with their start and end apart: 5, of which 4 were waited for; matrix products, arithmetic and copies ran while one was open for 13% of the time, Pallas kernels for 20%

profile of v3, /device:TPU:1, one launch (start us, length us, event | category | flops | bytes accessed | tf_op | source)
XLA Modules:
  0.0 480.2 jit_solution(15033505764743184880)
XLA Ops:
  0.7 9.7 %send_1.1 = bf16[128,72,128]{2,1,0:T(8,128)(2,1)} custom-call(s32[8192]{0:T(1024)} %bitcast.69, bf16[12288,128]{1,0:T(8,128)(2,1)} %refs_3_.1, f32[96,128]{1,0:T(8,128)} %bitcast.76), custom_call_target="tpu_custom_call" | custom-call | flops 40000000 | bytes 10000000 | tf_op jit(solution)/shard_map/send_1/pallas_call | solution.py:228
  10.4 11.5 %all-to-all-start = ((bf16[128,72,128]{2,1,0:T(8,128)(2,1)}), bf16[128,72,128]{2,1,0:T(8,128)(2,1)S(1)}, u32[]{:S(2)}, u32[]{:S(2)}) async-start(bf16[128,72,128]{2,1,0:T(8,128)(2,1)} %send_1.1), calls=%async_computation | async-start | bytes 4718592 | tf_op jit(solution)/shard_map/all_to_all | solution.py:588
  21.9 0.7 or_or_fusion
  23.8 8.6 %sort.14 = s32[24576]{0:T(1024)S(1)} sort(s32[24576]{0:T(1024)S(1)} %get-tuple-element.87), dimensions={0}, to_apply=%region_0.0 | sort | flops 368640 | bytes 196608 | tf_op jit(solution)/shard_map/sort | solution.py:616
  32.4 0.8 broadcast_select_fusion
  33.4 0.7 broadcast_select_fusion.1
  37.1 0.7 fusion.25
  37.8 2.0 concatenate.25.meta_ref
  39.7 3.9 broadcast_in_dim.66.refs_1_.refs_3_.refs_4_
  43.6 17.5 %near_1.1.refs_1_ = f32[12288,128]{1,0:T(8,128)} custom-call(s32[774]{0:T(1024)} %concatenate.25.meta_ref, s32[24576]{0:T(1024)} %get-tuple-element.98.idx_ref, s32[192,1,128]{2,1,0:T(1,128)} %bitcast.59, bf16[12288,128]{1,0:T(8,128)(2,1)} %refs_3_.1, f32[12288,128]{1,0:T(8,128)} %broadcast_in_dim.66.refs_1_.refs_3_.refs_4_), custom_call_target="tpu_custom_call" | custom-call | flops 80000000 | bytes 20000000 | tf_op jit(solution)/shard_map/near_1/pallas_call | solution.py:356
  61.1 0.7 compare_select_fusion.refs_5_
  62.0 0.7 pad_maximum_fusion.refs_11_
  62.8 1.4 copy-done.1
  64.2 29.6 %layer_1.1 = (bf16[12288,128]{1,0:T(8,128)(2,1)}, bf16[12288,256]{1,0:T(8,128)(2,1)}, bf16[128,64,128]{2,1,0:T(8,128)(2,1)}) custom-call(s32[774]{0:T(1024)} %concatenate.25.meta_ref, s32[24576]{0:T(1024)} %get-tuple-element.100.idx_ref, s32[192,1,128]{2,1,0:T(1,128)} %bitcast.56, bf16[128,72,128]{2,1,0:T(8,128)(2,1)} %copy-done.1, ...), custom_call_target="tpu_custom_call" | custom-call | flops 100000000 | bytes 25000000 | tf_op jit(solution)/shard_map/layer_1/pallas_call | solution.py:356
  93.8 11.4 %all-to-all-start.1 = ((bf16[128,64,128]{2,1,0:T(8,128)(2,1)}), bf16[128,64,128]{2,1,0:T(8,128)(2,1)S(1)}, u32[]{:S(2)}, u32[]{:S(2)}) async-start(bf16[128,64,128]{2,1,0:T(8,128)(2,1)} %get-tuple-element.43), calls=%async_computation.1 | async-start | bytes 4194304 | tf_op jit(solution)/shard_map/all_to_all | solution.py:588
  105.2 6.7 %select_convert_fusion.refs_1_.refs_4_ = bf16[12288,128]{1,0:T(8,128)(2,1)} fusion(s32[128]{0:T(128)S(1)} %and_select_fusion, f32[12288]{0:T(1024)S(1)} %copy-done.11, s32[12288]{0:T(1024)S(1)} %copy-done.17, pred[128]{0:T(512)(128)(4,1)S(1)} %iota_compare_fusion.3), kind=kLoop, calls=%fused_computation | loop fusion | flops 9437184 | bytes 3244672 | tf_op jit(solution)/shard_map/convert_element_type | solution.py:640
  111.9 21.2 %near_2.1.refs_2_ = f32[12288,256]{1,0:T(8,128)} custom-call(s32[774]{0:T(1024)} %concatenate.25.meta_ref, s32[24576]{0:T(1024)} %get-tuple-element.96.idx_ref, s32[192,1,128]{2,1,0:T(1,128)} %bitcast.60, bf16[12288,256]{1,0:T(8,128)(2,1)} %get-tuple-element.44.refs_0_.refs_3_.refs_2_), custom_call_target="tpu_custom_call" | custom-call | flops 80000000 | bytes 20000000 | tf_op jit(solution)/shard_map/near_2/pallas_call | solution.py:356
  133.1 6.4 %all-to-all-done.1.refs_1_ = bf16[128,64,128]{2,1,0:T(8,128)(2,1)S(1)} async-done(((bf16[128,64,128]{2,1,0:T(8,128)(2,1)}), bf16[128,64,128]{2,1,0:T(8,128)(2,1)S(1)}, u32[]{:S(2)}, u32[]{:S(2)}) %all-to-all-start.1) | async-done | bytes 2097184 | tf_op jit(solution)/shard_map/all_to_all | solution.py:588
  139.5 1.3 copy-done.4
  140.8 39.9 %layer_2.1 = (bf16[12288,256]{1,0:T(8,128)(2,1)}, bf16[12288,256]{1,0:T(8,128)(2,1)}, bf16[12288,128]{1,0:T(8,128)(2,1)}, f32[12288,128]{1,0:T(8,128)}, bf16[128,64,128]{2,1,0:T(8,128)(2,1)}) custom-call(s32[774]{0:T(1024)} %concatenate.25.meta_ref, s32[24576]{0:T(1024)} %get-tuple-element.97.idx_ref, s32[192,1,128]{2,1,0:T(1,128)} %bitcast.57, ...), custom_call_target="tpu_custom_call" | custom-call | flops 160000000 | bytes 40000000 | tf_op jit(solution)/shard_map/layer_2/pallas_call | solution.py:356
  180.6 6.4 %all-to-all-start.2 = ((bf16[128,64,128]{2,1,0:T(8,128)(2,1)}), bf16[128,64,128]{2,1,0:T(8,128)(2,1)S(1)}, u32[]{:S(2)}, u32[]{:S(2)}) async-start(bf16[128,64,128]{2,1,0:T(8,128)(2,1)} %get-tuple-element.45), calls=%async_computation.2 | async-start | bytes 4194304 | tf_op jit(solution)/shard_map/all_to_all | solution.py:588
  187.1 7.3 %sort.15 = s32[32768]{0:T(1024)S(1)} sort(s32[32768]{0:T(1024)S(1)} %pad_add_fusion), dimensions={0}, to_apply=%region_4.5 | sort | flops 491520 | bytes 262144 | tf_op jit(solution)/shard_map/sort | solution.py:689
  194.4 0.7 and_or_fusion
  196.5 1.0 slice_convert_fusion
  197.5 0.7 slice_reduce_fusion
  200.2 0.7 fusion.23
  200.8 2.6 concatenate.26.refs_8_.meta_ref
  203.5 17.6 %near_3.1.refs_1_ = f32[12288,128]{1,0:T(8,128)} custom-call(s32[774]{0:T(1024)} %concatenate.25.meta_ref, s32[24576]{0:T(1024)} %get-tuple-element.98.idx_ref, s32[192,1,128]{2,1,0:T(1,128)} %bitcast.61, bf16[12288,128]{1,0:T(8,128)(2,1)} %get-tuple-element.46.refs_0_, bf16[12288,128]{1,0:T(8,128)(2,1)} %select_convert_fusion.refs_1_.refs_4_), custom_call_target="tpu_custom_call" | custom-call | flops 80000000 | bytes 20000000 | tf_op jit(solution)/shard_map/near_3/pallas_call | solution.py:356
  221.9 0.8 tile.13
  222.7 42.8 %layer_3.1 = (bf16[12288,128]{1,0:T(8,128)(2,1)}, bf16[12288,128]{1,0:T(8,128)(2,1)}, f32[8,128]{1,0:T(8,128)}, f32[8,128]{1,0:T(8,128)}, bf16[8192,128]{1,0:T(8,128)(2,1)}) custom-call(s32[774]{0:T(1024)} %concatenate.25.meta_ref, s32[24576]{0:T(1024)} %get-tuple-element.100.idx_ref, s32[192,1,128]{2,1,0:T(1,128)} %bitcast.58, bf16[8192,128]{1,0:T(8,128)(2,1)} %bitcast.52, ...), custom_call_target="tpu_custom_call" | custom-call | flops 120000000 | bytes 30000000 | tf_op jit(solution)/shard_map/layer_3/pallas_call | solution.py:356
  265.4 11.9 %all-to-all-start.3 = ((bf16[128,64,128]{2,1,0:T(8,128)(2,1)}), bf16[128,64,128]{2,1,0:T(8,128)(2,1)S(1)}, u32[]{:S(2)}, u32[]{:S(2)}) async-start(bf16[128,64,128]{2,1,0:T(8,128)(2,1)} %bitcast.55), calls=%async_computation.3 | async-start | bytes 4194304 | tf_op jit(solution)/shard_map/all_to_all | solution.py:588
  277.4 0.8 copy.32
  278.2 0.7 pad_maximum_fusion.1.refs_5_
  278.8 17.4 %back_3_own.1.refs_1_ = f32[12288,128]{1,0:T(8,128)} custom-call(s32[905]{0:T(1024)} %concatenate.26.refs_8_.meta_ref, s32[24576]{0:T(1024)} %get-tuple-element.91.refs_9_.idx_ref, s32[192,1,128]{2,1,0:T(1,128)} %bitcast.62, bf16[12288,128]{1,0:T(8,128)(2,1)} %get-tuple-element.49.refs_0_), custom_call_target="tpu_custom_call" | custom-call | flops 80000000 | bytes 20000000 | tf_op jit(solution)/shard_map/back_3_own/pallas_call | solution.py:356
  296.2 15.4 %all-to-all-done.3 = bf16[128,64,128]{2,1,0:T(8,128)(2,1)S(1)} async-done(((bf16[128,64,128]{2,1,0:T(8,128)(2,1)}), bf16[128,64,128]{2,1,0:T(8,128)(2,1)S(1)}, u32[]{:S(2)}, u32[]{:S(2)}) %all-to-all-start.3) | async-done | bytes 2097184 | tf_op jit(solution)/shard_map/all_to_all | solution.py:588
  311.6 1.3 copy-done.5
  312.9 40.2 %owner_3.1 = (bf16[12288,128]{1,0:T(8,128)(2,1)}, bf16[12288,256]{1,0:T(8,128)(2,1)}, bf16[12288,256]{1,0:T(8,128)(2,1)}, f32[8,256]{1,0:T(8,128)}, bf16[8192,256]{1,0:T(8,128)(2,1)}) custom-call(s32[905]{0:T(1024)} %concatenate.26.refs_8_.meta_ref, s32[8192]{0:T(1024)} %get-tuple-element.93.idx_ref, s32[64,1,128]{2,1,0:T(1,128)} %bitcast.74, ...), custom_call_target="tpu_custom_call" | custom-call | flops 120000000 | bytes 30000000 | tf_op jit(solution)/shard_map/owner_3/pallas_call | solution.py:356
  353.2 8.1 %all-to-all-start.4 = ((bf16[128,64,256]{2,1,0:T(8,128)(2,1)}), bf16[128,64,256]{2,1,0:T(8,128)(2,1)}, u32[]{:S(2)}, u32[]{:S(2)}) async-start(bf16[128,64,256]{2,1,0:T(8,128)(2,1)} %bitcast.54), calls=%async_computation.4 | async-start | bytes 8388608 | tf_op jit(solution)/shard_map/all_to_all | solution.py:588
  361.3 0.8 copy.33
  362.0 4.6 fusion.29
  366.7 24.3 %back_2_own.1.refs_1_ = f32[12288,256]{1,0:T(8,128)} custom-call(s32[905]{0:T(1024)} %concatenate.26.refs_8_.meta_ref, s32[24576]{0:T(1024)} %get-tuple-element.89.refs_9_.idx_ref, s32[192,1,128]{2,1,0:T(1,128)} %bitcast.63, bf16[12288,256]{1,0:T(8,128)(2,1)} %get-tuple-element.53.refs_0_, bf16[12288,256]{1,0:T(8,128)(2,1)} %get-tuple-element.54.refs_1_, ...), custom_call_target="tpu_custom_call" | custom-call | flops 120000000 | bytes 30000000 | tf_op jit(solution)/shard_map/back_2_own/pallas_call | solution.py:356
  391.0 5.4 %convolution_select_fusion.refs_3_ = f32[256,128]{1,0:T(8,128)} fusion(f32[256,128]{1,0:T(8,128)S(1)} %fusion.29, bf16[12288,256]{1,0:T(8,128)(2,1)} %get-tuple-element.51.refs_3_, bf16[12288,128]{1,0:T(8,128)(2,1)S(1)} %copy-done.2, pred[128]{0:T(512)(128)(4,1)S(1)} %iota_compare_fusion.2), kind=kOutput, calls=%fused_computation.1 | convolution fusion | flops 805339136 | bytes 9699456 | tf_op jit(solution)/shard_map/nd,ne->de/dot_general | solution.py:824
  396.4 7.3 %fusion.27.refs_1_ = f32[256,256]{1,0:T(8,128)} fusion(bf16[12288,256]{1,0:T(8,128)(2,1)} %get-tuple-element.44.refs_0_.refs_3_.refs_2_, bf16[12288,256]{1,0:T(8,128)(2,1)} %get-tuple-element.54.refs_1_), kind=kOutput, calls=%fused_computation.84 | convolution fusion | flops 1610612736 | bytes 12845056 | tf_op jit(solution)/shard_map/nd,ne->de/dot_general | solution.py:824
  403.7 2.5 fusion.28.refs_2_
  406.3 13.6 %all-to-all-done.4 = bf16[128,64,256]{2,1,0:T(8,128)(2,1)} async-done(((bf16[128,64,256]{2,1,0:T(8,128)(2,1)}), bf16[128,64,256]{2,1,0:T(8,128)(2,1)}, u32[]{:S(2)}, u32[]{:S(2)}) %all-to-all-start.4) | async-done | bytes 4194336 | tf_op jit(solution)/shard_map/all_to_all | solution.py:588
  419.8 19.9 %owner_2.1 = (f32[256,256]{1,0:T(8,128)}, f32[8,256]{1,0:T(8,128)}) custom-call(s32[905]{0:T(1024)} %concatenate.26.refs_8_.meta_ref, s32[8192]{0:T(1024)} %get-tuple-element.94.idx_ref, s32[64,1,128]{2,1,0:T(1,128)} %bitcast.75, bf16[8192,256]{1,0:T(8,128)(2,1)} %bitcast.28.refs_0_, f32[12288,256]{1,0:T(8,128)} %back_2_own.1.refs_1_, ...), custom_call_target="tpu_custom_call" | custom-call | flops 100000000 | bytes 25000000 | tf_op jit(solution)/shard_map/owner_2/pallas_call | solution.py:356
  439.7 37.8 %sum_all.1.full_ref = f32[2,64,16,128]{3,2,1,0:T(8,128)} custom-call(f32[256,256]{1,0:T(8,128)} %get-tuple-element.55.refs_0_, f32[256,256]{1,0:T(8,128)} %fusion.27.refs_1_, f32[256,256]{1,0:T(8,128)} %fusion.28.refs_2_, f32[256,128]{1,0:T(8,128)} %convolution_select_fusion.refs_3_, f32[8,256]{1,0:T(8,128)} %get-tuple-element.58.refs_4_, ...), custom_call_target="tpu_custom_call" | custom-call | flops 100000000 | bytes 25000000 | tf_op jit(solution)/shard_map/sum_all/pallas_call | solution.py:511
  477.6 2.1 unpack_sums.1
  (68 shorter events, 4.4 us)
Async XLA Ops:
  0.6 21.2 %copy-start.12 = (s32[24576]{0:T(1024)S(1)}, s32[24576]{0:T(1024)}, u32[]{:S(2)}) copy-start(s32[24576]{0:T(1024)} %param.20) | copy-start | bytes 294916
  0.7 21.2 %copy-start.13 = (s32[24576]{0:T(1024)S(1)}, s32[24576]{0:T(1024)}, u32[]{:S(2)}) copy-start(s32[24576]{0:T(1024)} %param.21) | copy-start | bytes 294916
  0.7 36.2 %copy-start.14 = (bf16[256,40]{0,1:T(8,128)(2,1)S(1)}, bf16[256,40]{0,1:T(8,128)(2,1)}, u32[]{:S(2)}) copy-start(bf16[256,40]{0,1:T(8,128)(2,1)} %param.30) | copy-start | bytes 61444
  0.7 36.3 %copy-start.15 = (bf16[256,40]{0,1:T(8,128)(2,1)S(1)}, bf16[256,40]{0,1:T(8,128)(2,1)}, u32[]{:S(2)}) copy-start(bf16[256,40]{0,1:T(8,128)(2,1)} %param.29) | copy-start | bytes 61444
  0.7 39.1 %copy-start.16 = (f32[12288]{0:T(1024)S(1)}, f32[12288]{0:T(1024)}, u32[]{:S(2)}) copy-start(f32[12288]{0:T(1024)} %param.22) | copy-start | bytes 147460
  10.4 52.4 %all-to-all-start = ((bf16[128,72,128]{2,1,0:T(8,128)(2,1)}), bf16[128,72,128]{2,1,0:T(8,128)(2,1)S(1)}, u32[]{:S(2)}, u32[]{:S(2)}) async-start(bf16[128,72,128]{2,1,0:T(8,128)(2,1)} %send_1.1), calls=%async_computation | async-start | bytes 4718592 | tf_op jit(solution)/shard_map/all_to_all | solution.py:588
  43.6 17.5 %copy-start.18 = (f32[40]{0:T(128)S(1)}, f32[40]{0:T(128)}, u32[]{:S(2)}) copy-start(f32[40]{0:T(128)} %param.31) | copy-start | bytes 484
  43.6 19.1 %copy-start.7 = (s32[128,64]{0,1:T(8,128)S(1)}, s32[128,64]{0,1:T(8,128)}, u32[]{:S(2)}) copy-start(s32[128,64]{0,1:T(8,128)} %param.19) | copy-start | bytes 98308
  62.8 1.4 copy-start.1
  64.2 41.0 %copy-start.11 = (f32[12288]{0:T(1024)S(1)}, f32[12288]{0:T(1024)}, u32[]{:S(2)}) copy-start(f32[12288]{0:T(1024)} %param.18) | copy-start | bytes 147460
  64.2 41.0 %copy-start.17 = (s32[12288]{0:T(1024)S(1)}, s32[12288]{0:T(1024)}, u32[]{:S(2)}) copy-start(s32[12288]{0:T(1024)} %param.17) | copy-start | bytes 147460
  93.8 45.6 %all-to-all-start.1 = ((bf16[128,64,128]{2,1,0:T(8,128)(2,1)}), bf16[128,64,128]{2,1,0:T(8,128)(2,1)S(1)}, u32[]{:S(2)}, u32[]{:S(2)}) async-start(bf16[128,64,128]{2,1,0:T(8,128)(2,1)} %get-tuple-element.43), calls=%async_computation.1 | async-start | bytes 4194304 | tf_op jit(solution)/shard_map/all_to_all | solution.py:588
  139.5 1.3 copy-start.4
  180.6 40.7 %all-to-all-start.2 = ((bf16[128,64,128]{2,1,0:T(8,128)(2,1)}), bf16[128,64,128]{2,1,0:T(8,128)(2,1)S(1)}, u32[]{:S(2)}, u32[]{:S(2)}) async-start(bf16[128,64,128]{2,1,0:T(8,128)(2,1)} %get-tuple-element.45), calls=%async_computation.2 | async-start | bytes 4194304 | tf_op jit(solution)/shard_map/all_to_all | solution.py:588
  195.1 25.9 %copy-start.6 = (s32[24576]{0:T(1024)}, s32[24576]{0:T(1024)S(1)}, u32[]{:S(2)}) copy-start(s32[24576]{0:T(1024)S(1)} %get-tuple-element.92) | copy-start | bytes 294916
  196.2 24.8 %copy-start.10 = (s32[8192]{0:T(1024)}, s32[8192]{0:T(1024)S(1)}, u32[]{:S(2)}) copy-start(s32[8192]{0:T(1024)S(1)} %get-tuple-element.95) | copy-start | bytes 98308
  221.3 1.3 copy-start.3
  222.7 54.7 %copy-start.8 = (bf16[256,256]{1,0:T(8,128)(2,1)S(1)}, bf16[256,256]{1,0:T(8,128)(2,1)}, u32[]{:S(2)}) copy-start(bf16[256,256]{1,0:T(8,128)(2,1)} %refs_6_.1) | copy-start | bytes 393220
  265.4 46.2 %all-to-all-start.3 = ((bf16[128,64,128]{2,1,0:T(8,128)(2,1)}), bf16[128,64,128]{2,1,0:T(8,128)(2,1)S(1)}, u32[]{:S(2)}, u32[]{:S(2)}) async-start(bf16[128,64,128]{2,1,0:T(8,128)(2,1)} %bitcast.55), calls=%async_computation.3 | async-start | bytes 4194304 | tf_op jit(solution)/shard_map/all_to_all | solution.py:588
  311.6 1.3 copy-start.5
  353.2 8.1 %copy-start.9 = (bf16[256,256]{1,0:T(8,128)(2,1)S(1)}, bf16[256,256]{1,0:T(8,128)(2,1)}, u32[]{:S(2)}) copy-start(bf16[256,256]{1,0:T(8,128)(2,1)} %refs_5_.3) | copy-start | bytes 393220
  353.2 8.9 %copy-start = (bf16[12288,128]{1,0:T(8,128)(2,1)S(1)}, bf16[12288,128]{1,0:T(8,128)(2,1)}, u32[]{:S(2)}) copy-start(bf16[12288,128]{1,0:T(8,128)(2,1)} %get-tuple-element.50.refs_2_) | copy-start | bytes 9437188
  353.2 66.6 %all-to-all-start.4 = ((bf16[128,64,256]{2,1,0:T(8,128)(2,1)}), bf16[128,64,256]{2,1,0:T(8,128)(2,1)}, u32[]{:S(2)}, u32[]{:S(2)}) async-start(bf16[128,64,256]{2,1,0:T(8,128)(2,1)} %bitcast.54), calls=%async_computation.4 | async-start | bytes 8388608 | tf_op jit(solution)/shard_map/all_to_all | solution.py:588
  366.7 24.3 %copy-start.2 = (bf16[12288,128]{1,0:T(8,128)(2,1)S(1)}, bf16[12288,128]{1,0:T(8,128)(2,1)}, u32[]{:S(2)}) copy-start(bf16[12288,128]{1,0:T(8,128)(2,1)} %get-tuple-element.57) | copy-start | bytes 9437188
  391.0 12.7 %slice-start = ((s8[6291456]{0:T(1024)(128)(4,1)}), s8[4194304]{0:T(1024)(128)(4,1)S(1)}, s32[]{:S(2)}) async-start(s8[6291456]{0:T(1024)(128)(4,1)} %bitcast.48), calls=%async_computation.5 | async-start | bytes 8388608
  391.0 12.7 %slice-start.2 = ((s8[6291456]{0:T(1024)(128)(4,1)}), s8[4194304]{0:T(1024)(128)(4,1)S(1)}, s32[]{:S(2)}) async-start(s8[6291456]{0:T(1024)(128)(4,1)} %bitcast.50), calls=%async_computation.7 | async-start | bytes 8388608
  396.4 7.3 %slice-start.1 = ((s8[6291456]{0:T(1024)(128)(4,1)}), s8[2097152]{0:T(1024)(128)(4,1)S(1)}, s32[]{:S(2)}) async-start(s8[6291456]{0:T(1024)(128)(4,1)} %bitcast.48), calls=%async_computation.6 | async-start | bytes 4194304
  396.4 7.3 %slice-start.3 = ((s8[6291456]{0:T(1024)(128)(4,1)}), s8[2097152]{0:T(1024)(128)(4,1)S(1)}, s32[]{:S(2)}) async-start(s8[6291456]{0:T(1024)(128)(4,1)} %bitcast.50), calls=%async_computation.8 | async-start | bytes 4194304

commit v4 on v3

--- a/solution.py
+++ b/solution.py
@@ -235,16 +235,17 @@
         compiler_params=params(), cost_estimate=cost(10))(*operands)
 
 
-def pick_into(idx, tab, stage, peers, slots):
-    def body(p, carry):
-        for g in range(slots // 16):
-            stage[p, g * 16:g * 16 + 16, :] = gather_16(idx, p, g * 16, slots, tab, 1, peers)[0]
-        return carry
-    lax.fori_loop(0, peers, body, 0)
-
-
-def send_out(stage, out, sem):
-    done = pltpu.make_async_copy(stage, out, sem)
+PIECES = 4
+
+
+def send_part(stage, out, sem, k):
+    size = stage.shape[0] // PIECES
+    at = pl.multiple_of(k * size, size)
+    return pltpu.make_async_copy(stage.at[pl.ds(at, size)], out.at[pl.ds(at, size)], sem.at[k])
+
+
+def send_out(src, out, sem):
+    done = pltpu.make_async_copy(src, out, sem)
     done.start()
     done.wait()
 
@@ -268,7 +269,7 @@
         more_in.append(p_idx)
         more_specs.append(SMEM_SPEC)
         more_out.append(jax.ShapeDtypeStruct((peers, slots, LANES), BF16))
-        more_scratch.append(pltpu.VMEM((peers, slots, LANES), BF16))
+        more_scratch += [pltpu.VMEM((peers, slots, LANES), BF16), pltpu.SemaphoreType.DMA((PIECES,))]
     if then:
         (t_meta, t_at, t_idx, t_seg), t_nc, t_rows, t_window, finish = then
         t_width = t_nc * LANES
@@ -277,7 +278,8 @@
         more_specs += [SMEM_SPEC, SMEM_SPEC, whole_spec(t_seg.shape)]
         more_out.append(jax.ShapeDtypeStruct((t_rows, t_width), BF16))
         more_scratch += [pltpu.VMEM((t_total, t_width), F32), pltpu.VMEM((BLOCK, t_width), BF16),
-                         pltpu.VMEM((BLOCK, t_width), BF16), pltpu.VMEM((t_rows, t_width), BF16)]
+                         pltpu.VMEM((BLOCK, t_width), BF16), pltpu.VMEM((t_rows, t_width), BF16),
+                         pltpu.SemaphoreType.DMA((PIECES,))]
     nm = len(more_in)
 
     def kern(meta_ref, idx_ref, seg_ref, *refs):
@@ -298,7 +300,8 @@
             copies = [fetch(h, st, sm, parts) for h, st, sm in zip(hb, stages, sems)]
             if init is not None:
                 start = pltpu.make_async_copy(hb[init], begin if late else acc.at[pl.ds(0, acc_rows), :], isem)
-                start.start()
+                if not late:
+                    start.start()
             if init is None or late:
                 zero_rows(acc)
             for o, (_, _, sums) in zip(out, outs):
@@ -307,6 +310,8 @@
             if then:
                 zero_rows(scratch[1])
             build(copies, stages, tab, fx)
+            if late:
+                start.start()
             if init is not None and not late:
                 start.wait()
             segment_sums(meta_ref, meta_at, idx_ref, seg_ref, tab, acc, (buf_0, buf_1), nc, window, blocks)
@@ -332,22 +337,41 @@
         if pick:
             @pl.when(i == steps - 1)
             def _():
-                pick_into(extra[0], scratch[0], scratch[1], peers, slots)
-                send_out(scratch[1], last_out[0], isem)
+                kept, stage, out_sem = scratch
+                size = peers // PIECES
+
+                def piece(k, c):
+                    def body(p, carry):
+                        for g in range(slots // 16):
+                            rows = gather_16(extra[0], k * size + p, g * 16, slots, kept, 1, peers)[0]
+                            stage[k * size + p, g * 16:g * 16 + 16, :] = rows
+                        return carry
+                    lax.fori_loop(0, size, body, 0)
+                    send_part(stage, last_out[0], out_sem, k).start()
+                    return c
+                lax.fori_loop(0, PIECES, piece, 0)
+                for k in range(PIECES):
+                    send_part(stage, last_out[0], out_sem, k).wait()
         if then:
             @pl.when(i == steps - 1)
             def _():
-                kept, acc_2, buf_2, buf_3, stage = scratch
+                kept, acc_2, buf_2, buf_3, stage, out_sem = scratch
                 segment_sums(extra[0], t_at, extra[1], extra[2], kept, acc_2, (buf_2, buf_3), t_nc, t_window,
                              t_seg.shape[0])
-                step = math.gcd(1024, t_rows)
-
-                def part(j, carry):
-                    at = pl.multiple_of(j * step, step)
-                    stage[pl.ds(at, step), :] = finish(acc_2[pl.ds(at, step), :], fx)
-                    return carry
-                lax.fori_loop(0, t_rows // step, part, 0)
-                send_out(stage, last_out[0], isem)
+                size = t_rows // PIECES
+                step = math.gcd(1024, size)
+
+                def piece(k, c):
+                    def part(j, carry):
+                        at = pl.multiple_of(k * size + j * step, step)
+                        stage[pl.ds(at, step), :] = finish(acc_2[pl.ds(at, step), :], fx)
+                        return carry
+                    lax.fori_loop(0, size // step, part, 0)
+                    send_part(stage, last_out[0], out_sem, k).start()
+                    return c
+                lax.fori_loop(0, PIECES, piece, 0)
+                for k in range(PIECES):
+                    send_part(stage, last_out[0], out_sem, k).wait()
 
     out_shape, out_specs = [], []
     for shape, dtype, sums in outs:
@@ -606,7 +630,7 @@
         blocks = edges // BLOCK
         halo_blocks = halo // BLOCK
         zero = jnp.int32(0)
-        win_e, win_h, win_r = 176, 192, 240
+        win_e, win_h, win_r = 192, 208, 272
         owned = jnp.sum((src_idx < n).astype(jnp.int32))
         near_end = (owned + BLOCK - 1) // BLOCK
         far_start = owned // BLOCK
@@ -739,7 +763,7 @@
             [(peers, slots + TAIL, LANES), (peers, slots, LANES)], build_2, [got_1, got_2, near_2],
             [hidden_1, inv], [w_self_2, w_neigh_2, b2, w_self_1, w_neigh_1, b1, jnp.concatenate([wn3, ws3], axis=1)],
             [((n, hidden), BF16, False), ((n, hidden), BF16, False), ((n, LANES), BF16, False),
-             ((n, LANES), F32, False)], n, half_tile, epi_2, 40, init=2, keep=1, pick=(send_flat, peers, slots))
+             ((n, LANES), F32, False)], n, tile, epi_2, 40, init=2, keep=1, pick=(send_flat, peers, slots))
 
         got_3 = exchange(out_3).reshape(halo, LANES)
         near_3 = near_sums('near_3', 1, src_near, proj, [target])
@@ -771,7 +795,7 @@
             'layer_3', (meta_f, far_at, src_far, seg_far), 1, halo, n, win_e, [(halo, LANES)], rows_of(1), [got_3, near_3],
             [logits_self, inv, target], [b3, jnp.broadcast_to(inv_total, (1, LANES)), folder],
             [((n, LANES), BF16, False), ((n, LANES), BF16, False), ((8, LANES), F32, True), ((8, LANES), F32, True)],
-            n, half_tile, epi_3, 30, init=1, late=True, keep=1,
+            n, tile, epi_3, 30, init=1, late=True, keep=1,
             then=((meta_b, halo_at, dst_s, seg_h), 1, halo, win_h, finish_3))
 
         ret_3 = exchange(back_3.reshape(peers, slots, LANES)).reshape(halo, LANES)

time: 486 us -> 481 us (0.990)
  starting transfers between devices: 49.3 us -> 42.5 us
    all_to_all x5, starting transfers between devices: 49.3 us -> 42.5 us  [exchange(): return lax.all_to_all(x, GROUP_AXIS, 0, 0, tiled=True)]
  transfers between devices with their start and end apart: 5 -> 5, of which waited for: 4 -> 4; matrix products, arithmetic and copies ran while one was open for 13% -> 14% of each run, Pallas kernels for 20% -> 21%
where the time goes in v4:
time: 481 us; the launch traced here: 472 us
  Pallas kernels  318 us (66%)
  starting transfers between devices  42.5 us (9%)
  waiting for transfers between devices  35.7 us (7%)
  other arithmetic  32 us (7%)
  matrix products  19.9 us (4%)
  local copies, waits for them, and re-layouts  17.3 us (4%)
  between operations  6.21 us (1%)
    pallas_call x10, Pallas kernels, edge_call(): pl.pallas_call(kern, name=name, grid=(steps,), out_shape=out_shape + more...  270 us
    all_to_all x5, starting transfers between devices, exchange(): return lax.all_to_all(x, GROUP_AXIS, 0, 0, tiled=True)  42.5 us
    pallas_call x1, Pallas kernels, sum_over_devices(): pl.pallas_call(kern, name='sum_all', out_shape=jax.ShapeDtypeStruct(shape...  36.3 us
    all_to_all x5, waiting for transfers between devices, exchange(): return lax.all_to_all(x, GROUP_AXIS, 0, 0, tiled=True)  35.7 us
    dot_general x4, matrix products, contract(): return jnp.einsum('nd,ne->de', a, b, preferred_element_type=F32)  19.9 us
    pallas_call x1, Pallas kernels, pick_rows(): pl.pallas_call(kern, name=name, grid=(peers // per,), out_shape=jax.Shape...  9.65 us
  transfers between devices with their start and end apart: 5, of which 4 were waited for; matrix products, arithmetic and copies ran while one was open for 14% of the time, Pallas kernels for 21%

profile of v4, /device:TPU:1, one launch (start us, length us, event | category | flops | bytes accessed | tf_op | source)
XLA Modules:
  0.0 471.6 jit_solution(2617904404998442055)
XLA Ops:
  0.7 9.7 %send_1.1 = bf16[128,72,128]{2,1,0:T(8,128)(2,1)} custom-call(s32[8192]{0:T(1024)} %bitcast.69, bf16[12288,128]{1,0:T(8,128)(2,1)} %refs_3_.1, f32[96,128]{1,0:T(8,128)} %bitcast.76), custom_call_target="tpu_custom_call" | custom-call | flops 40000000 | bytes 10000000 | tf_op jit(solution)/shard_map/send_1/pallas_call | solution.py:228
  10.4 11.5 %all-to-all-start = ((bf16[128,72,128]{2,1,0:T(8,128)(2,1)}), bf16[128,72,128]{2,1,0:T(8,128)(2,1)S(1)}, u32[]{:S(2)}, u32[]{:S(2)}) async-start(bf16[128,72,128]{2,1,0:T(8,128)(2,1)} %send_1.1), calls=%async_computation | async-start | bytes 4718592 | tf_op jit(solution)/shard_map/all_to_all | solution.py:612
  21.9 0.7 or_or_fusion
  23.8 8.6 %sort.14 = s32[24576]{0:T(1024)S(1)} sort(s32[24576]{0:T(1024)S(1)} %get-tuple-element.87), dimensions={0}, to_apply=%region_0.0 | sort | flops 368640 | bytes 196608 | tf_op jit(solution)/shard_map/sort | solution.py:640
  32.4 0.8 broadcast_select_fusion
  33.4 0.7 broadcast_select_fusion.1
  37.1 0.7 fusion.25
  37.8 2.0 concatenate.25.meta_ref
  39.7 3.9 broadcast_in_dim.66.refs_1_.refs_3_.refs_4_
  43.6 17.3 %near_1.1.refs_1_ = f32[12288,128]{1,0:T(8,128)} custom-call(s32[774]{0:T(1024)} %concatenate.25.meta_ref, s32[24576]{0:T(1024)} %get-tuple-element.98.idx_ref, s32[192,1,128]{2,1,0:T(1,128)} %bitcast.59, bf16[12288,128]{1,0:T(8,128)(2,1)} %refs_3_.1, f32[12288,128]{1,0:T(8,128)} %broadcast_in_dim.66.refs_1_.refs_3_.refs_4_), custom_call_target="tpu_custom_call" | custom-call | flops 80000000 | bytes 20000000 | tf_op jit(solution)/shard_map/near_1/pallas_call | solution.py:380
  61.0 0.7 compare_select_fusion.refs_5_
  61.8 0.7 pad_maximum_fusion.refs_11_
  62.6 1.4 copy-done.1
  64.0 29.0 %layer_1.1 = (bf16[12288,128]{1,0:T(8,128)(2,1)}, bf16[12288,256]{1,0:T(8,128)(2,1)}, bf16[128,64,128]{2,1,0:T(8,128)(2,1)}) custom-call(s32[774]{0:T(1024)} %concatenate.25.meta_ref, s32[24576]{0:T(1024)} %get-tuple-element.100.idx_ref, s32[192,1,128]{2,1,0:T(1,128)} %bitcast.56, bf16[128,72,128]{2,1,0:T(8,128)(2,1)} %copy-done.1, ...), custom_call_target="tpu_custom_call" | custom-call | flops 100000000 | bytes 25000000 | tf_op jit(solution)/shard_map/layer_1/pallas_call | solution.py:380
  93.0 9.8 %all-to-all-start.1 = ((bf16[128,64,128]{2,1,0:T(8,128)(2,1)}), bf16[128,64,128]{2,1,0:T(8,128)(2,1)S(1)}, u32[]{:S(2)}, u32[]{:S(2)}) async-start(bf16[128,64,128]{2,1,0:T(8,128)(2,1)} %get-tuple-element.43), calls=%async_computation.1 | async-start | bytes 4194304 | tf_op jit(solution)/shard_map/all_to_all | solution.py:612
  102.8 6.7 %select_convert_fusion.refs_1_.refs_4_ = bf16[12288,128]{1,0:T(8,128)(2,1)} fusion(s32[128]{0:T(128)S(1)} %and_select_fusion, f32[12288]{0:T(1024)S(1)} %copy-done.11, s32[12288]{0:T(1024)S(1)} %copy-done.17, pred[128]{0:T(512)(128)(4,1)S(1)} %iota_compare_fusion.3), kind=kLoop, calls=%fused_computation | loop fusion | flops 9437184 | bytes 3244672 | tf_op jit(solution)/shard_map/convert_element_type | solution.py:664
  109.5 21.5 %near_2.1.refs_2_ = f32[12288,256]{1,0:T(8,128)} custom-call(s32[774]{0:T(1024)} %concatenate.25.meta_ref, s32[24576]{0:T(1024)} %get-tuple-element.96.idx_ref, s32[192,1,128]{2,1,0:T(1,128)} %bitcast.60, bf16[12288,256]{1,0:T(8,128)(2,1)} %get-tuple-element.44.refs_0_.refs_3_.refs_2_), custom_call_target="tpu_custom_call" | custom-call | flops 80000000 | bytes 20000000 | tf_op jit(solution)/shard_map/near_2/pallas_call | solution.py:380
  131.0 6.1 %all-to-all-done.1.refs_1_ = bf16[128,64,128]{2,1,0:T(8,128)(2,1)S(1)} async-done(((bf16[128,64,128]{2,1,0:T(8,128)(2,1)}), bf16[128,64,128]{2,1,0:T(8,128)(2,1)S(1)}, u32[]{:S(2)}, u32[]{:S(2)}) %all-to-all-start.1) | async-done | bytes 2097184 | tf_op jit(solution)/shard_map/all_to_all | solution.py:612
  137.1 1.3 copy-done.4
  138.4 39.7 %layer_2.1 = (bf16[12288,256]{1,0:T(8,128)(2,1)}, bf16[12288,256]{1,0:T(8,128)(2,1)}, bf16[12288,128]{1,0:T(8,128)(2,1)}, f32[12288,128]{1,0:T(8,128)}, bf16[128,64,128]{2,1,0:T(8,128)(2,1)}) custom-call(s32[774]{0:T(1024)} %concatenate.25.meta_ref, s32[24576]{0:T(1024)} %get-tuple-element.97.idx_ref, s32[192,1,128]{2,1,0:T(1,128)} %bitcast.57, ...), custom_call_target="tpu_custom_call" | custom-call | flops 160000000 | bytes 40000000 | tf_op jit(solution)/shard_map/layer_2/pallas_call | solution.py:380
  178.1 4.7 all-to-all-start.2
  182.8 7.3 %sort.15 = s32[32768]{0:T(1024)S(1)} sort(s32[32768]{0:T(1024)S(1)} %pad_add_fusion), dimensions={0}, to_apply=%region_4.5 | sort | flops 491520 | bytes 262144 | tf_op jit(solution)/shard_map/sort | solution.py:713
  190.1 0.7 and_or_fusion
  192.2 1.0 slice_convert_fusion
  193.2 0.7 slice_reduce_fusion
  195.9 0.7 fusion.23
  196.6 2.6 concatenate.26.refs_8_.meta_ref
  199.2 17.4 %near_3.1.refs_1_ = f32[12288,128]{1,0:T(8,128)} custom-call(s32[774]{0:T(1024)} %concatenate.25.meta_ref, s32[24576]{0:T(1024)} %get-tuple-element.98.idx_ref, s32[192,1,128]{2,1,0:T(1,128)} %bitcast.61, bf16[12288,128]{1,0:T(8,128)(2,1)} %get-tuple-element.46.refs_0_, bf16[12288,128]{1,0:T(8,128)(2,1)} %select_convert_fusion.refs_1_.refs_4_), custom_call_target="tpu_custom_call" | custom-call | flops 80000000 | bytes 20000000 | tf_op jit(solution)/shard_map/near_3/pallas_call | solution.py:380
  217.7 0.8 tile.13
  218.5 42.7 %layer_3.1 = (bf16[12288,128]{1,0:T(8,128)(2,1)}, bf16[12288,128]{1,0:T(8,128)(2,1)}, f32[8,128]{1,0:T(8,128)}, f32[8,128]{1,0:T(8,128)}, bf16[8192,128]{1,0:T(8,128)(2,1)}) custom-call(s32[774]{0:T(1024)} %concatenate.25.meta_ref, s32[24576]{0:T(1024)} %get-tuple-element.100.idx_ref, s32[192,1,128]{2,1,0:T(1,128)} %bitcast.58, bf16[8192,128]{1,0:T(8,128)(2,1)} %bitcast.52, ...), custom_call_target="tpu_custom_call" | custom-call | flops 120000000 | bytes 30000000 | tf_op jit(solution)/shard_map/layer_3/pallas_call | solution.py:380
  261.3 9.9 %all-to-all-start.3 = ((bf16[128,64,128]{2,1,0:T(8,128)(2,1)}), bf16[128,64,128]{2,1,0:T(8,128)(2,1)S(1)}, u32[]{:S(2)}, u32[]{:S(2)}) async-start(bf16[128,64,128]{2,1,0:T(8,128)(2,1)} %bitcast.55), calls=%async_computation.3 | async-start | bytes 4194304 | tf_op jit(solution)/shard_map/all_to_all | solution.py:612
  271.1 0.8 copy.32
  271.9 0.7 pad_maximum_fusion.1.refs_5_
  272.6 17.2 %back_3_own.1.refs_1_ = f32[12288,128]{1,0:T(8,128)} custom-call(s32[905]{0:T(1024)} %concatenate.26.refs_8_.meta_ref, s32[24576]{0:T(1024)} %get-tuple-element.91.refs_9_.idx_ref, s32[192,1,128]{2,1,0:T(1,128)} %bitcast.62, bf16[12288,128]{1,0:T(8,128)(2,1)} %get-tuple-element.49.refs_0_), custom_call_target="tpu_custom_call" | custom-call | flops 80000000 | bytes 20000000 | tf_op jit(solution)/shard_map/back_3_own/pallas_call | solution.py:380
  289.8 15.6 %all-to-all-done.3 = bf16[128,64,128]{2,1,0:T(8,128)(2,1)S(1)} async-done(((bf16[128,64,128]{2,1,0:T(8,128)(2,1)}), bf16[128,64,128]{2,1,0:T(8,128)(2,1)S(1)}, u32[]{:S(2)}, u32[]{:S(2)}) %all-to-all-start.3) | async-done | bytes 2097184 | tf_op jit(solution)/shard_map/all_to_all | solution.py:612
  305.4 1.3 copy-done.5
  306.7 40.3 %owner_3.1 = (bf16[12288,128]{1,0:T(8,128)(2,1)}, bf16[12288,256]{1,0:T(8,128)(2,1)}, bf16[12288,256]{1,0:T(8,128)(2,1)}, f32[8,256]{1,0:T(8,128)}, bf16[8192,256]{1,0:T(8,128)(2,1)}) custom-call(s32[905]{0:T(1024)} %concatenate.26.refs_8_.meta_ref, s32[8192]{0:T(1024)} %get-tuple-element.93.idx_ref, s32[64,1,128]{2,1,0:T(1,128)} %bitcast.74, ...), custom_call_target="tpu_custom_call" | custom-call | flops 120000000 | bytes 30000000 | tf_op jit(solution)/shard_map/owner_3/pallas_call | solution.py:380
  347.1 6.7 %all-to-all-start.4 = ((bf16[128,64,256]{2,1,0:T(8,128)(2,1)}), bf16[128,64,256]{2,1,0:T(8,128)(2,1)}, u32[]{:S(2)}, u32[]{:S(2)}) async-start(bf16[128,64,256]{2,1,0:T(8,128)(2,1)} %bitcast.54), calls=%async_computation.4 | async-start | bytes 8388608 | tf_op jit(solution)/shard_map/all_to_all | solution.py:612
  353.7 0.8 copy.33
  354.5 4.6 fusion.29
  359.1 24.6 %back_2_own.1.refs_1_ = f32[12288,256]{1,0:T(8,128)} custom-call(s32[905]{0:T(1024)} %concatenate.26.refs_8_.meta_ref, s32[24576]{0:T(1024)} %get-tuple-element.89.refs_9_.idx_ref, s32[192,1,128]{2,1,0:T(1,128)} %bitcast.63, bf16[12288,256]{1,0:T(8,128)(2,1)} %get-tuple-element.53.refs_0_, bf16[12288,256]{1,0:T(8,128)(2,1)} %get-tuple-element.54.refs_1_, ...), custom_call_target="tpu_custom_call" | custom-call | flops 120000000 | bytes 30000000 | tf_op jit(solution)/shard_map/back_2_own/pallas_call | solution.py:380
  383.7 5.4 %convolution_select_fusion.refs_3_ = f32[256,128]{1,0:T(8,128)} fusion(f32[256,128]{1,0:T(8,128)S(1)} %fusion.29, bf16[12288,256]{1,0:T(8,128)(2,1)} %get-tuple-element.51.refs_3_, bf16[12288,128]{1,0:T(8,128)(2,1)S(1)} %copy-done.2, pred[128]{0:T(512)(128)(4,1)S(1)} %iota_compare_fusion.2), kind=kOutput, calls=%fused_computation.1 | convolution fusion | flops 805339136 | bytes 9699456 | tf_op jit(solution)/shard_map/nd,ne->de/dot_general | solution.py:848
  389.2 7.3 %fusion.27.refs_1_ = f32[256,256]{1,0:T(8,128)} fusion(bf16[12288,256]{1,0:T(8,128)(2,1)} %get-tuple-element.44.refs_0_.refs_3_.refs_2_, bf16[12288,256]{1,0:T(8,128)(2,1)} %get-tuple-element.54.refs_1_), kind=kOutput, calls=%fused_computation.84 | convolution fusion | flops 1610612736 | bytes 12845056 | tf_op jit(solution)/shard_map/nd,ne->de/dot_general | solution.py:848
  396.5 2.5 fusion.28.refs_2_
  399.0 13.4 %all-to-all-done.4 = bf16[128,64,256]{2,1,0:T(8,128)(2,1)} async-done(((bf16[128,64,256]{2,1,0:T(8,128)(2,1)}), bf16[128,64,256]{2,1,0:T(8,128)(2,1)}, u32[]{:S(2)}, u32[]{:S(2)}) %all-to-all-start.4) | async-done | bytes 4194336 | tf_op jit(solution)/shard_map/all_to_all | solution.py:612
  412.4 20.3 %owner_2.1 = (f32[256,256]{1,0:T(8,128)}, f32[8,256]{1,0:T(8,128)}) custom-call(s32[905]{0:T(1024)} %concatenate.26.refs_8_.meta_ref, s32[8192]{0:T(1024)} %get-tuple-element.94.idx_ref, s32[64,1,128]{2,1,0:T(1,128)} %bitcast.75, bf16[8192,256]{1,0:T(8,128)(2,1)} %bitcast.28.refs_0_, f32[12288,256]{1,0:T(8,128)} %back_2_own.1.refs_1_, ...), custom_call_target="tpu_custom_call" | custom-call | flops 100000000 | bytes 25000000 | tf_op jit(solution)/shard_map/owner_2/pallas_call | solution.py:380
  432.7 36.3 %sum_all.1.full_ref = f32[2,64,16,128]{3,2,1,0:T(8,128)} custom-call(f32[256,256]{1,0:T(8,128)} %get-tuple-element.55.refs_0_, f32[256,256]{1,0:T(8,128)} %fusion.27.refs_1_, f32[256,256]{1,0:T(8,128)} %fusion.28.refs_2_, f32[256,128]{1,0:T(8,128)} %convolution_select_fusion.refs_3_, f32[8,256]{1,0:T(8,128)} %get-tuple-element.58.refs_4_, ...), custom_call_target="tpu_custom_call" | custom-call | flops 100000000 | bytes 25000000 | tf_op jit(solution)/shard_map/sum_all/pallas_call | solution.py:535
  469.1 2.1 unpack_sums.1
  (68 shorter events, 4.6 us)
Async XLA Ops:
  0.6 21.2 %copy-start.12 = (s32[24576]{0:T(1024)S(1)}, s32[24576]{0:T(1024)}, u32[]{:S(2)}) copy-start(s32[24576]{0:T(1024)} %param.20) | copy-start | bytes 294916
  0.7 21.2 %copy-start.13 = (s32[24576]{0:T(1024)S(1)}, s32[24576]{0:T(1024)}, u32[]{:S(2)}) copy-start(s32[24576]{0:T(1024)} %param.21) | copy-start | bytes 294916
  0.7 36.2 %copy-start.14 = (bf16[256,40]{0,1:T(8,128)(2,1)S(1)}, bf16[256,40]{0,1:T(8,128)(2,1)}, u32[]{:S(2)}) copy-start(bf16[256,40]{0,1:T(8,128)(2,1)} %param.30) | copy-start | bytes 61444
  0.7 36.3 %copy-start.15 = (bf16[256,40]{0,1:T(8,128)(2,1)S(1)}, bf16[256,40]{0,1:T(8,128)(2,1)}, u32[]{:S(2)}) copy-start(bf16[256,40]{0,1:T(8,128)(2,1)} %param.29) | copy-start | bytes 61444
  0.7 39.1 %copy-start.16 = (f32[12288]{0:T(1024)S(1)}, f32[12288]{0:T(1024)}, u32[]{:S(2)}) copy-start(f32[12288]{0:T(1024)} %param.22) | copy-start | bytes 147460
  10.4 52.3 %all-to-all-start = ((bf16[128,72,128]{2,1,0:T(8,128)(2,1)}), bf16[128,72,128]{2,1,0:T(8,128)(2,1)S(1)}, u32[]{:S(2)}, u32[]{:S(2)}) async-start(bf16[128,72,128]{2,1,0:T(8,128)(2,1)} %send_1.1), calls=%async_computation | async-start | bytes 4718592 | tf_op jit(solution)/shard_map/all_to_all | solution.py:612
  43.6 17.4 %copy-start.18 = (f32[40]{0:T(128)S(1)}, f32[40]{0:T(128)}, u32[]{:S(2)}) copy-start(f32[40]{0:T(128)} %param.31) | copy-start | bytes 484
  43.6 19.0 %copy-start.7 = (s32[128,64]{0,1:T(8,128)S(1)}, s32[128,64]{0,1:T(8,128)}, u32[]{:S(2)}) copy-start(s32[128,64]{0,1:T(8,128)} %param.19) | copy-start | bytes 98308
  62.6 1.4 copy-start.1
  64.0 38.8 %copy-start.11 = (f32[12288]{0:T(1024)S(1)}, f32[12288]{0:T(1024)}, u32[]{:S(2)}) copy-start(f32[12288]{0:T(1024)} %param.18) | copy-start | bytes 147460
  64.0 38.8 %copy-start.17 = (s32[12288]{0:T(1024)S(1)}, s32[12288]{0:T(1024)}, u32[]{:S(2)}) copy-start(s32[12288]{0:T(1024)} %param.17) | copy-start | bytes 147460
  93.0 44.1 %all-to-all-start.1 = ((bf16[128,64,128]{2,1,0:T(8,128)(2,1)}), bf16[128,64,128]{2,1,0:T(8,128)(2,1)S(1)}, u32[]{:S(2)}, u32[]{:S(2)}) async-start(bf16[128,64,128]{2,1,0:T(8,128)(2,1)} %get-tuple-element.43), calls=%async_computation.1 | async-start | bytes 4194304 | tf_op jit(solution)/shard_map/all_to_all | solution.py:612
  137.1 1.3 copy-start.4
  178.1 39.1 %all-to-all-start.2 = ((bf16[128,64,128]{2,1,0:T(8,128)(2,1)}), bf16[128,64,128]{2,1,0:T(8,128)(2,1)S(1)}, u32[]{:S(2)}, u32[]{:S(2)}) async-start(bf16[128,64,128]{2,1,0:T(8,128)(2,1)} %get-tuple-element.45), calls=%async_computation.2 | async-start | bytes 4194304 | tf_op jit(solution)/shard_map/all_to_all | solution.py:612
  190.8 25.7 %copy-start.6 = (s32[24576]{0:T(1024)}, s32[24576]{0:T(1024)S(1)}, u32[]{:S(2)}) copy-start(s32[24576]{0:T(1024)S(1)} %get-tuple-element.92) | copy-start | bytes 294916
  191.9 24.7 %copy-start.10 = (s32[8192]{0:T(1024)}, s32[8192]{0:T(1024)S(1)}, u32[]{:S(2)}) copy-start(s32[8192]{0:T(1024)S(1)} %get-tuple-element.95) | copy-start | bytes 98308
  217.2 1.3 copy-start.3
  218.5 52.6 %copy-start.8 = (bf16[256,256]{1,0:T(8,128)(2,1)S(1)}, bf16[256,256]{1,0:T(8,128)(2,1)}, u32[]{:S(2)}) copy-start(bf16[256,256]{1,0:T(8,128)(2,1)} %refs_6_.1) | copy-start | bytes 393220
  261.3 44.1 %all-to-all-start.3 = ((bf16[128,64,128]{2,1,0:T(8,128)(2,1)}), bf16[128,64,128]{2,1,0:T(8,128)(2,1)S(1)}, u32[]{:S(2)}, u32[]{:S(2)}) async-start(bf16[128,64,128]{2,1,0:T(8,128)(2,1)} %bitcast.55), calls=%async_computation.3 | async-start | bytes 4194304 | tf_op jit(solution)/shard_map/all_to_all | solution.py:612
  305.4 1.3 copy-start.5
  347.0 6.7 %copy-start.9 = (bf16[256,256]{1,0:T(8,128)(2,1)S(1)}, bf16[256,256]{1,0:T(8,128)(2,1)}, u32[]{:S(2)}) copy-start(bf16[256,256]{1,0:T(8,128)(2,1)} %refs_5_.3) | copy-start | bytes 393220
  347.1 7.5 %copy-start = (bf16[12288,128]{1,0:T(8,128)(2,1)S(1)}, bf16[12288,128]{1,0:T(8,128)(2,1)}, u32[]{:S(2)}) copy-start(bf16[12288,128]{1,0:T(8,128)(2,1)} %get-tuple-element.50.refs_2_) | copy-start | bytes 9437188
  347.1 65.4 %all-to-all-start.4 = ((bf16[128,64,256]{2,1,0:T(8,128)(2,1)}), bf16[128,64,256]{2,1,0:T(8,128)(2,1)}, u32[]{:S(2)}, u32[]{:S(2)}) async-start(bf16[128,64,256]{2,1,0:T(8,128)(2,1)} %bitcast.54), calls=%async_computation.4 | async-start | bytes 8388608 | tf_op jit(solution)/shard_map/all_to_all | solution.py:612
  359.1 24.6 %copy-start.2 = (bf16[12288,128]{1,0:T(8,128)(2,1)S(1)}, bf16[12288,128]{1,0:T(8,128)(2,1)}, u32[]{:S(2)}) copy-start(bf16[12288,128]{1,0:T(8,128)(2,1)} %get-tuple-element.57) | copy-start | bytes 9437188
  383.7 12.7 %slice-start = ((s8[6291456]{0:T(1024)(128)(4,1)}), s8[4194304]{0:T(1024)(128)(4,1)S(1)}, s32[]{:S(2)}) async-start(s8[6291456]{0:T(1024)(128)(4,1)} %bitcast.48), calls=%async_computation.5 | async-start | bytes 8388608
  383.7 12.7 %slice-start.2 = ((s8[6291456]{0:T(1024)(128)(4,1)}), s8[4194304]{0:T(1024)(128)(4,1)S(1)}, s32[]{:S(2)}) async-start(s8[6291456]{0:T(1024)(128)(4,1)} %bitcast.50), calls=%async_computation.7 | async-start | bytes 8388608
  389.2 7.3 %slice-start.1 = ((s8[6291456]{0:T(1024)(128)(4,1)}), s8[2097152]{0:T(1024)(128)(4,1)S(1)}, s32[]{:S(2)}) async-start(s8[6291456]{0:T(1024)(128)(4,1)} %bitcast.48), calls=%async_computation.6 | async-start | bytes 4194304
  389.2 7.3 %slice-start.3 = ((s8[6291456]{0:T(1024)(128)(4,1)}), s8[2097152]{0:T(1024)(128)(4,1)S(1)}, s32[]{:S(2)}) async-start(s8[6291456]{0:T(1024)(128)(4,1)} %bitcast.50), calls=%async_computation.8 | async-start | bytes 4194304

commit v5 on v4

--- a/solution.py
+++ b/solution.py
@@ -105,13 +105,14 @@
     return [jnp.concatenate(halves[c], axis=0).astype(BF16) for c in range(nc)]
 
 
-def segment_sums(meta, meta_at, idx, seg, tab, acc, bufs, nc, window, blocks):
+def segment_sums(meta, idx, seg, tab, acc, bufs, nc, window, blocks):
     unroll = group_of(blocks)
-    first_trip, end_trip, most = [meta[meta_at + 2 * blocks + k] for k in range(3)]
-
-    def fill(base, first, reach, buf):
+    base, counts = meta[:2]
+    first_trip, end_trip, most = [m[0] for m in meta[2:]]
+
+    def fill(start, first, reach, buf):
         for g in range(BLOCK // 16):
-            parts = gather_16(idx, base, first + g * 16, reach, tab, nc)
+            parts = gather_16(idx, start, first + g * 16, reach, tab, nc)
             for c in range(nc):
                 buf[g * 16:g * 16 + 16, c * LANES:(c + 1) * LANES] = parts[c]
 
@@ -130,7 +131,7 @@
         before = None
         for u in range(unroll):
             b = t * unroll + u
-            now = (meta[meta_at + b], sums(b, meta[meta_at + b], bufs[u % 2]))
+            now = (base[b], sums(b, base[b], bufs[u % 2]))
             if u + 1 < unroll:
                 fill(t * span, (u + 1) * BLOCK, span, bufs[(u + 1) % 2])
             else:
@@ -145,14 +146,14 @@
     @pl.when(most > 1)
     def _():
         def again(b, carry):
-            count = meta[meta_at + blocks + b]
+            count = counts[b]
 
             @pl.when(count > 1)
             def _():
                 fill(b * BLOCK, 0, BLOCK, bufs[0])
 
                 def more(w, c):
-                    at = meta[meta_at + b] + w * window
+                    at = base[b] + w * window
                     add(at, sums(b, at, bufs[0]))
                     return c
                 lax.fori_loop(1, count, more, 0)
@@ -251,8 +252,8 @@
 
 
 def edge_call(name, edges, nc, table_rows, acc_rows, window, sources, build, hbm_in, blocked, fixed, outs, rows_out,
-              tile, epilogue, micros, init=None, late=False, sub=1024, keep=0, pick=None, then=None):
-    meta, meta_at, idx, seg = edges
+              tile, epilogue, micros, init=None, late=False, sub=2048, keep=0, pick=None, then=None):
+    meta, idx, seg = edges
     blocks = seg.shape[0]
     width = nc * LANES
     nh, nb, nf, no, ns = len(hbm_in), len(blocked), len(fixed), len(outs), len(sources)
@@ -271,18 +272,19 @@
         more_out.append(jax.ShapeDtypeStruct((peers, slots, LANES), BF16))
         more_scratch += [pltpu.VMEM((peers, slots, LANES), BF16), pltpu.SemaphoreType.DMA((PIECES,))]
     if then:
-        (t_meta, t_at, t_idx, t_seg), t_nc, t_rows, t_window, finish = then
+        (t_meta, t_idx, t_seg), t_nc, t_rows, t_window, finish = then
         t_width = t_nc * LANES
         t_total = -(-(t_rows + t_window) // 256) * 256
-        more_in += [t_meta, t_idx, t_seg]
-        more_specs += [SMEM_SPEC, SMEM_SPEC, whole_spec(t_seg.shape)]
+        more_in += [*t_meta, t_idx, t_seg]
+        more_specs += [SMEM_SPEC] * 6 + [whole_spec(t_seg.shape)]
         more_out.append(jax.ShapeDtypeStruct((t_rows, t_width), BF16))
         more_scratch += [pltpu.VMEM((t_total, t_width), F32), pltpu.VMEM((BLOCK, t_width), BF16),
                          pltpu.VMEM((BLOCK, t_width), BF16), pltpu.VMEM((t_rows, t_width), BF16),
                          pltpu.SemaphoreType.DMA((PIECES,))]
     nm = len(more_in)
 
-    def kern(meta_ref, idx_ref, seg_ref, *refs):
+    def kern(*refs):
+        meta_refs, (idx_ref, seg_ref), refs = refs[:5], refs[5:7], refs[7:]
         hb, refs = refs[:nh], refs[nh:]
         bl, refs = refs[:nb], refs[nb:]
         fx, refs = refs[:nf], refs[nf:]
@@ -314,7 +316,7 @@
                 start.start()
             if init is not None and not late:
                 start.wait()
-            segment_sums(meta_ref, meta_at, idx_ref, seg_ref, tab, acc, (buf_0, buf_1), nc, window, blocks)
+            segment_sums(meta_refs, idx_ref, seg_ref, tab, acc, (buf_0, buf_1), nc, window, blocks)
             if late:
                 start.wait()
             if epilogue is None:
@@ -356,7 +358,7 @@
             @pl.when(i == steps - 1)
             def _():
                 kept, acc_2, buf_2, buf_3, stage, out_sem = scratch
-                segment_sums(extra[0], t_at, extra[1], extra[2], kept, acc_2, (buf_2, buf_3), t_nc, t_window,
+                segment_sums(extra[:5], extra[5], extra[6], kept, acc_2, (buf_2, buf_3), t_nc, t_window,
                              t_seg.shape[0])
                 size = t_rows // PIECES
                 step = math.gcd(1024, size)
@@ -379,7 +381,7 @@
         out_specs.append(HBM_SPEC if epilogue is None else whole_spec(shape) if sums else row_spec(tile, shape[1]))
     return pl.pallas_call(
         kern, name=name, grid=(steps,), out_shape=out_shape + more_out,
-        in_specs=([SMEM_SPEC, SMEM_SPEC, whole_spec(seg.shape)] + [HBM_SPEC] * nh
+        in_specs=([SMEM_SPEC] * 6 + [whole_spec(seg.shape)] + [HBM_SPEC] * nh
                   + [row_spec(tile, x.shape[1]) for x in blocked] + [whole_spec(x.shape) for x in fixed] + more_specs),
         out_specs=out_specs + [HBM_SPEC] * len(more_out),
         scratch_shapes=([pltpu.VMEM((table_rows * nc, LANES), F32), pltpu.VMEM((acc_total, width), F32),
@@ -387,7 +389,7 @@
                          pltpu.SemaphoreType.DMA(())]
                         + [pltpu.VMEM(shape, BF16) for shape in sources]
                         + [pltpu.SemaphoreType.DMA((parts,)) for _ in sources] + late_scratch + more_scratch),
-        compiler_params=params(), cost_estimate=cost(micros))(meta, idx, seg, *hbm_in, *blocked, *fixed, *more_in)
+        compiler_params=params(), cost_estimate=cost(micros))(*meta, idx, seg, *hbm_in, *blocked, *fixed, *more_in)
 
 
 SHARE = 16
@@ -564,7 +566,7 @@
                 wide = min(LANES, o.shape[1] - w * LANES)
                 o[:, w * LANES:w * LANES + wide] = small[line:line + 1, :wide]
                 line += 1
-        outs[-1][...] = jnp.sum(small[line:line + 1, :], axis=1, keepdims=True) / total_ref[...]
+        outs[-1][...] = jnp.sum(small[line:line + 1, :SPREAD], axis=1, keepdims=True) / total_ref[...]
     ng = len(grads)
     rows_3 = grads[-1].shape[0]
     rows_1, width_1 = grads[0].shape
@@ -576,20 +578,13 @@
 
 def edge_meta(seg_first, seg_last, window, first_block, end_block):
     blocks = seg_first.shape[0]
-    unroll = group_of(blocks)
+    shift = group_of(blocks).bit_length() - 1
     at = jnp.arange(blocks, dtype=jnp.int32)
     base = seg_first & ~7
-    count = jnp.where((at >= first_block) & (at < end_block), (seg_last - base) // window + 1, 1)
-    tail = jnp.stack([first_block // unroll, (end_block + unroll - 1) // unroll, jnp.max(count)])
-    return [base, count, tail]
-
-
-def join_meta(*metas):
-    offsets, at = [], 0
-    for m in metas:
-        offsets.append(at)
-        at += sum(x.shape[0] for x in m)
-    return jnp.concatenate([x for m in metas for x in m]).astype(jnp.int32), offsets
+    inside = (at >= first_block) & (at < end_block)
+    count = jnp.where(inside, lax.div(jnp.maximum(seg_last - base, 0), jnp.int32(window)) + 1, 1)
+    scalars = [first_block >> shift, (end_block + (1 << shift) - 1) >> shift, jnp.max(count)]
+    return [base, count] + [x.reshape(1) for x in scalars]
 
 
 def bits_for(n):
@@ -632,8 +627,9 @@
         zero = jnp.int32(0)
         win_e, win_h, win_r = 192, 208, 272
         owned = jnp.sum((src_idx < n).astype(jnp.int32))
-        near_end = (owned + BLOCK - 1) // BLOCK
-        far_start = owned // BLOCK
+        block_shift = BLOCK.bit_length() - 1
+        near_end = (owned + BLOCK - 1) >> block_shift
+        far_start = owned >> block_shift
 
         src_bits = bits_for(table)
         far_bit = dst_bits + src_bits
@@ -646,9 +642,8 @@
         seg_near = jnp.where(is_far, -1, dst_f).reshape(blocks, 1, BLOCK)
         seg_far = jnp.where(is_far, dst_f, -1).reshape(blocks, 1, BLOCK)
         first, last = dst_f[::BLOCK], dst_f[BLOCK - 1::BLOCK]
-        meta_f, (near_at, far_at) = join_meta(
-            edge_meta(first, jnp.where(is_far[BLOCK - 1::BLOCK], n - 1, last), win_e, zero, near_end),
-            edge_meta(jnp.where(is_far[::BLOCK], first, 0), last, win_e, far_start, jnp.int32(blocks)))
+        meta_near = edge_meta(first, jnp.where(is_far[BLOCK - 1::BLOCK], n - 1, last), win_e, zero, near_end)
+        meta_far = edge_meta(jnp.where(is_far[::BLOCK], first, 0), last, win_e, far_start, jnp.int32(blocks))
 
         inv = jnp.broadcast_to(inv_deg[:, None], (n, LANES))
         b1 = bias_1.reshape(1, -1)
@@ -671,7 +666,7 @@
             return build
 
         def near_sums(name, nc, idx, rows, also):
-            return edge_call(name, (meta_f, near_at, idx, seg_near), nc, n, n, win_e, [rows.shape], rows_of(nc),
+            return edge_call(name, (meta_near, idx, seg_near), nc, n, n, win_e, [rows.shape], rows_of(nc),
                              [rows] + also, [], [], [((n, nc * LANES), F32, False)], n, tile, None, 20)[0]
 
         out_1 = pick_rows('send_1', features, send_flat, peers, slots, train_mask.reshape(-1, LANES))
@@ -701,7 +696,7 @@
             put(mean.astype(F32))
 
         mean_1, hidden_1, out_2 = edge_call(
-            'layer_1', (meta_f, far_at, src_far, seg_far), 1, halo, n, win_e, [(peers, slots + TAIL, LANES)], build_1,
+            'layer_1', (meta_far, src_far, seg_far), 1, halo, n, win_e, [(peers, slots + TAIL, LANES)], build_1,
             [got_1, near_1], [features, inv], [w_self_1, w_neigh_1, b1],
             [((n, LANES), BF16, False), ((n, hidden), BF16, False)], n, tile, epi_1, 25, init=1, late=True,
             keep=1, pick=(send_flat, peers, slots))
@@ -717,10 +712,9 @@
         row_s = by_row >> slot_bits
         slot_s = by_row & ((1 << slot_bits) - 1)
         first, last = src_s[::BLOCK], src_s[BLOCK - 1::BLOCK]
-        meta_b, (own_at, halo_at, owner_at) = join_meta(
-            edge_meta(jnp.minimum(first, n - 1), jnp.minimum(last, n - 1), win_e, zero, near_end),
-            edge_meta(jnp.maximum(first - n, 0), jnp.maximum(last - n, 0), win_h, far_start, jnp.int32(blocks)),
-            edge_meta(row_s[::BLOCK], row_s[BLOCK - 1::BLOCK], win_r, zero, jnp.int32(halo_blocks)))
+        meta_own = edge_meta(jnp.minimum(first, n - 1), jnp.minimum(last, n - 1), win_e, zero, near_end)
+        meta_halo = edge_meta(jnp.maximum(first - n, 0), jnp.maximum(last - n, 0), win_h, far_start, jnp.int32(blocks))
+        meta_owner = edge_meta(row_s[::BLOCK], row_s[BLOCK - 1::BLOCK], win_r, zero, jnp.int32(halo_blocks))
         seg_o = src_s.reshape(blocks, 1, BLOCK)
         seg_h = seg_o - n
         seg_r = row_s.reshape(halo_blocks, 1, BLOCK)
@@ -759,7 +753,7 @@
             put(pieces.astype(F32))
 
         mean_2, hidden_2, proj, logits_self, out_3 = edge_call(
-            'layer_2', (meta_f, far_at, tile_linear(src_far), seg_far), 2, halo, n, win_e,
+            'layer_2', (meta_far, tile_linear(src_far), seg_far), 2, halo, n, win_e,
             [(peers, slots + TAIL, LANES), (peers, slots, LANES)], build_2, [got_1, got_2, near_2],
             [hidden_1, inv], [w_self_2, w_neigh_2, b2, w_self_1, w_neigh_1, b1, jnp.concatenate([wn3, ws3], axis=1)],
             [((n, hidden), BF16, False), ((n, hidden), BF16, False), ((n, LANES), BF16, False),
@@ -772,34 +766,34 @@
         def epi_3(a, bl, fx, out, put):
             scale = bl[1][...]
             z = bl[0][...] + fold3(a * scale, fx[2][...]) + fx[0][...]
-            lane = spread_lanes()
-            z = jnp.where(lane < 3 * SPREAD, z, -1e30)
             top = jnp.max(z, axis=1, keepdims=True)
-            e = jnp.where(lane < SPREAD, jnp.exp(z - top), 0.0)
-            lse = top + jnp.log(jnp.sum(e, axis=1, keepdims=True))
+            e = jnp.exp(z - top)
+            each = jnp.sum(e, axis=1, keepdims=True) * (1.0 / 3.0)
+            lse = top + jnp.log(each)
             t = bl[2][...].astype(F32)
-            hit = t > 1.5
-            d = jnp.where(t > 0.5, jnp.exp(z - lse) - jnp.where(hit, 1.0, 0.0), 0.0) * fx[1][...]
+            inside = jnp.minimum(t, 1.0)
+            hit = t - inside
+            d = (e * (1.0 / each) * inside - hit) * fx[1][...]
             db = d.astype(BF16)
             out[0][...] = db
             pieces = split3(db.astype(F32) * scale)
             out[1][...] = pieces
             put(pieces.astype(F32))
             add_rows(out[2], d)
-            add_rows(out[3], jnp.where(hit & (lane < SPREAD), lse - z, 0.0))
+            add_rows(out[3], hit * (lse - z))
 
         def finish_3(a, fx):
             return split3(fold3(a, fx[2][...]))
 
         d_bf_3, scaled_3, g_b3, loss_parts, back_3 = edge_call(
-            'layer_3', (meta_f, far_at, src_far, seg_far), 1, halo, n, win_e, [(halo, LANES)], rows_of(1), [got_3, near_3],
+            'layer_3', (meta_far, src_far, seg_far), 1, halo, n, win_e, [(halo, LANES)], rows_of(1), [got_3, near_3],
             [logits_self, inv, target], [b3, jnp.broadcast_to(inv_total, (1, LANES)), folder],
             [((n, LANES), BF16, False), ((n, LANES), BF16, False), ((8, LANES), F32, True), ((8, LANES), F32, True)],
             n, tile, epi_3, 30, init=1, late=True, keep=1,
-            then=((meta_b, halo_at, dst_s, seg_h), 1, halo, win_h, finish_3))
+            then=((meta_halo, dst_s, seg_h), 1, halo, win_h, finish_3))
 
         ret_3 = exchange(back_3.reshape(peers, slots, LANES)).reshape(halo, LANES)
-        own_3 = edge_call('back_3_own', (meta_b, own_at, dst_s, seg_o), 1, n, n, win_e, [(n, LANES)], rows_of(1),
+        own_3 = edge_call('back_3_own', (meta_own, dst_s, seg_o), 1, n, n, win_e, [(n, LANES)], rows_of(1),
                           [scaled_3], [], [], [((n, LANES), F32, False)], n, tile, None, 20)[0]
 
         def epi_o3(a, bl, fx, out, put):
@@ -819,17 +813,17 @@
             return a.astype(BF16)
 
         tb_3, d_bf_2, scaled_2, g_b2, back_2 = edge_call(
-            'owner_3', (meta_b, owner_at, slot_s, seg_r), 1, halo, n, win_r, [(halo, LANES)], rows_of(1), [ret_3, own_3],
+            'owner_3', (meta_owner, slot_s, seg_r), 1, halo, n, win_r, [(halo, LANES)], rows_of(1), [ret_3, own_3],
             [d_bf_3, hidden_2, inv], [jnp.concatenate([ws3_t, wn3_t], axis=0), w_neigh_2.T, folder],
             [((n, LANES), BF16, False), ((n, hidden), BF16, False), ((n, hidden), BF16, False), ((8, hidden), F32, True)],
-            n, half_tile, epi_o3, 30, init=1, late=True, sub=512, keep=2,
-            then=((meta_b, halo_at, dst_wide, seg_h), 2, halo, win_h, finish_2))
+            n, half_tile, epi_o3, 30, init=1, late=True, keep=2,
+            then=((meta_halo, dst_wide, seg_h), 2, halo, win_h, finish_2))
 
         def epi_b2o(a, bl, fx, out, put):
             out[0][...] = a + mm(bl[0][...], fx[0][...])
 
         ret_2 = exchange(back_2.reshape(peers, slots, hidden)).reshape(halo, hidden)
-        own_2 = edge_call('back_2_own', (meta_b, own_at, dst_wide, seg_o), 2, n, n, win_e, [(n, hidden)], rows_of(2),
+        own_2 = edge_call('back_2_own', (meta_own, dst_wide, seg_o), 2, n, n, win_e, [(n, hidden)], rows_of(2),
                           [scaled_2], [d_bf_2], [w_self_2.T], [((n, hidden), F32, False)], n, tile, epi_b2o, 30)[0]
 
         def epi_o2(a, bl, fx, out, put):
@@ -840,7 +834,7 @@
             add_rows(out[1], d_pre)
 
         g_1, g_b1 = edge_call(
-            'owner_2', (meta_b, owner_at, tile_linear(slot_s), seg_r), 2, halo, n, win_r, [(halo, hidden)], rows_of(2),
+            'owner_2', (meta_owner, tile_linear(slot_s), seg_r), 2, halo, n, win_r, [(halo, hidden)], rows_of(2),
             [ret_2, own_2], [hidden_1, features, mean_1], [],
             [((2 * LANES, hidden), F32, True), ((8, hidden), F32, True)], n, half_tile, epi_o2, 25, init=1, late=True)
 

time: 481 us -> 473 us (0.983)
  transfers between devices with their start and end apart: 5 -> 5, of which waited for: 4 -> 4; matrix products, arithmetic and copies ran while one was open for 14% -> 13% of each run, Pallas kernels for 21% -> 22%
where the time goes in v5:
time: 473 us; the launch traced here: 463 us
  Pallas kernels  319 us (67%)
  starting transfers between devices  39.6 us (8%)
  waiting for transfers between devices  34.6 us (7%)
  other arithmetic  33.7 us (7%)
  matrix products  19.9 us (4%)
  local copies, waits for them, and re-layouts  12.6 us (3%)
    pallas_call x10, Pallas kernels, edge_call(): pl.pallas_call(kern, name=name, grid=(steps,), out_shape=out_shape + more...  271 us
    all_to_all x5, starting transfers between devices, exchange(): return lax.all_to_all(x, GROUP_AXIS, 0, 0, tiled=True)  39.6 us
    pallas_call x1, Pallas kernels, sum_over_devices(): pl.pallas_call(kern, name='sum_all', out_shape=jax.ShapeDtypeStruct(shape...  36.4 us
    all_to_all x5, waiting for transfers between devices, exchange(): return lax.all_to_all(x, GROUP_AXIS, 0, 0, tiled=True)  34.6 us
    dot_general x4, matrix products, contract(): return jnp.einsum('nd,ne->de', a, b, preferred_element_type=F32)  19.9 us
    pallas_call x1, Pallas kernels, pick_rows(): pl.pallas_call(kern, name=name, grid=(peers // per,), out_shape=jax.Shape...  9.65 us
  transfers between devices with their start and end apart: 5, of which 4 were waited for; matrix products, arithmetic and copies ran while one was open for 13% of the time, Pallas kernels for 22%

profile of v5, /device:TPU:1, one launch (start us, length us, event | category | flops | bytes accessed | tf_op | source)
XLA Modules:
  0.0 463.4 jit_solution(4140378263358670196)
XLA Ops:
  0.7 9.7 %send_1.1 = bf16[128,72,128]{2,1,0:T(8,128)(2,1)} custom-call(s32[8192]{0:T(1024)} %bitcast.69, bf16[12288,128]{1,0:T(8,128)(2,1)} %refs_10_.1, f32[96,128]{1,0:T(8,128)} %bitcast.76), custom_call_target="tpu_custom_call" | custom-call | flops 40000000 | bytes 10000000 | tf_op jit(solution)/shard_map/send_1/pallas_call | solution.py:229
  10.4 11.5 %all-to-all-start = ((bf16[128,72,128]{2,1,0:T(8,128)(2,1)}), bf16[128,72,128]{2,1,0:T(8,128)(2,1)S(1)}, u32[]{:S(2)}, u32[]{:S(2)}) async-start(bf16[128,72,128]{2,1,0:T(8,128)(2,1)} %send_1.1), calls=%async_computation | async-start | bytes 4718592 | tf_op jit(solution)/shard_map/all_to_all | solution.py:607
  21.9 0.7 or_or_fusion
  22.5 8.6 %sort.14 = s32[24576]{0:T(1024)S(1)} sort(s32[24576]{0:T(1024)S(1)} %get-tuple-element.87), dimensions={0}, to_apply=%region_0.0 | sort | flops 368640 | bytes 196608 | tf_op jit(solution)/shard_map/sort | solution.py:636
  31.1 0.8 broadcast_select_fusion
  32.1 0.7 broadcast_select_fusion.1
  35.1 1.2 fusion.25
  36.3 3.8 broadcast_in_dim.69.refs_8_.refs_10_.refs_11_
  40.1 17.8 %near_1.1.refs_8_ = f32[12288,128]{1,0:T(8,128)} custom-call(s32[192]{0:T(256)} %get-tuple-element.110.refs_0_, s32[192]{0:T(256)} %get-tuple-element.83.refs_1_, s32[1]{0:T(128)} %constant.134.clone.1.refs_2_, s32[1]{0:T(128)} %bitcast.7.refs_3_, s32[1]{0:T(128)} %bitcast.8.refs_4_, s32[24576]{0:T(1024)} %get-tuple-element.98.refs_5_, ...), custom_call_target="tpu_custom_call" | custom-call | flops 80000000 | bytes 20000000 | tf_op jit(solution)/shard_map/near_1/pallas_call | solution.py:382
  58.1 0.7 pad_maximum_fusion.refs_18_
  58.8 1.4 copy-done.1
  60.1 29.5 %layer_1.1 = (bf16[12288,128]{1,0:T(8,128)(2,1)}, bf16[12288,256]{1,0:T(8,128)(2,1)}, bf16[128,64,128]{2,1,0:T(8,128)(2,1)}) custom-call(s32[192]{0:T(256)} %get-tuple-element.107.refs_0_, s32[192]{0:T(256)} %get-tuple-element.106.refs_1_, s32[1]{0:T(128)} %bitcast.2.refs_2_.refs_17_, s32[1]{0:T(128)} %constant.130.clone.1.refs_3_.refs_18_, ...), custom_call_target="tpu_custom_call" | custom-call | flops 100000000 | bytes 25000000 | tf_op jit(solution)/shard_map/layer_1/pallas_call | solution.py:382
  89.7 9.8 %all-to-all-start.1 = ((bf16[128,64,128]{2,1,0:T(8,128)(2,1)}), bf16[128,64,128]{2,1,0:T(8,128)(2,1)S(1)}, u32[]{:S(2)}, u32[]{:S(2)}) async-start(bf16[128,64,128]{2,1,0:T(8,128)(2,1)} %get-tuple-element.43), calls=%async_computation.1 | async-start | bytes 4194304 | tf_op jit(solution)/shard_map/all_to_all | solution.py:607
  99.5 6.7 %select_convert_fusion.refs_8_.refs_11_ = bf16[12288,128]{1,0:T(8,128)(2,1)} fusion(s32[128]{0:T(128)S(1)} %and_select_fusion, f32[12288]{0:T(1024)S(1)} %copy-done.11, s32[12288]{0:T(1024)S(1)} %copy-done.17, pred[128]{0:T(512)(128)(4,1)S(1)} %iota_compare_fusion.3), kind=kLoop, calls=%fused_computation | loop fusion | flops 9437184 | bytes 3244672 | tf_op jit(solution)/shard_map/convert_element_type | solution.py:659
  106.1 22.1 %near_2.1.refs_9_ = f32[12288,256]{1,0:T(8,128)} custom-call(s32[192]{0:T(256)} %get-tuple-element.110.refs_0_, s32[192]{0:T(256)} %get-tuple-element.83.refs_1_, s32[1]{0:T(128)} %constant.134.clone.1.refs_2_, s32[1]{0:T(128)} %bitcast.7.refs_3_, s32[1]{0:T(128)} %bitcast.8.refs_4_, s32[24576]{0:T(1024)} %get-tuple-element.96.refs_5_, ...), custom_call_target="tpu_custom_call" | custom-call | flops 80000000 | bytes 20000000 | tf_op jit(solution)/shard_map/near_2/pallas_call | solution.py:382
  128.3 5.4 %all-to-all-done.1.refs_8_ = bf16[128,64,128]{2,1,0:T(8,128)(2,1)S(1)} async-done(((bf16[128,64,128]{2,1,0:T(8,128)(2,1)}), bf16[128,64,128]{2,1,0:T(8,128)(2,1)S(1)}, u32[]{:S(2)}, u32[]{:S(2)}) %all-to-all-start.1) | async-done | bytes 2097184 | tf_op jit(solution)/shard_map/all_to_all | solution.py:607
  133.7 1.3 copy-done.3
  135.0 39.2 %layer_2.1 = (bf16[12288,256]{1,0:T(8,128)(2,1)}, bf16[12288,256]{1,0:T(8,128)(2,1)}, bf16[12288,128]{1,0:T(8,128)(2,1)}, f32[12288,128]{1,0:T(8,128)}, bf16[128,64,128]{2,1,0:T(8,128)(2,1)}) custom-call(s32[192]{0:T(256)} %get-tuple-element.107.refs_0_, s32[192]{0:T(256)} %get-tuple-element.106.refs_1_, s32[1]{0:T(128)} %bitcast.2.refs_2_.refs_17_, ...), custom_call_target="tpu_custom_call" | custom-call | flops 160000000 | bytes 40000000 | tf_op jit(solution)/shard_map/layer_2/pallas_call | solution.py:382
  174.2 4.8 %all-to-all-start.2 = ((bf16[128,64,128]{2,1,0:T(8,128)(2,1)}), bf16[128,64,128]{2,1,0:T(8,128)(2,1)S(1)}, u32[]{:S(2)}, u32[]{:S(2)}) async-start(bf16[128,64,128]{2,1,0:T(8,128)(2,1)} %get-tuple-element.45), calls=%async_computation.2 | async-start | bytes 4194304 | tf_op jit(solution)/shard_map/all_to_all | solution.py:607
  179.7 7.3 %sort.15 = s32[32768]{0:T(1024)S(1)} sort(s32[32768]{0:T(1024)S(1)} %pad_add_fusion), dimensions={0}, to_apply=%region_4.5 | sort | flops 491520 | bytes 262144 | tf_op jit(solution)/shard_map/sort | solution.py:708
  187.1 0.7 and_or_fusion
  188.2 1.0 slice_convert_fusion
  189.2 0.7 slice_reduce_fusion
  191.1 1.3 fusion.22
  192.5 18.0 %near_3.1.refs_8_ = f32[12288,128]{1,0:T(8,128)} custom-call(s32[192]{0:T(256)} %get-tuple-element.110.refs_0_, s32[192]{0:T(256)} %get-tuple-element.83.refs_1_, s32[1]{0:T(128)} %constant.134.clone.1.refs_2_, s32[1]{0:T(128)} %bitcast.7.refs_3_, s32[1]{0:T(128)} %bitcast.8.refs_4_, s32[24576]{0:T(1024)} %get-tuple-element.98.refs_5_, ...), custom_call_target="tpu_custom_call" | custom-call | flops 80000000 | bytes 20000000 | tf_op jit(solution)/shard_map/near_3/pallas_call | solution.py:382
  210.5 2.8 all-to-all-done.2
  213.8 0.8 tile.13
  214.6 41.7 %layer_3.1 = (bf16[12288,128]{1,0:T(8,128)(2,1)}, bf16[12288,128]{1,0:T(8,128)(2,1)}, f32[8,128]{1,0:T(8,128)}, f32[8,128]{1,0:T(8,128)}, bf16[8192,128]{1,0:T(8,128)(2,1)}) custom-call(s32[192]{0:T(256)} %get-tuple-element.107.refs_0_, s32[192]{0:T(256)} %get-tuple-element.106.refs_1_, s32[1]{0:T(128)} %bitcast.2.refs_2_.refs_17_, ...), custom_call_target="tpu_custom_call" | custom-call | flops 120000000 | bytes 30000000 | tf_op jit(solution)/shard_map/layer_3/pallas_call | solution.py:382
  256.3 7.8 %all-to-all-start.3 = ((bf16[128,64,128]{2,1,0:T(8,128)(2,1)}), bf16[128,64,128]{2,1,0:T(8,128)(2,1)S(1)}, u32[]{:S(2)}, u32[]{:S(2)}) async-start(bf16[128,64,128]{2,1,0:T(8,128)(2,1)} %bitcast.55), calls=%async_computation.3 | async-start | bytes 4194304 | tf_op jit(solution)/shard_map/all_to_all | solution.py:607
  264.1 0.8 copy.32
  264.9 0.7 pad_maximum_fusion.1.refs_12_
  265.5 0.6 fusion.20
  266.5 1.2 fusion.24
  267.6 17.7 %back_3_own.1.refs_8_ = f32[12288,128]{1,0:T(8,128)} custom-call(s32[192]{0:T(256)} %get-tuple-element.108.refs_0_, s32[192]{0:T(256)} %get-tuple-element.75.refs_1_, s32[1]{0:T(128)} %constant.134.clone.1.refs_2_, s32[1]{0:T(128)} %bitcast.7.refs_3_, s32[1]{0:T(128)} %bitcast.22.refs_4_, s32[24576]{0:T(1024)} %get-tuple-element.91.refs_20_.refs_5_, ...), custom_call_target="tpu_custom_call" | custom-call | flops 80000000 | bytes 20000000 | tf_op jit(solution)/shard_map/back_3_own/pallas_call | solution.py:382
  285.3 13.0 %all-to-all-done.3 = bf16[128,64,128]{2,1,0:T(8,128)(2,1)S(1)} async-done(((bf16[128,64,128]{2,1,0:T(8,128)(2,1)}), bf16[128,64,128]{2,1,0:T(8,128)(2,1)S(1)}, u32[]{:S(2)}, u32[]{:S(2)}) %all-to-all-start.3) | async-done | bytes 2097184 | tf_op jit(solution)/shard_map/all_to_all | solution.py:607
  298.3 1.3 copy-done.5
  299.6 39.9 %owner_3.1 = (bf16[12288,128]{1,0:T(8,128)(2,1)}, bf16[12288,256]{1,0:T(8,128)(2,1)}, bf16[12288,256]{1,0:T(8,128)(2,1)}, f32[8,256]{1,0:T(8,128)}, bf16[8192,256]{1,0:T(8,128)(2,1)}) custom-call(s32[64]{0:T(128)} %get-tuple-element.111.refs_0_, s32[64]{0:T(128)} %get-tuple-element.79.refs_1_, s32[1]{0:T(128)} %constant.134.clone.1.refs_2_, ...), custom_call_target="tpu_custom_call" | custom-call | flops 120000000 | bytes 30000000 | tf_op jit(solution)/shard_map/owner_3/pallas_call | solution.py:382
  339.5 5.8 %all-to-all-start.4 = ((bf16[128,64,256]{2,1,0:T(8,128)(2,1)}), bf16[128,64,256]{2,1,0:T(8,128)(2,1)}, u32[]{:S(2)}, u32[]{:S(2)}) async-start(bf16[128,64,256]{2,1,0:T(8,128)(2,1)} %bitcast.54), calls=%async_computation.4 | async-start | bytes 8388608 | tf_op jit(solution)/shard_map/all_to_all | solution.py:607
  345.4 0.8 copy.33
  346.1 4.6 fusion.29
  350.8 24.6 %back_2_own.1.refs_8_ = f32[12288,256]{1,0:T(8,128)} custom-call(s32[192]{0:T(256)} %get-tuple-element.108.refs_0_, s32[192]{0:T(256)} %get-tuple-element.75.refs_1_, s32[1]{0:T(128)} %constant.134.clone.1.refs_2_, s32[1]{0:T(128)} %bitcast.7.refs_3_, s32[1]{0:T(128)} %bitcast.22.refs_4_, s32[24576]{0:T(1024)} %get-tuple-element.89.refs_20_.refs_5_, ...), custom_call_target="tpu_custom_call" | custom-call | flops 120000000 | bytes 30000000 | tf_op jit(solution)/shard_map/back_2_own/pallas_call | solution.py:382
  375.4 5.4 %convolution_select_fusion.refs_3_ = f32[256,128]{1,0:T(8,128)} fusion(f32[256,128]{1,0:T(8,128)S(1)} %fusion.29, bf16[12288,256]{1,0:T(8,128)(2,1)} %get-tuple-element.51.refs_10_, bf16[12288,128]{1,0:T(8,128)(2,1)S(1)} %copy-done.2, pred[128]{0:T(512)(128)(4,1)S(1)} %iota_compare_fusion.2), kind=kOutput, calls=%fused_computation.1 | convolution fusion | flops 805339136 | bytes 9699456 | tf_op jit(solution)/shard_map/nd,ne->de/dot_general | solution.py:842
  380.8 7.3 %fusion.27.refs_1_ = f32[256,256]{1,0:T(8,128)} fusion(bf16[12288,256]{1,0:T(8,128)(2,1)} %get-tuple-element.44.refs_7_.refs_10_.refs_9_, bf16[12288,256]{1,0:T(8,128)(2,1)} %get-tuple-element.54.refs_8_), kind=kOutput, calls=%fused_computation.79 | convolution fusion | flops 1610612736 | bytes 12845056 | tf_op jit(solution)/shard_map/nd,ne->de/dot_general | solution.py:842
  388.1 2.5 fusion.28.refs_2_
  390.7 13.4 %all-to-all-done.4 = bf16[128,64,256]{2,1,0:T(8,128)(2,1)} async-done(((bf16[128,64,256]{2,1,0:T(8,128)(2,1)}), bf16[128,64,256]{2,1,0:T(8,128)(2,1)}, u32[]{:S(2)}, u32[]{:S(2)}) %all-to-all-start.4) | async-done | bytes 4194336 | tf_op jit(solution)/shard_map/all_to_all | solution.py:607
  404.0 20.3 %owner_2.1 = (f32[256,256]{1,0:T(8,128)}, f32[8,256]{1,0:T(8,128)}) custom-call(s32[64]{0:T(128)} %get-tuple-element.111.refs_0_, s32[64]{0:T(128)} %get-tuple-element.79.refs_1_, s32[1]{0:T(128)} %constant.134.clone.1.refs_2_, s32[1]{0:T(128)} %constant.137.clone.1.refs_3_, s32[1]{0:T(128)} %bitcast.11.refs_4_, s32[8192]{0:T(1024)} %get-tuple-element.94.refs_5_, ...), custom_call_target="tpu_custom_call" | custom-call | flops 100000000 | bytes 25000000 | tf_op jit(solution)/shard_map/owner_2/pallas_call | solution.py:382
  424.4 36.4 %sum_all.1.full_ref = f32[2,64,16,128]{3,2,1,0:T(8,128)} custom-call(f32[256,256]{1,0:T(8,128)} %get-tuple-element.55.refs_0_, f32[256,256]{1,0:T(8,128)} %fusion.27.refs_1_, f32[256,256]{1,0:T(8,128)} %fusion.28.refs_2_, f32[256,128]{1,0:T(8,128)} %convolution_select_fusion.refs_3_, f32[8,256]{1,0:T(8,128)} %get-tuple-element.58.refs_4_, ...), custom_call_target="tpu_custom_call" | custom-call | flops 100000000 | bytes 25000000 | tf_op jit(solution)/shard_map/sum_all/pallas_call | solution.py:537
  460.8 2.1 unpack_sums.1
  (66 shorter events, 3.4 us)
Async XLA Ops:
  0.6 21.2 %copy-start.12 = (s32[24576]{0:T(1024)S(1)}, s32[24576]{0:T(1024)}, u32[]{:S(2)}) copy-start(s32[24576]{0:T(1024)} %param.20) | copy-start | bytes 294916
  0.7 21.2 %copy-start.13 = (s32[24576]{0:T(1024)S(1)}, s32[24576]{0:T(1024)}, u32[]{:S(2)}) copy-start(s32[24576]{0:T(1024)} %param.21) | copy-start | bytes 294916
  0.7 34.2 %copy-start.14 = (bf16[256,40]{0,1:T(8,128)(2,1)S(1)}, bf16[256,40]{0,1:T(8,128)(2,1)}, u32[]{:S(2)}) copy-start(bf16[256,40]{0,1:T(8,128)(2,1)} %param.30) | copy-start | bytes 61444
  0.7 34.3 %copy-start.15 = (bf16[256,40]{0,1:T(8,128)(2,1)S(1)}, bf16[256,40]{0,1:T(8,128)(2,1)}, u32[]{:S(2)}) copy-start(bf16[256,40]{0,1:T(8,128)(2,1)} %param.29) | copy-start | bytes 61444
  0.7 35.6 %copy-start.16 = (f32[12288]{0:T(1024)S(1)}, f32[12288]{0:T(1024)}, u32[]{:S(2)}) copy-start(f32[12288]{0:T(1024)} %param.22) | copy-start | bytes 147460
  10.4 48.4 %all-to-all-start = ((bf16[128,72,128]{2,1,0:T(8,128)(2,1)}), bf16[128,72,128]{2,1,0:T(8,128)(2,1)S(1)}, u32[]{:S(2)}, u32[]{:S(2)}) async-start(bf16[128,72,128]{2,1,0:T(8,128)(2,1)} %send_1.1), calls=%async_computation | async-start | bytes 4718592 | tf_op jit(solution)/shard_map/all_to_all | solution.py:607
  58.7 1.4 copy-start.1
  60.1 39.3 %copy-start.11 = (f32[12288]{0:T(1024)S(1)}, f32[12288]{0:T(1024)}, u32[]{:S(2)}) copy-start(f32[12288]{0:T(1024)} %param.18) | copy-start | bytes 147460
  60.1 39.3 %copy-start.17 = (s32[12288]{0:T(1024)S(1)}, s32[12288]{0:T(1024)}, u32[]{:S(2)}) copy-start(s32[12288]{0:T(1024)} %param.17) | copy-start | bytes 147460
  89.7 44.0 %all-to-all-start.1 = ((bf16[128,64,128]{2,1,0:T(8,128)(2,1)}), bf16[128,64,128]{2,1,0:T(8,128)(2,1)S(1)}, u32[]{:S(2)}, u32[]{:S(2)}) async-start(bf16[128,64,128]{2,1,0:T(8,128)(2,1)} %get-tuple-element.43), calls=%async_computation.1 | async-start | bytes 4194304 | tf_op jit(solution)/shard_map/all_to_all | solution.py:607
  133.7 1.3 copy-start.3
  135.0 44.1 %copy-start.18 = (f32[40]{0:T(128)S(1)}, f32[40]{0:T(128)}, u32[]{:S(2)}) copy-start(f32[40]{0:T(128)} %param.31) | copy-start | bytes 484
  135.0 44.7 %copy-start.7 = (s32[128,64]{0,1:T(8,128)S(1)}, s32[128,64]{0,1:T(8,128)}, u32[]{:S(2)}) copy-start(s32[128,64]{0,1:T(8,128)} %param.19) | copy-start | bytes 98308
  174.2 39.0 %all-to-all-start.2 = ((bf16[128,64,128]{2,1,0:T(8,128)(2,1)}), bf16[128,64,128]{2,1,0:T(8,128)(2,1)S(1)}, u32[]{:S(2)}, u32[]{:S(2)}) async-start(bf16[128,64,128]{2,1,0:T(8,128)(2,1)} %get-tuple-element.45), calls=%async_computation.2 | async-start | bytes 4194304 | tf_op jit(solution)/shard_map/all_to_all | solution.py:607
  187.8 22.7 %copy-start.6 = (s32[24576]{0:T(1024)}, s32[24576]{0:T(1024)S(1)}, u32[]{:S(2)}) copy-start(s32[24576]{0:T(1024)S(1)} %get-tuple-element.92) | copy-start | bytes 294916
  213.3 1.3 copy-start.4
  214.6 49.5 %copy-start.8 = (bf16[256,256]{1,0:T(8,128)(2,1)S(1)}, bf16[256,256]{1,0:T(8,128)(2,1)}, u32[]{:S(2)}) copy-start(bf16[256,256]{1,0:T(8,128)(2,1)} %refs_13_.1) | copy-start | bytes 393220
  256.3 42.0 %all-to-all-start.3 = ((bf16[128,64,128]{2,1,0:T(8,128)(2,1)}), bf16[128,64,128]{2,1,0:T(8,128)(2,1)S(1)}, u32[]{:S(2)}, u32[]{:S(2)}) async-start(bf16[128,64,128]{2,1,0:T(8,128)(2,1)} %bitcast.55), calls=%async_computation.3 | async-start | bytes 4194304 | tf_op jit(solution)/shard_map/all_to_all | solution.py:607
  266.2 32.2 %copy-start.10 = (s32[8192]{0:T(1024)}, s32[8192]{0:T(1024)S(1)}, u32[]{:S(2)}) copy-start(s32[8192]{0:T(1024)S(1)} %get-tuple-element.95) | copy-start | bytes 98308
  298.3 1.3 copy-start.5
  339.5 5.8 %copy-start.9 = (bf16[256,256]{1,0:T(8,128)(2,1)S(1)}, bf16[256,256]{1,0:T(8,128)(2,1)}, u32[]{:S(2)}) copy-start(bf16[256,256]{1,0:T(8,128)(2,1)} %refs_12_.3) | copy-start | bytes 393220
  339.5 6.6 %copy-start = (bf16[12288,128]{1,0:T(8,128)(2,1)S(1)}, bf16[12288,128]{1,0:T(8,128)(2,1)}, u32[]{:S(2)}) copy-start(bf16[12288,128]{1,0:T(8,128)(2,1)} %get-tuple-element.50.refs_9_) | copy-start | bytes 9437188
  339.5 64.5 %all-to-all-start.4 = ((bf16[128,64,256]{2,1,0:T(8,128)(2,1)}), bf16[128,64,256]{2,1,0:T(8,128)(2,1)}, u32[]{:S(2)}, u32[]{:S(2)}) async-start(bf16[128,64,256]{2,1,0:T(8,128)(2,1)} %bitcast.54), calls=%async_computation.4 | async-start | bytes 8388608 | tf_op jit(solution)/shard_map/all_to_all | solution.py:607
  350.8 24.6 %copy-start.2 = (bf16[12288,128]{1,0:T(8,128)(2,1)S(1)}, bf16[12288,128]{1,0:T(8,128)(2,1)}, u32[]{:S(2)}) copy-start(bf16[12288,128]{1,0:T(8,128)(2,1)} %get-tuple-element.57) | copy-start | bytes 9437188
  375.4 12.7 %slice-start = ((s8[6291456]{0:T(1024)(128)(4,1)}), s8[4194304]{0:T(1024)(128)(4,1)S(1)}, s32[]{:S(2)}) async-start(s8[6291456]{0:T(1024)(128)(4,1)} %bitcast.48), calls=%async_computation.5 | async-start | bytes 8388608
  375.4 12.7 %slice-start.2 = ((s8[6291456]{0:T(1024)(128)(4,1)}), s8[4194304]{0:T(1024)(128)(4,1)S(1)}, s32[]{:S(2)}) async-start(s8[6291456]{0:T(1024)(128)(4,1)} %bitcast.50), calls=%async_computation.7 | async-start | bytes 8388608
  380.8 7.3 %slice-start.1 = ((s8[6291456]{0:T(1024)(128)(4,1)}), s8[2097152]{0:T(1024)(128)(4,1)S(1)}, s32[]{:S(2)}) async-start(s8[6291456]{0:T(1024)(128)(4,1)} %bitcast.48), calls=%async_computation.6 | async-start | bytes 4194304
  380.8 7.3 %slice-start.3 = ((s8[6291456]{0:T(1024)(128)(4,1)}), s8[2097152]{0:T(1024)(128)(4,1)S(1)}, s32[]{:S(2)}) async-start(s8[6291456]{0:T(1024)(128)(4,1)} %bitcast.50), calls=%async_computation.8 | async-start | bytes 4194304
